TPU v7x, 128 devices: a whole 4x4x4 slice. The times are simulated.
128 devices in a mesh: res: 32 (over x_lo, y, z), seq: 4 (over x_hi, core).
Axes of the slice: x: 4 (x_hi: 2, x_lo: 2; x = x_hi * 2 + x_lo), y: 4, z: 4, core: 2. Of those that a mesh axis runs over, the one named last changes fastest.
Arguments:
- alignment: bfloat16 [384, 1024, 256], P('seq', 'res'), may hold values from -6 to 6
- query_weight: bfloat16 [256, 256], replicated, may hold values from -1 to 1
- w_keyval: bfloat16 [256, 512], replicated, may hold values from -0.375 to 0.375
- w_gate: bfloat16 [256, 256], replicated, may hold values from -0.375 to 0.375
- output_weight: bfloat16 [256, 256], replicated, may hold values from -0.75 to 0.75
- w_factors: bfloat16 [256, 64], replicated, may hold values from -1.5 to 1.5
- w_pair_out: bfloat16 [1024, 128], replicated, may hold values from -0.1875 to 0.1875
Outputs:
- alignment_update: bfloat16 [384, 1024, 256], P('seq', 'res')
- pair_representation_update: bfloat16 [1024, 1024, 128], P(('res', 'seq'))
All inputs are finite; a program needn't handle non-finite values.
Results may differ from a plain program's by a relative error of at most 0.012.
The roundings to bfloat16 on the way count: a program that leaves them out, or rounds other values in their place, can miss the bound.
Values may be sent and summed in bfloat16 or wider, within the bound.
No kernel may reach another device: no remote copies, remote signals or barrier semaphores. Data moves between devices by JAX's collectives and lax.ppermute only.
A program may use at most 256 MiB of HBM per device.

v0:
```python
import math

import jax
import jax.numpy as jnp
from jax import lax
from jax.sharding import Mesh
from jax.sharding import PartitionSpec as P

HEADS = 8
HC = 32
SEQ = ("seq_0", "seq_1")
RES_SEQ = ("res", "seq_0", "seq_1")


epsilon = 1e-05


def joined_along(parts, dim):
    lengths = list(parts.shape[1:])
    lengths[dim] *= parts.shape[0]
    return jnp.moveaxis(parts, 0, dim).reshape(lengths)


def all_blocks(x, axes, order):
    parts = x
    for k in order:
        parts = lax.all_gather(parts, axes[k])
    done = order[::-1]
    back = [done.index(k) for k in range(len(axes))]
    parts = parts.transpose(*back, *range(len(axes), parts.ndim))
    return parts.reshape(-1, *x.shape)


def whole_of(x, axes, order, dim):
    return joined_along(all_blocks(x, axes, order), dim)


def piecewise(x, axis, dim, work, out_dim):
    span = x.shape[dim]
    pieces = jnp.split(x, 2, axis=dim) if span % 2 == 0 else [x]
    leading = jnp.arange(lax.axis_size(axis)) * span
    parts = [lax.all_gather(share, axis) for share in pieces]
    made = [jax.vmap(work)(b, leading + k * (span // len(pieces))) for k, b in enumerate(parts)]
    return joined_along(jnp.concatenate(made, axis=out_dim + 1), out_dim)


def normalize(alignment):
    values = alignment.astype(jnp.float32)
    centered = values - jnp.mean(values, axis=-1, keepdims=True)
    spread = jnp.mean(centered * centered, axis=-1, keepdims=True)
    return (centered * lax.rsqrt(spread + epsilon)).astype(jnp.bfloat16)


def apply_projection(normed, weight):
    return jnp.dot(normed, weight, preferred_element_type=jnp.float32)


def attend_group(query_rows, keyval_rows, running, start_row, group_size):
    denominators, accumulated = running
    hidden = query_rows.shape[2]
    query_slice = lax.dynamic_slice_in_dim(query_rows, start_row, group_size, 1)
    keyval_slice = lax.dynamic_slice_in_dim(keyval_rows, start_row, group_size, 1)
    query_count = query_slice.shape[0]
    key_count = keyval_slice.shape[0]
    per_head_query = query_slice.reshape(query_count, group_size, HEADS, HC)
    head_keys = keyval_slice[:, :, :hidden].reshape(key_count, group_size, HEADS, HC)
    head_values = keyval_slice[:, :, hidden:].reshape(key_count, group_size, HEADS, HC)
    scores = jnp.einsum(
        "qrhd,krhd->rhqk", per_head_query, head_keys, preferred_element_type=jnp.float32
    ) * (1.0 / math.sqrt(HC))
    exponent = jnp.exp(scores)
    weights = exponent.astype(jnp.bfloat16)
    summed = jnp.transpose(jnp.sum(exponent, axis=-1), (2, 0, 1))
    weighted = jnp.einsum(
        "rhqk,krhd->qrhd", weights, head_values, preferred_element_type=jnp.float32
    ).reshape(query_count, group_size, hidden)
    prior_sums = lax.dynamic_slice_in_dim(denominators, start_row, group_size, 1)
    prior_values = lax.dynamic_slice_in_dim(accumulated, start_row, group_size, 1)
    denominators = lax.dynamic_update_slice_in_dim(denominators, prior_sums + summed, start_row, 1)
    accumulated = lax.dynamic_update_slice_in_dim(
        accumulated, prior_values + weighted, start_row, 1
    )
    return (denominators, accumulated)


def attend_piece(query_rows, running, keyval_rows):
    group_size = 4
    group_total = query_rows.shape[1] // group_size

    def one_group(group_index, current):
        return attend_group(query_rows, keyval_rows, current, group_index * group_size, group_size)

    return lax.fori_loop(0, group_total, one_group, running)


def outer_panel(left_rows, right_cols, scaling, pair_weight):
    factor = pair_weight.shape[0]
    row_count = left_rows.shape[1] // factor
    column_total = right_cols.shape[1] // factor
    products = (
        lax.dot_general(
            left_rows, right_cols, (((0,), (0,)), ((), ())), preferred_element_type=jnp.float32
        )
        * scaling
    )
    products = products.reshape(row_count, factor, column_total, factor)
    upper_part = products.astype(jnp.bfloat16)
    lower_part = (products - upper_part.astype(jnp.float32)).astype(jnp.bfloat16)
    upper_terms = jnp.einsum(
        "icje,cep->ijp", upper_part, pair_weight, preferred_element_type=jnp.float32
    )
    lower_terms = jnp.einsum(
        "icje,cep->ijp", lower_part, pair_weight, preferred_element_type=jnp.float32
    )
    return upper_terms + lower_terms


def outer_blocks(left_rows, right_cols, scaling, pair_weight):
    factor = pair_weight.shape[0]
    column_total = right_cols.shape[1] // factor
    panel_width = math.gcd(column_total, 128)
    panel_total = column_total // panel_width
    if panel_total == 1:
        return outer_panel(left_rows, right_cols, scaling, pair_weight)

    def one_panel(panel_index):
        column_slice = lax.dynamic_slice_in_dim(
            right_cols, panel_index * panel_width * factor, panel_width * factor, 1
        )
        return outer_panel(left_rows, column_slice, scaling, pair_weight)

    stacked = lax.map(one_panel, jnp.arange(panel_total, dtype=jnp.int32))
    return jnp.transpose(stacked, (1, 0, 2, 3)).reshape(
        stacked.shape[1], column_total, stacked.shape[3]
    )


def per_device(alignment, query_weight, w_keyval, w_gate, output_weight, w_factors, w_pair_out):
    normed = normalize(alignment)
    queries = apply_projection(normed, query_weight).astype(jnp.bfloat16)
    gating = jax.nn.sigmoid(apply_projection(normed, w_gate))
    seq_rows = normed.shape[0]
    residues = normed.shape[1]
    hidden = queries.shape[2]
    totals = (
        jnp.zeros((seq_rows, residues, HEADS), jnp.float32),
        jnp.zeros((seq_rows, residues, hidden), jnp.float32),
    )
    keyvals = apply_projection(lax.all_gather(normed, SEQ, axis=0, tiled=True), w_keyval).astype(
        jnp.bfloat16
    )
    denominators, accumulated = attend_piece(queries, totals, keyvals)
    attended = (
        accumulated.reshape(seq_rows, residues, HEADS, HC) / denominators[:, :, :, None]
    ).reshape(seq_rows, residues, hidden)
    gated_output_rows = (gating * attended).astype(jnp.bfloat16)
    alignment_update = apply_projection(gated_output_rows, output_weight).astype(jnp.bfloat16)
    factors = apply_projection(normed, w_factors).astype(jnp.bfloat16)
    factor = factors.shape[2] // 2
    left_factor = factors[:, :, :factor].reshape(seq_rows, residues * factor)
    right_factor = factors[:, :, factor:].reshape(seq_rows, residues * factor)
    pair_weight = w_pair_out.reshape(factor, factor, w_pair_out.shape[1])
    groups = lax.axis_size(SEQ)
    own_rows = residues // groups
    scaling = 1.0 / (seq_rows * groups)
    left_all, right_all = (
        whole_of(left_factor, SEQ, (0, 1), 0),
        whole_of(right_factor, SEQ, (0, 1), 0),
    )
    own_left = lax.dynamic_slice_in_dim(
        left_all, lax.axis_index(SEQ) * (own_rows * factor), own_rows * factor, 1
    )

    def panel_terms(shard_piece, start_col):
        return outer_blocks(own_left, shard_piece, scaling, pair_weight)

    pair_representation_update = piecewise(right_all, "res", 1, panel_terms, 1)
    return (alignment_update, pair_representation_update.astype(jnp.bfloat16))


def solution(mesh):
    split = Mesh(mesh.devices.reshape(mesh.shape["res"], 2, 2), ("res", "seq_0", "seq_1"))
    in_specs = (P(SEQ, "res", None), P(), P(), P(), P(), P(), P())
    out_specs = (P(SEQ, "res", None), P(RES_SEQ, None, None))
    return jax.shard_map(
        per_device, mesh=split, in_specs=in_specs, out_specs=out_specs, check_vma=False
    )
```

profile of v0, /device:TPU:0, one launch (start us, length us, event | category | flops | bytes accessed | tf_op | source)
XLA Modules:
  0.0 599.9 jit_solution(4230690787443213538)
XLA Ops:
  19.7 8.7 %all_gather.37 = bf16[2,96,1024]{2,1,0:T(8,128)(2,1)S(1)} all-gather(bf16[1,96,1024]{2,1,0:T(8,128)(2,1)S(1)} %copy.57), channel_id=1, replica_groups=mesh['res'=32,'seq_0'=2,'seq_1'=2] {'seq_0'}, dimensions={0}, use_global_device_ids=true | all-gather | bytes 589824 | tf_op jit(solution)/shard_map/all_gather | solution.py:27
  33.7 13.9 %all_gather.34 = bf16[2,96,1024]{2,1,0:T(8,128)(2,1)S(1)} all-gather(bf16[1,96,1024]{2,1,0:T(8,128)(2,1)S(1)} %copy.53), channel_id=1, replica_groups=mesh['res'=32,'seq_0'=2,'seq_1'=2] {'seq_0'}, dimensions={0}, use_global_device_ids=true | all-gather | bytes 589824 | tf_op jit(solution)/shard_map/all_gather | solution.py:27
  52.3 20.7 %all-gather.8.cloned.1.call-done = bf16[384,32,256]{2,0,1:T(8,128)(2,1)} async-done(((bf16[96,32,256]{2,0,1:T(8,128)(2,1)}), bf16[384,32,256]{2,0,1:T(8,128)(2,1)}) %all-gather.8.cloned.1.call-update) | async-done | bytes 6291472 | tf_op jit(solution)/shard_map/all_gather | solution.py:149
  73.0 9.7 %convolution_convert_fusion = bf16[384,32,512]{2,0,1:T(8,128)(2,1)} fusion(bf16[384,32,256]{2,0,1:T(8,128)(2,1)} %all-gather.8.cloned.1.call-done, bf16[256,512]{1,0:T(8,128)(2,1)S(1)} %copy-done), kind=kOutput, calls=%fused_computation.20 | convolution fusion | flops 3227516928 | bytes 19136512 | tf_op jit(solution)/shard_map/dot_general | solution.py:55
  84.8 98.4 %while.15 = (s32[]{:T(128)}, f32[96,32,8]{0,2,1:T(8,128)S(1)}, f32[96,32,256]{2,0,1:T(8,128)}, bf16[96,32,256]{2,1,0:T(8,128)(2,1)}, bf16[384,32,512]{2,0,1:T(8,...) while((s32[]{:T(128)}, f32[96,32,8]{0,2,1:T(8,128)S(1)}, f32[96,32,256]{2,0,1:T(8,128)}, ...), condition=%wide.region_4.0_spmd, body=%wide.region_2.0_spmd.sunk | while | flops 155811840 | bytes 23064760 | solution.py:93
  91.4 3.3 fusion.63
  100.2 3.1 fusion.61
  103.7 3.3 fusion.63
  116.1 3.3 fusion.63
  124.8 3.1 fusion.61
  128.3 3.3 fusion.63
  140.6 3.3 fusion.63
  149.4 3.1 fusion.61
  152.9 3.3 fusion.63
  165.2 3.3 fusion.63
  177.5 3.3 fusion.63
  185.4 5.4 copy.49
  190.8 4.3 multiply_convert_fusion
  197.4 51.6 %all-gather.10.cloned.1.call-done = bf16[12288,512]{1,0:T(8,128)(2,1)} async-done(((bf16[384,512]{1,0:T(8,128)(2,1)}), bf16[12288,512]{1,0:T(8,128)(2,1)}) %all-gather.10.cloned.1.call-update) | async-done | bytes 12582928 | tf_op jit(solution)/shard_map/all_gather | solution.py:42
  249.0 15.4 %bitcast_convert_fusion.1 = (bf16[32,256,512]{2,1,0:T(8,128)(2,1)}, f32[256,32,512]{2,0,1:T(8,128)}) fusion(bf16[32,384,512]{2,1,0:T(8,128)(2,1)} %bitcast.124, bf16[384,1024]{1,0:T(8,128)(2,1)S(1)} %bitcast.129, s32[]{:T(128)S(6)} %select_n.15), kind=kOutput, calls=%fused_computation.18 | convolution fusion | flops 3229614080 | bytes 37945348 | tf_op jit(solution)/shard_map/vmap()/dot_general | solution.py:101
  264.4 36.9 %convert_element_type.77 = bf16[32,8,32,16,32]{4,3,2,1,0:T(8,128)(2,1)} reshape(bf16[32,256,512]{2,1,0:T(8,128)(2,1)} %get-tuple-element.139) | data formatting | bytes 16777216 | tf_op jit(solution)/shard_map/vmap()/convert_element_type | solution.py:107
  301.3 9.9 %fusion.8 = bf16[32,256,512]{2,1,0:T(8,128)(2,1)} fusion(f32[256,32,512]{2,0,1:T(8,128)} %get-tuple-element.140), kind=kLoop, calls=%fused_computation.19 | loop fusion | flops 20971520 | bytes 25165824 | tf_op jit(solution)/shard_map/vmap()/convert_element_type | solution.py:108
  311.2 37.0 %convert_element_type.80 = bf16[32,8,32,16,32]{4,3,2,1,0:T(8,128)(2,1)} reshape(bf16[32,256,512]{2,1,0:T(8,128)(2,1)} %fusion.8) | data formatting | bytes 16777216 | tf_op jit(solution)/shard_map/vmap()/convert_element_type | solution.py:108
  348.2 76.1 %all-gather.12.cloned.1.call-done = bf16[12288,512]{1,0:T(8,128)(2,1)} async-done(((bf16[384,512]{1,0:T(8,128)(2,1)}), bf16[12288,512]{1,0:T(8,128)(2,1)}) %all-gather.12.cloned.1.call-update) | async-done | bytes 12582928 | tf_op jit(solution)/shard_map/all_gather | solution.py:42
  424.3 15.2 %bitcast_convert_fusion = (bf16[32,256,512]{2,1,0:T(8,128)(2,1)}, f32[256,32,512]{2,0,1:T(8,128)}) fusion(bf16[32,384,512]{2,1,0:T(8,128)(2,1)} %bitcast.123, bf16[384,1024]{1,0:T(8,128)(2,1)S(1)} %bitcast.130, s32[]{:T(128)S(6)} %select_n.15), kind=kOutput, calls=%fused_computation.15 | convolution fusion | flops 3229614080 | bytes 37945348 | tf_op jit(solution)/shard_map/vmap()/dot_general | solution.py:101
  439.5 36.9 %convert_element_type.82 = bf16[32,8,32,16,32]{4,3,2,1,0:T(8,128)(2,1)} reshape(bf16[32,256,512]{2,1,0:T(8,128)(2,1)} %get-tuple-element.137) | data formatting | bytes 16777216 | tf_op jit(solution)/shard_map/vmap()/convert_element_type | solution.py:107
  476.4 14.1 %fusion.33 = f32[32,8,16,128,1]{3,2,4,1,0:T(8,128)S(1)} fusion(bf16[32,8,32,16,32]{4,3,2,1,0:T(8,128)(2,1)} %convert_element_type.77, bf16[32,32,128,1,1]{2,1,0,4,3:T(8,128)(2,1)S(1)} %bitcast.133), kind=kOutput, calls=%fused_computation.56 | convolution fusion | flops 1073741824 | bytes 10747904 | tf_op jit(solution)/shard_map/vmap(icje,cep->ijp)/dot_general | solution.py:109
  490.5 18.5 %fusion.34 = f32[32,8,16,128,1]{3,2,4,1,0:T(8,128)} fusion(bf16[32,8,32,16,32]{4,3,2,1,0:T(8,128)(2,1)} %convert_element_type.82, bf16[32,32,128,1,1]{2,1,0,4,3:T(8,128)(2,1)S(1)} %bitcast.134), kind=kOutput, calls=%fused_computation.57 | convolution fusion | flops 1073741824 | bytes 10747904 | tf_op jit(solution)/shard_map/vmap(icje,cep->ijp)/dot_general | solution.py:109
  509.0 9.7 %fusion.7 = bf16[32,256,512]{2,1,0:T(8,128)(2,1)} fusion(f32[256,32,512]{2,0,1:T(8,128)} %get-tuple-element.138), kind=kLoop, calls=%fused_computation.16 | loop fusion | flops 20971520 | bytes 25165824 | tf_op jit(solution)/shard_map/vmap()/convert_element_type | solution.py:108
  518.7 37.1 %convert_element_type.85 = bf16[32,8,32,16,32]{4,3,2,1,0:T(8,128)(2,1)} reshape(bf16[32,256,512]{2,1,0:T(8,128)(2,1)} %fusion.7) | data formatting | bytes 16777216 | tf_op jit(solution)/shard_map/vmap()/convert_element_type | solution.py:108
  555.8 17.4 %fusion.14 = bf16[32,8,16,128]{3,2,1,0:T(8,128)(2,1)S(1)} fusion(f32[32,8,16,128,1]{3,2,4,1,0:T(8,128)S(1)} %fusion.33, bf16[32,8,32,16,32]{4,3,2,1,0:T(8,128)(2,1)} %convert_element_type.80, bf16[32,32,128,1,1]{2,1,0,4,3:T(8,128)(2,1)S(1)} %bitcast.135), kind=kOutput, calls=%fused_computation.32 | convolution fusion | flops 1074790400 | bytes 11796480 | tf_op jit(solution)/shard_map/vmap(icje,cep->ijp)/dot_general | solution.py:112
  573.2 17.6 %fusion.13 = bf16[32,8,16,128]{3,2,1,0:T(8,128)(2,1)S(1)} fusion(f32[32,8,16,128,1]{3,2,4,1,0:T(8,128)S(1)} %copy-done.10, bf16[32,8,32,16,32]{4,3,2,1,0:T(8,128)(2,1)} %convert_element_type.85, bf16[32,32,128,1,1]{2,1,0,4,3:T(8,128)(2,1)S(1)} %bitcast.136), kind=kOutput, calls=%fused_computation.30 | convolution fusion | flops 1074790400 | bytes 11796480 | tf_op jit(solution)/shard_map/vmap(icje,cep->ijp)/dot_general | solution.py:112
  (144 shorter events, 93.0 us)
Async XLA Ops:
  7.2 65.9 %copy-start = (bf16[256,512]{1,0:T(8,128)(2,1)S(1)}, bf16[256,512]{1,0:T(8,128)(2,1)}, u32[]{:S(2)}) copy-start(bf16[256,512]{1,0:T(8,128)(2,1)} %param.11) | copy-start | bytes 786436
  7.2 5.5 copy-start.2
  7.2 65.8 %all-gather.8.cloned.1.call-start = ((), (), s32[]{:S(2)}) async-start(), calls=%async_computation | async-start | bytes 7864320 | tf_op jit(solution)/shard_map/all_gather | solution.py:149
  9.7 6.1 %copy-start.9 = (bf16[256,64]{0,1:T(8,128)(2,1)S(1)}, bf16[256,64]{0,1:T(8,128)(2,1)}, u32[]{:S(2)}) copy-start(bf16[256,64]{0,1:T(8,128)(2,1)} %param.14) | copy-start | bytes 98308
  15.8 233.2 %all-gather.10.cloned.1.call-start = ((), (), s32[]{:S(2)}) async-start(), calls=%async_computation.1 | async-start | bytes 12976128 | tf_op jit(solution)/shard_map/all_gather | solution.py:42
  31.9 18.1 %copy-start.3 = (bf16[96,32,256]{2,0,1:T(8,128)(2,1)S(1)}, bf16[96,32,256]{2,0,1:T(8,128)(2,1)}, u32[]{:S(2)}) copy-start(bf16[96,32,256]{2,0,1:T(8,128)(2,1)} %fusion.12) | copy-start | bytes 4718596
  31.9 18.1 %copy-start.5 = (bf16[256,256]{1,0:T(8,128)(2,1)S(1)}, bf16[256,256]{1,0:T(8,128)(2,1)}, u32[]{:S(2)}) copy-start(bf16[256,256]{1,0:T(8,128)(2,1)} %param.10) | copy-start | bytes 393220
  31.9 392.3 %all-gather.12.cloned.1.call-start = ((), (), s32[]{:S(2)}) async-start(), calls=%async_computation.2 | async-start | bytes 12976128 | tf_op jit(solution)/shard_map/all_gather | solution.py:42
  185.4 5.4 copy-start.4
  185.4 5.4 copy-start.8
  190.8 4.3 copy-start.6
  439.5 36.9 %copy-start.7 = (bf16[1024,128]{1,0:T(8,128)(2,1)S(1)}, bf16[1024,128]{1,0:T(8,128)(2,1)}, u32[]{:S(2)}) copy-start(bf16[1024,128]{1,0:T(8,128)(2,1)} %param.15) | copy-start | bytes 786436
  555.8 17.4 %copy-start.10 = (f32[32,8,16,128,1]{3,2,4,1,0:T(8,128)S(1)}, f32[32,8,16,128,1]{3,2,4,1,0:T(8,128)}, u32[]{:S(2)}) copy-start(f32[32,8,16,128,1]{3,2,4,1,0:T(8,128)} %fusion.34) | copy-start | bytes 6291460
  590.8 2.1 copy-start.1
Sparse Core Ops, SparseCore 0:
  15.9 57.0 all-gather.7
  74.7 174.2 all-gather.9
  250.7 173.5 all-gather.11
where the time goes:
time: 611 us; the launch traced here: 600 us
  local copies, waits for them, and re-layouts  208 us (34%)
  matrix products  171 us (28%)
  waiting for transfers between devices  149 us (24%)
  other arithmetic  29 us (5%)
  blocking collectives  27.5 us (5%)
  between operations  14.5 us (2%)
    all_gather x2, waiting for transfers between devices, piecewise(): parts = [lax.all_gather(share, axis) for share in pieces]  128 us
    convert_element_type x2, local copies, waits for them, and re-layouts, outer_panel(): (products - upper_part.astype(jnp.float32)).astype(jnp.bfloat16)  74.1 us
    convert_element_type x2, local copies, waits for them, and re-layouts, outer_panel(): upper_part = products.astype(jnp.bfloat16)  73.8 us
    dot_general x2, matrix products, outer_panel(): jnp.einsum('icje,cep->ijp', lower_part, pair_weight, preferred_element_ty...  35 us
    dot_general x2, matrix products, outer_panel(): jnp.einsum('icje,cep->ijp', upper_part, pair_weight, preferred_element_ty...  32.6 us
    dot_general x2, matrix products, outer_panel(): lax.dot_general(left_rows, right_cols, (((0,), (0,)), ((), ())), preferre...  30.6 us
    all_gather x4, blocking collectives, all_blocks(): parts = lax.all_gather(parts, axes[k])  27.5 us
    dot_general x8, matrix products, attend_group(): jnp.einsum('rhqk,krhd->qrhd', weights, head_values, preferred_element_typ...  26.4 us
  transfers between devices with their start and end apart: 3, of which 3 were waited for; matrix products, arithmetic and copies ran while one was open for 39% of the time, Pallas kernels for 0%

commit v1 on v0

v1 whole, which is shorter than its diff:
```python
import math

import jax
import jax.numpy as jnp
from jax import lax
from jax.experimental import pallas as pl
from jax.experimental.pallas import tpu as pltpu
from jax.sharding import Mesh
from jax.sharding import PartitionSpec as P

HEADS = 8
HC = 32
EPS = 1e-05
SEQ = ("xh", "c")
ROWS = ("yl", "z")
COLS = ("xl", "yh", "xh", "c")
NT = (((1,), (1,)), ((), ()))
NN = (((1,), (0,)), ((), ()))
TN = (((0,), (0,)), ((), ()))
F32 = jnp.float32
BF16 = jnp.bfloat16


def dot(a, b, dims):
    return lax.dot_general(a, b, dims, preferred_element_type=F32)


def norm_kernel(x_ref, wf_ref, n_ref, l_ref, r_ref, nf, rf):
    rows = x_ref.shape[0]
    step = 256

    def one(k, _):
        sl = pl.ds(pl.multiple_of(k * step, step), step)
        v = x_ref[sl, :].astype(F32)
        v = v - jnp.mean(v, axis=-1, keepdims=True)
        spread = jnp.mean(v * v, axis=-1, keepdims=True)
        y = (v * lax.rsqrt(spread + EPS)).astype(BF16).astype(F32)
        nf[0, sl, :] = y[:, :128]
        nf[1, sl, :] = y[:, 128:]
        return 0

    lax.fori_loop(0, rows // step, one, 0)
    seqs = rows // 8
    for r in range(8):
        x = jnp.concatenate(
            [nf[0, pl.ds(r, seqs, stride=8), :], nf[1, pl.ds(r, seqs, stride=8), :]], axis=1
        ).astype(BF16)
        n_ref[r] = x
        f = dot(wf_ref[...], x, NT)
        l_ref[r] = f[:32].astype(BF16)
        for t in range(3):
            rf[t, pl.ds(r, 32, stride=8), :] = f[32:, t * 128:(t + 1) * 128]
    for t in range(3):
        r_ref[:, t * 128:(t + 1) * 128] = rf[t].astype(BF16)


def norm_and_factors(x, wf_t):
    rows = x.shape[0]
    seqs = rows // 8
    return pl.pallas_call(
        norm_kernel,
        out_shape=(
            jax.ShapeDtypeStruct((8, seqs, 256), BF16),
            jax.ShapeDtypeStruct((8, 32, seqs), BF16),
            jax.ShapeDtypeStruct((256, seqs), BF16),
        ),
        scratch_shapes=[pltpu.VMEM((2, rows, 128), F32), pltpu.VMEM((3, 256, 128), F32)],
        cost_estimate=pl.CostEstimate(flops=2 * rows * 256 * 64, transcendentals=rows, bytes_accessed=4 * rows * 256),
        name="norm_factors",
    )(x, wf_t)


def attention_kernel(x_ref, wq_ref, wk_ref, wv_ref, wg_ref, wo_ref, o_ref, of):
    r = pl.program_id(0)
    x = x_ref[0]
    seqs = x.shape[0]
    q_t = dot(wq_ref[...], x, NT).astype(BF16)
    keys = dot(x, wk_ref[...], NN).astype(BF16)
    v_t = dot(wv_ref[...], x, NT).astype(BF16)
    g_t = jax.nn.sigmoid(dot(wg_ref[...], x, NT))
    ones = jnp.ones((16, seqs), BF16)
    scale = math.log2(math.e) / math.sqrt(HC)
    gated = []

    def spread(h):
        parts = []
        if h:
            parts.append(jnp.zeros((h * HC, seqs), BF16))
        parts.append(q_t[h * HC:(h + 1) * HC])
        if h < HEADS - 1:
            parts.append(jnp.zeros(((HEADS - 1 - h) * HC, seqs), BF16))
        return jnp.concatenate(parts, axis=0)

    for p in range(HEADS // 2):
        rhs = jnp.concatenate([spread(2 * p), spread(2 * p + 1)], axis=1)
        scores = dot(keys, rhs, NN)
        weights = jnp.exp2(scores * scale).astype(BF16)
        for u in range(2):
            h = 2 * p + u
            lhs = jnp.concatenate([v_t[h * HC:(h + 1) * HC], ones], axis=0)
            out = dot(lhs, weights[:, u * seqs:(u + 1) * seqs], NN)
            att = out[:HC] / out[HC:HC + 1]
            gated.append((g_t[h * HC:(h + 1) * HC] * att).astype(BF16))
    gated = jnp.concatenate(gated, axis=0)
    update = dot(gated, wo_ref[...], TN)
    of[0, pl.ds(r, seqs, stride=8), :] = update[:, :128]
    of[1, pl.ds(r, seqs, stride=8), :] = update[:, 128:]

    @pl.when(r == pl.num_programs(0) - 1)
    def _():
        o_ref[:, :128] = of[0].astype(BF16)
        o_ref[:, 128:] = of[1].astype(BF16)


def attention(normed, wq_t, wk, wv_t, wg_t, wo):
    count, seqs, width = normed.shape
    full = pl.BlockSpec((256, 256), lambda r: (0, 0))
    return pl.pallas_call(
        attention_kernel,
        grid=(count,),
        in_specs=[pl.BlockSpec((1, seqs, width), lambda r: (r, 0, 0)), full, full, full, full, full],
        out_specs=pl.BlockSpec((seqs * count, width), lambda r: (0, 0)),
        out_shape=jax.ShapeDtypeStruct((seqs * count, width), BF16),
        scratch_shapes=[pltpu.VMEM((2, seqs * count, 128), F32)],
        cost_estimate=pl.CostEstimate(
            flops=count * (2 * seqs * seqs * 256 * 9 + 2 * seqs * 256 * 256 * 5),
            transcendentals=count * HEADS * seqs * seqs,
            bytes_accessed=4 * count * seqs * width,
        ),
        name="attention",
    )(normed, wq_t, wk, wv_t, wg_t, wo)


def pair_kernel(scaling, l_ref, r_ref, w_ref, o_ref, scr):
    seqs = l_ref.shape[-1]
    left = l_ref[...].reshape(512, seqs)
    for n in range(8):
        right = r_ref[n * 512:(n + 1) * 512, :]
        o = dot(left, right, NT).astype(BF16)
        for i in range(16):
            for e in range(4):
                row = (n * 4 + e) * 32
                scr[i, row:row + 32, :] = o[i * 32:(i + 1) * 32, e * 128:(e + 1) * 128]
    for k in range(8):
        rhs = jnp.concatenate([scr[2 * k], scr[2 * k + 1]], axis=1)
        t = dot(w_ref[...], rhs, NN) * scaling
        o_ref[k, 0] = t[:, :128].T.astype(BF16)
        o_ref[k, 1] = t[:, 128:].T.astype(BF16)


def pair_block(left, right, w_t, part, scaling):
    seqs = left.shape[-1]
    return pl.pallas_call(
        lambda *refs: pair_kernel(scaling, *refs),
        grid=(1,),
        in_specs=[
            pl.BlockSpec((8, 2, 32, seqs), lambda g: (0, part, 0, 0)),
            pl.BlockSpec((4096, seqs), lambda g: (0, 0)),
            pl.BlockSpec((128, 1024), lambda g: (0, 0)),
        ],
        out_specs=pl.BlockSpec((8, 2, 128, 128), lambda g: (0, 0, 0, 0)),
        out_shape=jax.ShapeDtypeStruct((8, 2, 128, 128), BF16),
        scratch_shapes=[pltpu.VMEM((16, 1024, 128), BF16)],
        cost_estimate=pl.CostEstimate(
            flops=2 * 512 * 4096 * seqs + 2 * 16 * 128 * 128 * 1024,
            transcendentals=0,
            bytes_accessed=2 * (4096 + 512) * seqs,
        ),
        name="pair",
    )(left, right, w_t)


def spread_to(x, axes):
    n = lax.axis_size(axes)
    return lax.all_to_all(jnp.broadcast_to(x[None], (n, *x.shape)), axes, 0, 0)


def per_device(alignment, query_weight, w_keyval, w_gate, output_weight, w_factors, w_pair_out):
    seqs, residues, width = alignment.shape
    groups = 4
    own = residues // groups
    total = seqs * groups
    send = alignment.reshape(seqs, groups, own, width).transpose(1, 0, 2, 3)
    rows = lax.all_to_all(send, SEQ, 0, 0).reshape(total * own, width)
    normed, left, right = norm_and_factors(rows, w_factors.T)
    left_all = spread_to(left, ROWS)
    right_all = spread_to(right.reshape(32, 8, total), COLS)
    right_all = right_all.transpose(1, 0, 2, 3).reshape(32 * 128, total)
    update = attention(
        normed, query_weight.T, w_keyval[:, :256], w_keyval[:, 256:].T, w_gate.T, output_weight
    )
    back = lax.all_to_all(update.reshape(groups, seqs, own, width), SEQ, 0, 0)
    alignment_update = back.transpose(1, 0, 2, 3).reshape(seqs, residues, width)
    w_t = w_pair_out.reshape(32, 32, 128).transpose(2, 1, 0).reshape(128, 1024)
    pieces = []
    for part in range(4):
        block = pair_block(left_all, right_all, w_t, part, 1.0 / total)
        got = lax.all_to_all(block, ROWS, 0, 0)
        pieces.append(got.reshape(8, 2, 4, 32, 128).transpose(1, 2, 0, 3, 4).reshape(2, 1024, 128))
    return alignment_update, jnp.concatenate(pieces, axis=0)


def solution(mesh):
    split = Mesh(
        mesh.devices.reshape(2, 2, 2, 4, 2, 2), ("xl", "yh", "yl", "z", "xh", "c")
    )
    res = ("xl", "yh", "yl", "z")
    in_specs = (P(SEQ, res, None), P(), P(), P(), P(), P(), P())
    out_specs = (P(SEQ, res, None), P((*res, *SEQ), None, None))
    return jax.shard_map(
        per_device, mesh=split, in_specs=in_specs, out_specs=out_specs, check_vma=False
    )
```

time: 611 us -> 193 us (0.32); the launches traced: 600 us -> 190 us
  local copies, waits for them, and re-layouts: 208 us -> 19.4 us
  matrix products: 171 us -> 0 us
  waiting for transfers between devices: 149 us -> 40.3 us
  Pallas kernels: 0 us -> 49.5 us
  other arithmetic: 29 us -> 1.58 us
  blocking collectives: 27.5 us -> 53.1 us
  starting transfers between devices: 0.12 us -> 25.3 us
  between operations: 14.5 us -> 0.76 us
    dot_general x27 -> x0, matrix products: 171 us -> none  [the longest x2 35 us: outer_panel(): jnp.einsum('icje,cep->ijp', lower_part, pair_weight, preferred_element_ty...]
    convert_element_type x5 -> x0, local copies, waits for them, and re-layouts: 150 us -> none  [the longest x2 74.1 us: outer_panel(): (products - upper_part.astype(jnp.float32)).astype(jnp.bfloat16)]
    all_gather x3 -> x0, waiting for transfers between devices: 148 us -> none  [the longest x2 128 us: piecewise(): parts = [lax.all_gather(share, axis) for share in pieces]]
    all_to_all x0 -> x2, blocking collectives: none -> 53.1 us  [the longest x1 27.3 us: spread_to(): return lax.all_to_all(jnp.broadcast_to(x[None], (n, *x.shape)), axes, 0, 0)]
    pallas_call x0 -> x6, Pallas kernels: none -> 49.5 us  [the longest x4 23.3 us: pair_block(): pl.pallas_call(lambda *refs: pair_kernel(scaling, *refs), grid=(1,), in_s...]
    all_to_all x0 -> x6, waiting for transfers between devices: none -> 40.3 us  [the longest x1 17.7 us: spread_to(): return lax.all_to_all(jnp.broadcast_to(x[None], (n, *x.shape)), axes, 0, 0)]
    all_gather x4 -> x0, blocking collectives: 27.5 us -> none  [all_blocks(): parts = lax.all_gather(parts, axes[k])]
    all_to_all x0 -> x6, starting transfers between devices: none -> 25.3 us  [the longest x4 16.8 us: per_device(): got = lax.all_to_all(block, ROWS, 0, 0)]
  transfers between devices with their start and end apart: 3 -> 6, of which waited for: 3 -> 6; matrix products, arithmetic and copies ran while one was open for 39% -> 7% of each run, Pallas kernels for 0% -> 23%
where the time goes in v1:
time: 193 us; the launch traced here: 190 us
  blocking collectives  53.1 us (28%)
  Pallas kernels  49.5 us (26%)
  waiting for transfers between devices  40.3 us (21%)
  starting transfers between devices  25.3 us (13%)
  local copies, waits for them, and re-layouts  19.4 us (10%)
    all_to_all x1, blocking collectives, spread_to(): return lax.all_to_all(jnp.broadcast_to(x[None], (n, *x.shape)), axes, 0, 0)  27.3 us
    all_to_all x1, blocking collectives, per_device(): rows = lax.all_to_all(send, SEQ, 0, 0).reshape(total * own, width)  25.9 us
    pallas_call x4, Pallas kernels, pair_block(): pl.pallas_call(lambda *refs: pair_kernel(scaling, *refs), grid=(1,), in_s...  23.3 us
    pallas_call x1, Pallas kernels, attention(): pl.pallas_call(attention_kernel, grid=(count,), in_specs=[pl.BlockSpec((1...  20.3 us
    all_to_all x1, waiting for transfers between devices, spread_to(): return lax.all_to_all(jnp.broadcast_to(x[None], (n, *x.shape)), axes, 0, 0)  17.7 us
    all_to_all x4, starting transfers between devices, per_device(): got = lax.all_to_all(block, ROWS, 0, 0)  16.8 us
    all_to_all x4, waiting for transfers between devices, per_device(): got = lax.all_to_all(block, ROWS, 0, 0)  13 us
    all_to_all x1, waiting for transfers between devices, per_device(): back = lax.all_to_all(update.reshape(groups, seqs, own, width), SEQ, 0, 0)  9.65 us
  transfers between devices with their start and end apart: 6, of which 6 were waited for; matrix products, arithmetic and copies ran while one was open for 7% of the time, Pallas kernels for 23%

profile of v1, /device:TPU:0, one launch (start us, length us, event | category | flops | bytes accessed | tf_op | source)
XLA Modules:
  0.0 190.1 jit_solution(16775936166783972596)
XLA Ops:
  0.6 1.4 copy-done
  2.1 25.9 %all_to_all.40 = bf16[4,96,8,256]{3,2,1,0:T(8,128)(2,1)} all-to-all(bf16[4,96,8,256]{3,2,1,0:T(8,128)(2,1)S(1)} %copy_bitcast_fusion.1), channel_id=1, replica_groups=mesh['xl'=2,'yh'=2,'yl'=2,'z'=4,'xh'=2,'c'=2] {'xh','c'}, dimensions={0} | all-to-all | bytes 3145728 | tf_op jit(solution)/shard_map/all_to_all | solution.py:184
  28.0 5.9 %norm_factors.1 = (bf16[8,384,256]{2,1,0:T(8,128)(2,1)}, bf16[8,32,384]{2,1,0:T(8,128)(2,1)}, bf16[256,384]{1,0:T(8,128)(2,1)}) custom-call(bf16[3072,256]{1,0:T(8,128)(2,1)} %bitcast.39, bf16[64,256]{1,0:T(8,128)(2,1)} %bitcast.55), custom_call_target="tpu_custom_call" | custom-call | flops 100663296 | bytes 3145728 | tf_op jit(solution)/shard_map/norm_factors/pallas_call | solution.py:60
  33.9 1.1 broadcast_in_dim.6
  35.0 27.3 %all_to_all.41.refs_0_ = bf16[8,8,32,384]{3,2,1,0:T(8,128)(2,1)} all-to-all(bf16[8,8,32,384]{3,2,1,0:T(8,128)(2,1)S(1)} %broadcast_in_dim.6), channel_id=1, replica_groups=mesh['xl'=2,'yh'=2,'yl'=2,'z'=4,'xh'=2,'c'=2] {'yl','z'}, dimensions={0} | all-to-all | bytes 3145728 | tf_op jit(solution)/shard_map/all_to_all | solution.py:175
  62.3 2.1 %broadcast_in_dim.15 = bf16[16,32,8,384]{3,2,1,0:T(8,128)(2,1)} broadcast(bf16[32,8,384]{2,1,0:T(8,128)(2,1)S(1)} %bitcast.51), dimensions={1,2,3} | broadcast | bytes 3342336 | tf_op jit(solution)/shard_map/broadcast_in_dim | solution.py:175
  64.4 5.0 %all-to-all-start.3 = ((bf16[16,32,8,384]{3,2,1,0:T(8,128)(2,1)}), bf16[16,32,8,384]{3,2,1,0:T(8,128)(2,1)}, u32[]{:S(2)}, u32[]{:S(2)}) async-start(bf16[16,32,8,384]{3,2,1,0:T(8,128)(2,1)} %broadcast_in_dim.15), calls=%async_computation.3 | async-start | bytes 6291456 | tf_op jit(solution)/shard_map/all_to_all | solution.py:175
  72.3 20.3 %attention.1 = bf16[3072,256]{1,0:T(8,128)(2,1)} custom-call(bf16[8,384,256]{2,1,0:T(8,128)(2,1)} %get-tuple-element.5.x_ref, bf16[256,256]{1,0:T(8,128)(2,1)} %bitcast.53, bf16[256,256]{1,0:T(8,128)(2,1)} %get-tuple-element.9.wk_ref, bf16[256,256]{1,0:T(8,128)(2,1)} %bitcast.52, bf16[256,256]{1,0:T(8,128)(2,1)} %bitcast.54, bf16[256,256]{1,0:T(8,128)(2,1)} %wo_ref.1), custom_call_target="tpu_custom_call" | custom-call | flops 7449083904 | bytes 3145728 | tf_op jit(solution)/shard_map/attention/pallas_call | solution.py:118
  92.7 17.7 %all-to-all-done.3 = bf16[16,32,8,384]{3,2,1,0:T(8,128)(2,1)} async-done(((bf16[16,32,8,384]{3,2,1,0:T(8,128)(2,1)}), bf16[16,32,8,384]{3,2,1,0:T(8,128)(2,1)}, u32[]{:S(2)}, u32[]{:S(2)}) %all-to-all-start.3) | async-done | bytes 3145760 | tf_op jit(solution)/shard_map/all_to_all | solution.py:175
  110.4 3.6 %all-to-all-start.1 = ((bf16[4,96,8,256]{3,2,1,0:T(8,128)(2,1)}), bf16[4,96,8,256]{3,2,1,0:T(8,128)(2,1)S(1)}, u32[]{:S(2)}, u32[]{:S(2)}) async-start(bf16[4,96,8,256]{3,2,1,0:T(8,128)(2,1)} %bitcast.48), calls=%async_computation.1 | async-start | bytes 3145728 | tf_op jit(solution)/shard_map/all_to_all | solution.py:192
  114.0 1.1 copy.52
  115.0 0.9 copy.53.refs_2_
  115.9 4.1 %copy.51 = bf16[32,16,8,384]{3,2,1,0:T(8,128)(2,1)} copy(bf16[32,16,8,384]{3,2,0,1:T(8,128)(2,1)} %bitcast.11) | data formatting | bytes 6291456 | tf_op jit(solution)/shard_map/transpose | solution.py:188
  120.0 5.8 %pair.4 = bf16[8,2,128,128]{3,2,1,0:T(8,128)(2,1)} custom-call(bf16[8,8,32,384]{3,2,1,0:T(8,128)(2,1)} %all_to_all.41.refs_0_, bf16[4096,384]{1,0:T(8,128)(2,1)} %bitcast.40, bf16[128,1024]{1,0:T(8,128)(2,1)} %copy.53.refs_2_), custom_call_target="tpu_custom_call" | custom-call | flops 2147483648 | bytes 3538944 | tf_op jit(solution)/shard_map/pair/pallas_call | solution.py:153
  125.8 9.6 %all-to-all-done.1 = bf16[4,96,8,256]{3,2,1,0:T(8,128)(2,1)S(1)} async-done(((bf16[4,96,8,256]{3,2,1,0:T(8,128)(2,1)}), bf16[4,96,8,256]{3,2,1,0:T(8,128)(2,1)S(1)}, u32[]{:S(2)}, u32[]{:S(2)}) %all-to-all-start.1) | async-done | bytes 1572896 | tf_op jit(solution)/shard_map/all_to_all | solution.py:192
  135.5 4.2 %all-to-all-start.4 = ((bf16[8,2,128,128]{3,2,1,0:T(8,128)(2,1)}), bf16[8,2,128,128]{3,2,1,0:T(8,128)(2,1)}, u32[]{:S(2)}, u32[]{:S(2)}) async-start(bf16[8,2,128,128]{3,2,1,0:T(8,128)(2,1)} %pair.4), calls=%async_computation.4 | async-start | bytes 1048576 | tf_op jit(solution)/shard_map/all_to_all | solution.py:198
  139.6 5.8 %pair.5 = bf16[8,2,128,128]{3,2,1,0:T(8,128)(2,1)} custom-call(bf16[8,8,32,384]{3,2,1,0:T(8,128)(2,1)} %all_to_all.41.refs_0_, bf16[4096,384]{1,0:T(8,128)(2,1)} %bitcast.41, bf16[128,1024]{1,0:T(8,128)(2,1)} %copy.53.refs_2_), custom_call_target="tpu_custom_call" | custom-call | flops 2147483648 | bytes 3538944 | tf_op jit(solution)/shard_map/pair/pallas_call | solution.py:153
  145.5 3.7 %all-to-all-done.4 = bf16[8,2,128,128]{3,2,1,0:T(8,128)(2,1)} async-done(((bf16[8,2,128,128]{3,2,1,0:T(8,128)(2,1)}), bf16[8,2,128,128]{3,2,1,0:T(8,128)(2,1)}, u32[]{:S(2)}, u32[]{:S(2)}) %all-to-all-start.4) | async-done | bytes 524320 | tf_op jit(solution)/shard_map/all_to_all | solution.py:198
  149.2 4.3 %all-to-all-start.5 = ((bf16[8,2,128,128]{3,2,1,0:T(8,128)(2,1)}), bf16[8,2,128,128]{3,2,1,0:T(8,128)(2,1)}, u32[]{:S(2)}, u32[]{:S(2)}) async-start(bf16[8,2,128,128]{3,2,1,0:T(8,128)(2,1)} %pair.5), calls=%async_computation.5 | async-start | bytes 1048576 | tf_op jit(solution)/shard_map/all_to_all | solution.py:198
  153.5 5.8 %pair.6 = bf16[8,2,128,128]{3,2,1,0:T(8,128)(2,1)} custom-call(bf16[8,8,32,384]{3,2,1,0:T(8,128)(2,1)} %all_to_all.41.refs_0_, bf16[4096,384]{1,0:T(8,128)(2,1)} %bitcast.42, bf16[128,1024]{1,0:T(8,128)(2,1)} %copy.53.refs_2_), custom_call_target="tpu_custom_call" | custom-call | flops 2147483648 | bytes 3538944 | tf_op jit(solution)/shard_map/pair/pallas_call | solution.py:153
  159.4 3.0 %all-to-all-done.5 = bf16[8,2,128,128]{3,2,1,0:T(8,128)(2,1)} async-done(((bf16[8,2,128,128]{3,2,1,0:T(8,128)(2,1)}), bf16[8,2,128,128]{3,2,1,0:T(8,128)(2,1)}, u32[]{:S(2)}, u32[]{:S(2)}) %all-to-all-start.5) | async-done | bytes 524320 | tf_op jit(solution)/shard_map/all_to_all | solution.py:198
  162.4 4.2 %all-to-all-start.6 = ((bf16[8,2,128,128]{3,2,1,0:T(8,128)(2,1)}), bf16[8,2,128,128]{3,2,1,0:T(8,128)(2,1)}, u32[]{:S(2)}, u32[]{:S(2)}) async-start(bf16[8,2,128,128]{3,2,1,0:T(8,128)(2,1)} %pair.6), calls=%async_computation.6 | async-start | bytes 1048576 | tf_op jit(solution)/shard_map/all_to_all | solution.py:198
  166.6 5.8 %pair.7 = bf16[8,2,128,128]{3,2,1,0:T(8,128)(2,1)} custom-call(bf16[8,8,32,384]{3,2,1,0:T(8,128)(2,1)} %all_to_all.41.refs_0_, bf16[4096,384]{1,0:T(8,128)(2,1)} %bitcast.43, bf16[128,1024]{1,0:T(8,128)(2,1)} %copy.53.refs_2_), custom_call_target="tpu_custom_call" | custom-call | flops 2147483648 | bytes 3538944 | tf_op jit(solution)/shard_map/pair/pallas_call | solution.py:153
  172.4 2.6 %all-to-all-done.6 = bf16[8,2,128,128]{3,2,1,0:T(8,128)(2,1)} async-done(((bf16[8,2,128,128]{3,2,1,0:T(8,128)(2,1)}), bf16[8,2,128,128]{3,2,1,0:T(8,128)(2,1)}, u32[]{:S(2)}, u32[]{:S(2)}) %all-to-all-start.6) | async-done | bytes 524320 | tf_op jit(solution)/shard_map/all_to_all | solution.py:198
  174.9 4.1 %all-to-all-start.7 = ((bf16[8,2,128,128]{3,2,1,0:T(8,128)(2,1)}), bf16[8,2,128,128]{3,2,1,0:T(8,128)(2,1)}, u32[]{:S(2)}, u32[]{:S(2)}) async-start(bf16[8,2,128,128]{3,2,1,0:T(8,128)(2,1)} %pair.7), calls=%async_computation.7 | async-start | bytes 1048576 | tf_op jit(solution)/shard_map/all_to_all | solution.py:198
  179.1 1.4 copy_bitcast_fusion
  180.5 1.1 copy.54
  181.5 1.1 copy.56
  182.6 1.1 copy.58
  183.7 3.7 %all-to-all-done.7 = bf16[8,2,128,128]{3,2,1,0:T(8,128)(2,1)} async-done(((bf16[8,2,128,128]{3,2,1,0:T(8,128)(2,1)}), bf16[8,2,128,128]{3,2,1,0:T(8,128)(2,1)}, u32[]{:S(2)}, u32[]{:S(2)}) %all-to-all-start.7) | async-done | bytes 524320 | tf_op jit(solution)/shard_map/all_to_all | solution.py:198
  187.4 1.1 copy.60
  188.5 1.6 pad_maximum_fusion
  (14 shorter events, 3.1 us)
Async XLA Ops:
  0.6 1.4 copy-start
  35.0 27.3 %copy-start.2 = (bf16[256,384]{1,0:T(8,128)(2,1)S(1)}, bf16[256,384]{1,0:T(8,128)(2,1)}, u32[]{:S(2)}) copy-start(bf16[256,384]{1,0:T(8,128)(2,1)} %get-tuple-element.7) | copy-start | bytes 589828
  64.3 5.0 %copy-start.1 = (bf16[256,512]{1,0:T(8,128)(2,1)S(1)}, bf16[256,512]{1,0:T(8,128)(2,1)}, u32[]{:S(2)}) copy-start(bf16[256,512]{1,0:T(8,128)(2,1)} %param.9) | copy-start | bytes 786436
  64.3 6.5 %copy-start.3 = (bf16[256,256]{1,0:T(8,128)(2,1)S(1)}, bf16[256,256]{1,0:T(8,128)(2,1)}, u32[]{:S(2)}) copy-start(bf16[256,256]{1,0:T(8,128)(2,1)} %param.8) | copy-start | bytes 393220
  64.4 7.2 %copy-start.4 = (bf16[256,256]{1,0:T(8,128)(2,1)S(1)}, bf16[256,256]{1,0:T(8,128)(2,1)}, u32[]{:S(2)}) copy-start(bf16[256,256]{1,0:T(8,128)(2,1)} %param.10) | copy-start | bytes 393220
  64.4 46.0 %all-to-all-start.3 = ((bf16[16,32,8,384]{3,2,1,0:T(8,128)(2,1)}), bf16[16,32,8,384]{3,2,1,0:T(8,128)(2,1)}, u32[]{:S(2)}, u32[]{:S(2)}) async-start(bf16[16,32,8,384]{3,2,1,0:T(8,128)(2,1)} %broadcast_in_dim.15), calls=%async_computation.3 | async-start | bytes 6291456 | tf_op jit(solution)/shard_map/all_to_all | solution.py:175
  110.4 25.1 %all-to-all-start.1 = ((bf16[4,96,8,256]{3,2,1,0:T(8,128)(2,1)}), bf16[4,96,8,256]{3,2,1,0:T(8,128)(2,1)S(1)}, u32[]{:S(2)}, u32[]{:S(2)}) async-start(bf16[4,96,8,256]{3,2,1,0:T(8,128)(2,1)} %bitcast.48), calls=%async_computation.1 | async-start | bytes 3145728 | tf_op jit(solution)/shard_map/all_to_all | solution.py:192
  135.5 13.7 %all-to-all-start.4 = ((bf16[8,2,128,128]{3,2,1,0:T(8,128)(2,1)}), bf16[8,2,128,128]{3,2,1,0:T(8,128)(2,1)}, u32[]{:S(2)}, u32[]{:S(2)}) async-start(bf16[8,2,128,128]{3,2,1,0:T(8,128)(2,1)} %pair.4), calls=%async_computation.4 | async-start | bytes 1048576 | tf_op jit(solution)/shard_map/all_to_all | solution.py:198
  149.2 13.2 %all-to-all-start.5 = ((bf16[8,2,128,128]{3,2,1,0:T(8,128)(2,1)}), bf16[8,2,128,128]{3,2,1,0:T(8,128)(2,1)}, u32[]{:S(2)}, u32[]{:S(2)}) async-start(bf16[8,2,128,128]{3,2,1,0:T(8,128)(2,1)} %pair.5), calls=%async_computation.5 | async-start | bytes 1048576 | tf_op jit(solution)/shard_map/all_to_all | solution.py:198
  162.4 12.6 %all-to-all-start.6 = ((bf16[8,2,128,128]{3,2,1,0:T(8,128)(2,1)}), bf16[8,2,128,128]{3,2,1,0:T(8,128)(2,1)}, u32[]{:S(2)}, u32[]{:S(2)}) async-start(bf16[8,2,128,128]{3,2,1,0:T(8,128)(2,1)} %pair.6), calls=%async_computation.6 | async-start | bytes 1048576 | tf_op jit(solution)/shard_map/all_to_all | solution.py:198
  174.9 12.4 %all-to-all-start.7 = ((bf16[8,2,128,128]{3,2,1,0:T(8,128)(2,1)}), bf16[8,2,128,128]{3,2,1,0:T(8,128)(2,1)}, u32[]{:S(2)}, u32[]{:S(2)}) async-start(bf16[8,2,128,128]{3,2,1,0:T(8,128)(2,1)} %pair.7), calls=%async_computation.7 | async-start | bytes 1048576 | tf_op jit(solution)/shard_map/all_to_all | solution.py:198

commit v2 on v1

v2 whole, which is shorter than its diff:
```python
import math

import jax
import jax.numpy as jnp
from jax import lax
from jax.experimental import pallas as pl
from jax.experimental.pallas import tpu as pltpu
from jax.sharding import Mesh
from jax.sharding import PartitionSpec as P


HEADS = 8
HC = 32
EPS = 1e-05
SEQ = ("xh", "c")
ROWS = ("yl", "z")
XY = ("xl", "yh", "xh")
NT = (((1,), (1,)), ((), ()))
NN = (((1,), (0,)), ((), ()))
TN = (((0,), (0,)), ((), ()))
F32 = jnp.float32
BF16 = jnp.bfloat16


def dot(a, b, dims):
    return lax.dot_general(a, b, dims, preferred_element_type=F32)


def after(*arrays):
    return [pl.BlockSpec(memory_space=pl.ANY)] * len(arrays)


def front_kernel(q_ref, x_ref, wf_ref, n0, n1, n2, n3, l0, l1, l2, l3, r_ref, nf, nb, lf, rf, lb):
    rows = x_ref.shape[0]
    seqs = rows // 32
    step = 256

    def one(n, _):
        at = pl.ds(pl.multiple_of(n * step, step), step)
        v = x_ref[at, :].astype(F32)
        v = v - jnp.mean(v, axis=-1, keepdims=True)
        spread = jnp.mean(v * v, axis=-1, keepdims=True)
        y = v * lax.rsqrt(spread + EPS)
        nf[0, at, :] = y[:, :128]
        nf[1, at, :] = y[:, 128:]
        return 0

    lax.fori_loop(0, rows // step, one, 0)
    for r in range(32):
        at = pl.ds(r, seqs, stride=32)
        x = jnp.concatenate([nf[0, at, :], nf[1, at, :]], axis=1).astype(BF16)
        nb[r] = x
        f = dot(wf_ref[...], x, NT)
        lf[r * 32:(r + 1) * 32, :seqs] = f[:32]
        rf[pl.ds(r, 32, stride=32), :] = jnp.concatenate([f[32:], jnp.zeros((32, 128 - seqs), F32)], axis=1)
    for g in range(8):
        sl = slice(g * 128, (g + 1) * 128)
        r_ref[:, sl] = rf[sl, :].T[:seqs].astype(BF16)
        lb[g // 2, :, (g % 2) * 128:(g % 2 + 1) * 128] = lf[sl, :].T[:seqs].astype(BF16)
    q = q_ref[0]
    for k, (n_ref, l_ref) in enumerate(((n0, l0), (n1, l1), (n2, l2), (n3, l3))):
        for r in range(8):
            n_ref[r] = nb[(q ^ k) * 8 + r]
        l_ref[...] = lb[q ^ k]


def front(q, x, wf_t):
    rows = x.shape[0]
    seqs = rows // 32
    vmem = pl.BlockSpec(memory_space=pltpu.VMEM)
    outs = pl.pallas_call(
        front_kernel,
        in_specs=[pl.BlockSpec(memory_space=pltpu.SMEM), vmem, vmem],
        out_shape=[jax.ShapeDtypeStruct((8, seqs, 256), BF16)] * 4
        + [jax.ShapeDtypeStruct((seqs, 256), BF16)] * 4
        + [jax.ShapeDtypeStruct((seqs, 1024), BF16)],
        scratch_shapes=[
            pltpu.VMEM((2, rows, 128), F32),
            pltpu.VMEM((32, seqs, 256), BF16),
            pltpu.VMEM((1024, 128), F32),
            pltpu.VMEM((1024, 128), F32),
            pltpu.VMEM((4, seqs, 256), BF16),
        ],
        cost_estimate=pl.CostEstimate(flops=800_000_000, transcendentals=rows, bytes_accessed=4 * rows * 256),
        name="front",
    )(q, x, wf_t)
    return outs[:4], outs[4:8], outs[8]


def merge_left(pieces):
    seqs = pieces[0].shape[0] * 4

    def kernel(p0, p1, p2, p3, o_ref):
        x = jnp.concatenate([p0[...], p1[...], p2[...], p3[...]], axis=0).astype(F32)
        o_ref[...] = x.T.astype(BF16)

    vmem = pl.BlockSpec(memory_space=pltpu.VMEM)
    out = pl.pallas_call(
        kernel,
        in_specs=[vmem] * 4,
        out_shape=jax.ShapeDtypeStruct((256, seqs), BF16),
        cost_estimate=pl.CostEstimate(flops=100_000_000, transcendentals=0, bytes_accessed=4 * 256 * seqs),
        name="merge_left",
    )(*pieces)
    return out.reshape(8, 32, seqs)


def attention_kernel(which, n_wait, *refs):
    x_refs, (wq_ref, wk_ref, wv_ref, wg_ref, wo_ref) = refs[:4], refs[4:9]
    oa, ob, of = refs[9 + n_wait:]
    r = pl.program_id(0)
    part = x_refs[0].shape[1]
    x = jnp.concatenate([b[0] for b in x_refs], axis=0)
    mine = x[which * part:(which + 2) * part]
    seqs = 2 * part
    q_t = dot(wq_ref[...], mine, NT).astype(BF16)
    keys = dot(x, wk_ref[...], NN).astype(BF16)
    v_t = dot(wv_ref[...], x, NT).astype(BF16)
    g_t = jax.nn.sigmoid(dot(wg_ref[...], mine, NT))
    ones = jnp.ones((16, 4 * part), BF16)
    scale = math.log2(math.e) / math.sqrt(HC)
    gated = []

    def spread(h):
        parts = []
        if h:
            parts.append(jnp.zeros((h * HC, seqs), BF16))
        parts.append(q_t[h * HC:(h + 1) * HC])
        if h < HEADS - 1:
            parts.append(jnp.zeros(((HEADS - 1 - h) * HC, seqs), BF16))
        return jnp.concatenate(parts, axis=0)

    for p in range(HEADS // 4):
        rhs = jnp.concatenate([spread(4 * p + u) for u in range(4)], axis=1)
        scores = dot(keys, rhs, NN)
        weights = jnp.exp2(scores * scale).astype(BF16)
        for u in range(2):
            h = 4 * p + 2 * u
            lhs = jnp.concatenate([v_t[h * HC:(h + 2) * HC], ones], axis=0)
            out = dot(lhs, weights[:, u * 2 * seqs:(u + 1) * 2 * seqs], NN)
            inv = 1.0 / out[2 * HC:2 * HC + 1]
            for w in range(2):
                lanes = slice(w * seqs, (w + 1) * seqs)
                att = out[w * HC:(w + 1) * HC, lanes] * inv[:, lanes]
                gated.append((g_t[(h + w) * HC:(h + w + 1) * HC] * att).astype(BF16))
    gated = jnp.concatenate(gated, axis=0)
    update = dot(gated, wo_ref[...], TN)
    of[0, pl.ds(r, seqs, stride=8), :] = update[:, :128]
    of[1, pl.ds(r, seqs, stride=8), :] = update[:, 128:]

    @pl.when(r == pl.num_programs(0) - 1)
    def _():
        for k, o_ref in enumerate((oa, ob)):
            sl = slice(k * part * 8, (k + 1) * part * 8)
            o_ref[:, :128] = of[0, sl, :].astype(BF16)
            o_ref[:, 128:] = of[1, sl, :].astype(BF16)


def attention(which, blocks, weights, waits):
    count, part, width = blocks[0].shape
    full = pl.BlockSpec((256, 256), lambda r: (0, 0))
    seqs = 4 * part
    return pl.pallas_call(
        lambda *refs: attention_kernel(which, len(waits), *refs),
        grid=(count,),
        in_specs=[pl.BlockSpec((1, part, width), lambda r: (r, 0, 0))] * 4 + [full] * 5 + after(*waits),
        out_specs=[pl.BlockSpec((part * count, width), lambda r: (0, 0))] * 2,
        out_shape=[jax.ShapeDtypeStruct((part * count, width), BF16)] * 2,
        scratch_shapes=[pltpu.VMEM((2, 2 * part * count, 128), F32)],
        cost_estimate=pl.CostEstimate(
            flops=count * (seqs * seqs * 256 * 9 + 2 * seqs * 256 * 256 * 4),
            transcendentals=count * HEADS * seqs * seqs // 2,
            bytes_accessed=4 * count * seqs * width,
        ),
    )(*blocks, *weights, *waits)


def pair_kernel(scaling, i_ref, *refs):
    l_refs, (n_ref, f_ref, w_ref) = refs[:4], refs[4:7]
    o_ref, scr = refs[-2:]
    _, count, _, seqs = l_refs[0].shape
    rows = 8 * count
    left = jnp.concatenate([l[b].reshape(count * 32, seqs) for b in range(2) for l in l_refs], axis=0)
    for n in range(8):
        lanes = slice(n * 128, (n + 1) * 128)
        src = [
            jnp.concatenate([x[2 * b + h, :, lanes] for h in range(2) for x in (n_ref, f_ref)], axis=0)
            for b in range(4)
        ]
        right = jnp.concatenate([x[:, e * 32:(e + 1) * 32] for e in range(4) for x in src], axis=1)
        o = dot(left, right, NN).astype(BF16)
        for i in range(rows):
            for e in range(4):
                row = (n * 4 + e) * 32
                scr[i, row:row + 32, :] = o[i * 32:(i + 1) * 32, e * 128:(e + 1) * 128]
    at = i_ref[0]
    for k in range(rows // 2):
        rhs = jnp.concatenate([scr[2 * k], scr[2 * k + 1]], axis=1)
        t = dot(w_ref[...], rhs, NN) * scaling
        for u in range(2):
            i = 2 * k + u
            o_ref[at ^ (i // count), i % count] = t[:, u * 128:(u + 1) * 128].T.astype(BF16)


def pair_block(index, left, near, far, w_t, part, parts, scaling, waits):
    seqs = left[0].shape[-1]
    count = 8 // parts
    half = pl.BlockSpec(near.shape, lambda g: (0, 0, 0))
    return pl.pallas_call(
        lambda *refs: pair_kernel(scaling, *refs),
        grid=(1,),
        in_specs=[pl.BlockSpec(memory_space=pltpu.SMEM)]
        + [pl.BlockSpec((2, count, 32, seqs), lambda g: (0, part, 0, 0))] * 4
        + [half, half, pl.BlockSpec((128, 1024), lambda g: (0, 0))] + after(*waits),
        out_specs=pl.BlockSpec((8, count, 128, 128), lambda g: (0, 0, 0, 0)),
        out_shape=jax.ShapeDtypeStruct((8, count, 128, 128), BF16),
        scratch_shapes=[pltpu.VMEM((8 * count, 1024, 128), BF16)],
        cost_estimate=pl.CostEstimate(
            flops=(2 * 256 * 4096 * seqs + 2 * 8 * 128 * 128 * 1024) * count,
            transcendentals=0,
            bytes_accessed=2 * (4096 + 512) * seqs,
        ),
    )(index, *left, near, far, w_t, *waits)


def place_update(q, blocks):
    seqs, own, width = blocks[0].shape

    def kernel(q_ref, b0, b1, b2, b3, o_ref):
        q = q_ref[0]
        for k, b in enumerate((b0, b1, b2, b3)):
            o_ref[:, q ^ k] = b[...]

    vmem = pl.BlockSpec(memory_space=pltpu.VMEM)
    out = pl.pallas_call(
        kernel,
        in_specs=[pl.BlockSpec(memory_space=pltpu.SMEM)] + [vmem] * 4,
        out_specs=vmem,
        out_shape=jax.ShapeDtypeStruct((seqs, 4, own, width), BF16),
        cost_estimate=pl.CostEstimate(flops=300_000_000, transcendentals=0, bytes_accessed=16 * seqs * own * width),
        name="place_update",
    )(q, *blocks)
    return out.reshape(seqs, 4 * own, width)


def place_pair(col, got, prior, part, parts):
    count = 8 // parts

    def kernel(c_ref, g_ref, *refs):
        o_ref = refs[-1]
        for b in range(4):
            v = c_ref[0] ^ b
            a = (v % 2) * 2 + v // 2
            for k in range(8):
                o_ref[:, a, k] = g_ref[k, :, b]

    shape = (8, 4, 8, 32, 128)
    more = [] if prior is None else [prior]
    return pl.pallas_call(
        kernel,
        grid=(1,),
        in_specs=[
            pl.BlockSpec(memory_space=pltpu.SMEM),
            pl.BlockSpec((8, count, 4, 32, 128), lambda g: (0, 0, 0, 0, 0)),
        ] + after(*more),
        out_specs=pl.BlockSpec((count, *shape[1:]), lambda g: (part, 0, 0, 0, 0)),
        out_shape=jax.ShapeDtypeStruct(shape, BF16),
        input_output_aliases={2: 0} if more else {},
        cost_estimate=pl.CostEstimate(flops=300_000_000, transcendentals=0, bytes_accessed=4_000_000),
        name="place_pair",
    )(col, got.reshape(8, count, 4, 32, 128), *more)


def swap(x, axes, k):
    n = lax.axis_size(axes)
    return lax.ppermute(x, axes, [(j, j ^ k) for j in range(n)])


def layer(alignment, query_weight, w_keyval, w_gate, output_weight, w_factors, w_pair_out):
    seqs, residues, width = alignment.shape
    own = residues // 4
    total = seqs * 4
    q1 = lax.axis_index(SEQ).astype(jnp.int32)[None]
    row = lax.axis_index(ROWS).astype(jnp.int32)[None]
    col = lax.axis_index(("yh", "xl")).astype(jnp.int32)[None]
    weights = (query_weight.T, w_keyval[:, :256], w_keyval[:, 256:].T, w_gate.T, output_weight)
    w_t = w_pair_out.reshape(32, 32, 128).transpose(2, 1, 0).reshape(128, 1024)

    normed, lefts, right = front(q1, alignment.reshape(seqs * residues, width), w_factors.T)
    pieces = [lefts[0]] + [swap(lefts[k], SEQ, k) for k in (1, 2, 3)]
    x4 = jnp.stack([right, swap(right, XY, 1), swap(right, XY, 4), swap(right, XY, 5)])
    blocks = [normed[0]] + [swap(normed[k], SEQ, k) for k in (1, 2, 3)]
    near = jnp.concatenate([x4, swap(x4, XY, 2)], axis=0)
    left = merge_left(pieces)
    left2 = jnp.stack([left, swap(left, ROWS, 4)])
    left4 = [left2] + [swap(left2, ROWS, k) for k in (1, 2, 3)]
    far = swap(near, ("c",), 1)

    scaling = 1.0 / total
    u2, u3 = attention(2, blocks, weights, (left2, x4))
    backs = [None, None, swap(u2, SEQ, 2), swap(u3, SEQ, 3)]
    out0 = pair_block(row, left4, near, far, w_t, 0, 2, scaling, (u2,))
    got0 = lax.all_to_all(out0, ROWS, 0, 0)
    out1 = pair_block(row, left4, near, far, w_t, 1, 2, scaling, (out0,))
    got1 = lax.all_to_all(out1, ROWS, 0, 0)
    u0, u1 = attention(0, blocks, weights, (out1,))
    backs[0], backs[1] = u0, swap(u1, SEQ, 1)
    pair = place_pair(col, got0, None, 0, 2)
    pair = place_pair(col, got1, pair, 1, 2)
    alignment_update = place_update(q1, [b.reshape(seqs, own, width) for b in backs])
    return alignment_update, pair.reshape(8, 1024, 128)


def solution(mesh):
    split = Mesh(
        mesh.devices.reshape(2, 2, 2, 4, 2, 2), ("xl", "yh", "yl", "z", "xh", "c")
    )
    res = ("xl", "yh", "yl", "z")
    in_specs = (P(SEQ, res, None), P(), P(), P(), P(), P(), P())
    out_specs = (P(SEQ, res, None), P((*res, *SEQ), None, None))
    return jax.shard_map(layer, mesh=split, in_specs=in_specs, out_specs=out_specs, check_vma=False)
```

time: 193 us -> 150 us (0.78)
  blocking collectives: 53.1 us -> 0 us
  Pallas kernels: 49.5 us -> 63.3 us
  local copies, waits for them, and re-layouts: 19.4 us -> 6.64 us
  starting transfers between devices: 25.3 us -> 34.8 us
    all_to_all x2 -> x0, blocking collectives: 53.1 us -> none  [the longest x1 27.3 us: spread_to(): return lax.all_to_all(jnp.broadcast_to(x[None], (n, *x.shape)), axes, 0, 0)]
    ppermute x0 -> x18, waiting for transfers between devices: none -> 34.9 us  [swap(): return lax.ppermute(x, axes, [(j, j ^ k) for j in range(n)])]
    all_to_all x6 -> x2, waiting for transfers between devices: 40.3 us -> 5.42 us  [the longest x1 5.42 us: layer(): got0 = lax.all_to_all(out0, ROWS, 0, 0)]
    ppermute x0 -> x18, starting transfers between devices: none -> 26 us  [swap(): return lax.ppermute(x, axes, [(j, j ^ k) for j in range(n)])]
    pallas_call x2 -> x7, Pallas kernels: 26.2 us -> 45 us  [the longest x2 28.6 us: attention(): pl.pallas_call(lambda *refs: attention_kernel(which, len(waits), *refs),...]
    all_to_all x6 -> x2, starting transfers between devices: 25.3 us -> 8.87 us  [the longest x1 5.23 us: layer(): got0 = lax.all_to_all(out0, ROWS, 0, 0)]
    transpose x7 -> x1, local copies, waits for them, and re-layouts: 9.61 us -> 0.1 us  [layer(): w_t = w_pair_out.reshape(32, 32, 128).transpose(2, 1, 0).reshape(128, 1024)]
    pallas_call x4 -> x2, Pallas kernels: 23.3 us -> 18.3 us  [pair_block(): pl.pallas_call(lambda *refs: pair_kernel(scaling, *refs), grid=(1,), in_s...]
  transfers between devices with their start and end apart: 6 -> 20, of which waited for: 6 -> 10; matrix products, arithmetic and copies ran while one was open for 7% -> 3% of each run, Pallas kernels for 23% -> 30%
where the time goes in v2:
time: 150 us; the launch traced here: 148 us
  Pallas kernels  63.3 us (42%)
  waiting for transfers between devices  40.4 us (27%)
  starting transfers between devices  34.8 us (23%)
  local copies, waits for them, and re-layouts  6.64 us (4%)
  other arithmetic  2 us (1%)
    ppermute x18, waiting for transfers between devices, swap(): return lax.ppermute(x, axes, [(j, j ^ k) for j in range(n)])  34.9 us
    pallas_call x2, Pallas kernels, attention(): pl.pallas_call(lambda *refs: attention_kernel(which, len(waits), *refs),...  28.6 us
    ppermute x18, starting transfers between devices, swap(): return lax.ppermute(x, axes, [(j, j ^ k) for j in range(n)])  26 us
    pallas_call x2, Pallas kernels, pair_block(): pl.pallas_call(lambda *refs: pair_kernel(scaling, *refs), grid=(1,), in_s...  18.3 us
    pallas_call x1, Pallas kernels, front(): pl.pallas_call(front_kernel, in_specs=[pl.BlockSpec(memory_space=pltpu.SM...  7.44 us
    all_to_all x1, waiting for transfers between devices, layer(): got0 = lax.all_to_all(out0, ROWS, 0, 0)  5.42 us
    all_to_all x1, starting transfers between devices, layer(): got0 = lax.all_to_all(out0, ROWS, 0, 0)  5.23 us
    unnamed x55, local copies, waits for them, and re-layouts  4.98 us
  transfers between devices with their start and end apart: 20, of which 10 were waited for; matrix products, arithmetic and copies ran while one was open for 3% of the time, Pallas kernels for 30%

profile of v2, /device:TPU:0, one launch (start us, length us, event | category | flops | bytes accessed | tf_op | source)
XLA Modules:
  0.0 148.0 jit_solution(10985862974899186928)
XLA Ops:
  0.6 7.4 %front.1 = (bf16[8,96,256]{2,1,0:T(8,128)(2,1)}, bf16[8,96,256]{2,1,0:T(8,128)(2,1)}, bf16[8,96,256]{2,1,0:T(8,128)(2,1)}, bf16[8,96,256]{2,1,0:T(8,128)(2,1)}, ...) custom-call(s32[1]{0:T(128)} %bitcast.q_ref, ...), custom_call_target="tpu_custom_call" | custom-call | flops 800000000 | bytes 3145728 | tf_op jit(solution)/shard_map/front/pallas_call | solution.py:71
  8.1 2.9 %collective-permute-start.12 = (bf16[96,1024]{1,0:T(8,128)(2,1)}, bf16[96,1024]{1,0:T(8,128)(2,1)S(1)}, u32[]{:S(2)}, u32[]{:S(2)}) collective-permute-start(bf16[96,1024]{1,0:T(8,128)(2,1)} %get-tuple-element.23), channel_id=1, source_target_pairs={{0,66},{2,64},{32,98},{34,96},{64,2},{66,0},{96,34},{98,32},{1,67}... | collective-permute-start | bytes 589832 | tf_op jit(solution)/shard_map/ppermute | solution.py:276
  11.2 1.6 %collective-permute-start.10 = (bf16[96,1024]{1,0:T(8,128)(2,1)}, bf16[96,1024]{1,0:T(8,128)(2,1)S(1)}, u32[]{:S(2)}, u32[]{:S(2)}) collective-permute-start(bf16[96,1024]{1,0:T(8,128)(2,1)} %get-tuple-element.23), channel_id=1, source_target_pairs={{0,2},{2,0},{32,34},{34,32},{64,66},{66,64},{96,98},{98,96},{1,3},... | collective-permute-start | bytes 589832 | tf_op jit(solution)/shard_map/ppermute | solution.py:276
  12.8 3.5 %collective-permute-done.12 = bf16[96,1024]{1,0:T(8,128)(2,1)S(1)} collective-permute-done((bf16[96,1024]{1,0:T(8,128)(2,1)}, bf16[96,1024]{1,0:T(8,128)(2,1)S(1)}, u32[]{:S(2)}, u32[]{:S(2)}) %collective-permute-start.12) | collective-permute-done | bytes 196640 | tf_op jit(solution)/shard_map/ppermute | solution.py:276
  16.3 2.7 %collective-permute-done.11 = bf16[96,1024]{1,0:T(8,128)(2,1)S(1)} collective-permute-done((bf16[96,1024]{1,0:T(8,128)(2,1)}, bf16[96,1024]{1,0:T(8,128)(2,1)S(1)}, u32[]{:S(2)}, u32[]{:S(2)}) %collective-permute-start.11) | collective-permute-done | bytes 196640 | tf_op jit(solution)/shard_map/ppermute | solution.py:276
  19.0 2.6 %collective-permute-done.10 = bf16[96,1024]{1,0:T(8,128)(2,1)S(1)} collective-permute-done((bf16[96,1024]{1,0:T(8,128)(2,1)}, bf16[96,1024]{1,0:T(8,128)(2,1)S(1)}, u32[]{:S(2)}, u32[]{:S(2)}) %collective-permute-start.10) | collective-permute-done | bytes 196640 | tf_op jit(solution)/shard_map/ppermute | solution.py:276
  21.6 1.0 pad_maximum_fusion.refs_10_
  22.7 3.4 %collective-permute-start.13 = (bf16[4,96,1024]{2,1,0:T(8,128)(2,1)S(1)}, bf16[4,96,1024]{2,1,0:T(8,128)(2,1)S(1)}, u32[]{:S(2)}, u32[]{:S(2)}) collective-permute-start(bf16[4,96,1024]{2,1,0:T(8,128)(2,1)S(1)} %pad_maximum_fusion.refs_10_), channel_id=1, source_target_pairs={{0,32},{2,34},{32,0},{34,2},{64,96},{66,98},{96,64},{98,66},{1,33}... | collective-permute-start | bytes 2359304 | tf_op jit(solution)/shard_map/ppermute | solution.py:276
  26.2 16.3 %collective-permute-done.13 = bf16[4,96,1024]{2,1,0:T(8,128)(2,1)S(1)} collective-permute-done((bf16[4,96,1024]{2,1,0:T(8,128)(2,1)S(1)}, bf16[4,96,1024]{2,1,0:T(8,128)(2,1)S(1)}, u32[]{:S(2)}, u32[]{:S(2)}) %collective-permute-start.13) | collective-permute-done | bytes 786464 | tf_op jit(solution)/shard_map/ppermute | solution.py:276
  43.1 2.0 %collective-permute-start.4 = (bf16[96,256]{1,0:T(8,128)(2,1)S(1)}, bf16[96,256]{1,0:T(8,128)(2,1)S(1)}, u32[]{:S(2)}, u32[]{:S(2)}) collective-permute-start(bf16[96,256]{1,0:T(8,128)(2,1)S(1)} %copy-done.22), channel_id=1, source_target_pairs={{0,2},{1,3},{2,0},{3,1},{4,6},{5,7},{6,4},{7,5},{8,10},{9,11},{10,... | collective-permute-start | bytes 147464 | tf_op jit(solution)/shard_map/ppermute | solution.py:276
  46.8 2.0 %collective-permute-start.1 = (bf16[8,96,256]{2,1,0:T(8,128)(2,1)}, bf16[8,96,256]{2,1,0:T(8,128)(2,1)}, u32[]{:S(2)}, u32[]{:S(2)}) collective-permute-start(bf16[8,96,256]{2,1,0:T(8,128)(2,1)} %get-tuple-element.17), channel_id=1, source_target_pairs={{0,2},{1,3},{2,0},{3,1},{4,6},{5,7},{6,4},{7,5},{8,10},{9,11},{10,... | collective-permute-start | bytes 1179656 | tf_op jit(solution)/shard_map/ppermute | solution.py:276
  52.9 1.7 %merge_left.1 = bf16[256,384]{1,0:T(8,128)(2,1)} custom-call(bf16[96,256]{1,0:T(8,128)(2,1)} %get-tuple-element.19.p0, bf16[96,256]{1,0:T(8,128)(2,1)} %copy-done.12, bf16[96,256]{1,0:T(8,128)(2,1)} %copy-done.13, bf16[96,256]{1,0:T(8,128)(2,1)} %copy-done.14), custom_call_target="tpu_custom_call" | custom-call | flops 100000000 | bytes 393216 | tf_op jit(solution)/shard_map/merge_left/pallas_call | solution.py:98
  54.6 1.6 %collective-permute-start.6 = (bf16[8,32,384]{2,1,0:T(8,128)(2,1)}, bf16[8,32,384]{2,1,0:T(8,128)(2,1)S(1)}, u32[]{:S(2)}, u32[]{:S(2)}) collective-permute-start(bf16[8,32,384]{2,1,0:T(8,128)(2,1)} %bitcast.40), channel_id=1, source_target_pairs={{0,16},{4,20},{8,24},{12,28},{16,0},{20,4},{24,8},{28,12},{1,17},{... | collective-permute-start | bytes 589832 | tf_op jit(solution)/shard_map/ppermute | solution.py:276
  57.6 4.8 %collective-permute-done.6 = bf16[8,32,384]{2,1,0:T(8,128)(2,1)S(1)} collective-permute-done((bf16[8,32,384]{2,1,0:T(8,128)(2,1)}, bf16[8,32,384]{2,1,0:T(8,128)(2,1)S(1)}, u32[]{:S(2)}, u32[]{:S(2)}) %collective-permute-start.6) | collective-permute-done | bytes 196640 | tf_op jit(solution)/shard_map/ppermute | solution.py:276
  62.5 1.0 pad_maximum_fusion.1.refs_9_.refs_1_
  63.4 4.2 %collective-permute-start.9 = (bf16[2,8,32,384]{3,2,1,0:T(8,128)(2,1)S(1)}, bf16[2,8,32,384]{3,2,1,0:T(8,128)(2,1)S(1)}, u32[]{:S(2)}, u32[]{:S(2)}) collective-permute-start(bf16[2,8,32,384]{3,2,1,0:T(8,128)(2,1)S(1)} %pad_maximum_fusion.1.refs_9_.refs_1_), channel_id=1, source_target_pairs={{0,12},{4,8},{8,4},{12,0},{16,28},{20,24},{24,20},{28,16},{1,13},{... | collective-permute-start | bytes 1179656 | tf_op jit(solution)/shard_map/ppermute | solution.py:276
  68.7 14.3 %shard_map.86 = (bf16[768,256]{1,0:T(8,128)(2,1)}, bf16[768,256]{1,0:T(8,128)(2,1)}) custom-call(bf16[8,96,256]{2,1,0:T(8,128)(2,1)} %get-tuple-element.15.refs_0_, bf16[8,96,256]{2,1,0:T(8,128)(2,1)} %copy-done.17, bf16[8,96,256]{2,1,0:T(8,128)(2,1)} %collective-permute-done.1.refs_2_, bf16[8,96,256]{2,1,0:T(8,128)(2,1)} %collective-permute-done.2.refs_3_, ...), custom_call_target="tpu_custom_call" | custom-call | flops 4328521728 | bytes 3145728 | tf_op jit(solution)/shard_map/pallas_call | solution.py:163
  83.0 2.7 %collective-permute-done.9.refs_4_ = bf16[2,8,32,384]{3,2,1,0:T(8,128)(2,1)S(1)} collective-permute-done((bf16[2,8,32,384]{3,2,1,0:T(8,128)(2,1)S(1)}, bf16[2,8,32,384]{3,2,1,0:T(8,128)(2,1)S(1)}, u32[]{:S(2)}, u32[]{:S(2)}) %collective-permute-start.9) | collective-permute-done | bytes 393248 | tf_op jit(solution)/shard_map/ppermute | solution.py:276
  86.6 9.2 %shard_map.87.refs_8_ = bf16[8,4,128,128]{3,2,1,0:T(8,128)(2,1)} custom-call(s32[1]{0:T(128)} %bitcast.6.refs_0_, bf16[2,8,32,384]{3,2,1,0:T(8,128)(2,1)} %copy-done.4, bf16[2,8,32,384]{3,2,1,0:T(8,128)(2,1)} %collective-permute-done.7.refs_2_, bf16[2,8,32,384]{3,2,1,0:T(8,128)(2,1)} %copy-done.20, bf16[2,8,32,384]{3,2,1,0:T(8,128)(2,1)} %copy-done.19, ...), custom_call_target="tpu_custom_call" | custom-call | flops 4294967296 | bytes 3538944 | tf_op jit(solution)/shard_map/pallas_call | solution.py:209
  95.7 5.2 %all-to-all-start.1 = ((bf16[8,4,128,128]{3,2,1,0:T(8,128)(2,1)}), bf16[8,4,128,128]{3,2,1,0:T(8,128)(2,1)S(1)}, u32[]{:S(2)}, u32[]{:S(2)}) async-start(bf16[8,4,128,128]{3,2,1,0:T(8,128)(2,1)} %shard_map.87.refs_8_), calls=%async_computation.1 | async-start | bytes 2097152 | tf_op jit(solution)/shard_map/all_to_all | solution.py:303
  101.0 9.1 %shard_map.88.refs_9_ = bf16[8,4,128,128]{3,2,1,0:T(8,128)(2,1)} custom-call(s32[1]{0:T(128)} %bitcast.6.refs_0_, bf16[2,8,32,384]{3,2,1,0:T(8,128)(2,1)} %copy-done.4, bf16[2,8,32,384]{3,2,1,0:T(8,128)(2,1)} %collective-permute-done.7.refs_2_, bf16[2,8,32,384]{3,2,1,0:T(8,128)(2,1)} %copy-done.20, bf16[2,8,32,384]{3,2,1,0:T(8,128)(2,1)} %copy-done.19, ...), custom_call_target="tpu_custom_call" | custom-call | flops 4294967296 | bytes 3538944 | tf_op jit(solution)/shard_map/pallas_call | solution.py:209
  110.1 5.4 %all-to-all-done.1 = bf16[8,4,128,128]{3,2,1,0:T(8,128)(2,1)S(1)} async-done(((bf16[8,4,128,128]{3,2,1,0:T(8,128)(2,1)}), bf16[8,4,128,128]{3,2,1,0:T(8,128)(2,1)S(1)}, u32[]{:S(2)}, u32[]{:S(2)}) %all-to-all-start.1) | async-done | bytes 1048608 | tf_op jit(solution)/shard_map/all_to_all | solution.py:303
  115.5 3.6 %all-to-all-start = ((bf16[8,4,128,128]{3,2,1,0:T(8,128)(2,1)}), bf16[8,4,128,128]{3,2,1,0:T(8,128)(2,1)S(1)}, u32[]{:S(2)}, u32[]{:S(2)}) async-start(bf16[8,4,128,128]{3,2,1,0:T(8,128)(2,1)} %shard_map.88.refs_9_), calls=%async_computation | async-start | bytes 2097152 | tf_op jit(solution)/shard_map/all_to_all | solution.py:305
  119.2 1.5 %collective-permute-start.16 = (bf16[768,256]{1,0:T(8,128)(2,1)S(1)}, bf16[768,256]{1,0:T(8,128)(2,1)S(1)}, u32[]{:S(2)}, u32[]{:S(2)}) collective-permute-start(bf16[768,256]{1,0:T(8,128)(2,1)S(1)} %copy-done.18), channel_id=1, source_target_pairs={{0,2},{1,3},{2,0},{3,1},{4,6},{5,7},{6,4},{7,5},{8,10},{9,11},{10,... | collective-permute-start | bytes 1179656 | tf_op jit(solution)/shard_map/ppermute | solution.py:276
  120.7 1.1 collective-permute-start.17
  121.9 14.3 %shard_map.89 = (bf16[768,256]{1,0:T(8,128)(2,1)}, bf16[768,256]{1,0:T(8,128)(2,1)}) custom-call(bf16[8,96,256]{2,1,0:T(8,128)(2,1)} %get-tuple-element.15.refs_0_, bf16[8,96,256]{2,1,0:T(8,128)(2,1)} %copy-done.17, bf16[8,96,256]{2,1,0:T(8,128)(2,1)} %collective-permute-done.1.refs_2_, bf16[8,96,256]{2,1,0:T(8,128)(2,1)} %collective-permute-done.2.refs_3_, ...), custom_call_target="tpu_custom_call" | custom-call | flops 4328521728 | bytes 3145728 | tf_op jit(solution)/shard_map/pallas_call | solution.py:163
  136.2 1.1 collective-permute-start.15
  137.3 1.4 collective-permute-done.17
  139.7 2.7 %place_update.1 = bf16[96,4,8,256]{3,2,1,0:T(8,128)(2,1)} custom-call(s32[1]{0:T(128)} %bitcast.q_ref, bf16[96,8,256]{2,1,0:T(8,128)(2,1)} %bitcast.44, bf16[96,8,256]{2,1,0:T(8,128)(2,1)} %bitcast.45, bf16[96,8,256]{2,1,0:T(8,128)(2,1)} %bitcast.42, bf16[96,8,256]{2,1,0:T(8,128)(2,1)} %bitcast.43), custom_call_target="tpu_custom_call" | custom-call | flops 300000000 | bytes 3145728 | tf_op jit(solution)/shard_map/place_update/pallas_call | solution.py:235
  142.5 2.3 %place_pair.2.refs_0_ = bf16[8,4,8,32,128]{4,3,2,1,0:T(8,128)(2,1)} custom-call(s32[1]{0:T(128)} %bitcast.22.c_ref, bf16[8,4,4,32,128]{4,3,2,1,0:T(8,128)(2,1)} %bitcast.32), custom_call_target="tpu_custom_call" | custom-call | flops 300000000 | bytes 4000000 | tf_op jit(solution)/shard_map/place_pair/pallas_call | solution.py:259
  144.7 1.0 copy-done.1
  145.7 2.3 %place_pair.3 = bf16[8,4,8,32,128]{4,3,2,1,0:T(8,128)(2,1)} custom-call(s32[1]{0:T(128)} %bitcast.22.c_ref, bf16[8,4,4,32,128]{4,3,2,1,0:T(8,128)(2,1)} %bitcast.33, bf16[8,4,8,32,128]{4,3,2,1,0:T(8,128)(2,1)} %place_pair.2.refs_0_), custom_call_target="tpu_custom_call", output_to_operand_aliasing={{}: (2, {})} | custom-call | flops 300000000 | bytes 4000000 | tf_op jit(solution)/shard_map/place_pair/pallas_call | solution.py:259
  (78 shorter events, 11.0 us)
Async XLA Ops:
  8.1 18.0 %copy-start.2 = (bf16[96,1024]{1,0:T(8,128)(2,1)S(1)}, bf16[96,1024]{1,0:T(8,128)(2,1)}, u32[]{:S(2)}) copy-start(bf16[96,1024]{1,0:T(8,128)(2,1)} %get-tuple-element.23) | copy-start | bytes 589828
  8.1 8.2 %collective-permute-start.12 = (bf16[96,1024]{1,0:T(8,128)(2,1)}, bf16[96,1024]{1,0:T(8,128)(2,1)S(1)}, u32[]{:S(2)}, u32[]{:S(2)}) collective-permute-start(bf16[96,1024]{1,0:T(8,128)(2,1)} %get-tuple-element.23), channel_id=1, source_target_pairs={{0,66},{2,64},{32,98},{34,96},{64,2},{66,0},{96,34},{98,32},{1,67}... | collective-permute-start | bytes 589832 | tf_op jit(solution)/shard_map/ppermute | solution.py:276
  11.0 8.0 %collective-permute-start.11 = (bf16[96,1024]{1,0:T(8,128)(2,1)}, bf16[96,1024]{1,0:T(8,128)(2,1)S(1)}, u32[]{:S(2)}, u32[]{:S(2)}) collective-permute-start(bf16[96,1024]{1,0:T(8,128)(2,1)} %get-tuple-element.23), channel_id=1, source_target_pairs={{0,64},{2,66},{32,96},{34,98},{64,0},{66,2},{96,32},{98,34},{1,65}... | collective-permute-start | bytes 589832 | tf_op jit(solution)/shard_map/ppermute | solution.py:276
  11.2 10.4 %collective-permute-start.10 = (bf16[96,1024]{1,0:T(8,128)(2,1)}, bf16[96,1024]{1,0:T(8,128)(2,1)S(1)}, u32[]{:S(2)}, u32[]{:S(2)}) collective-permute-start(bf16[96,1024]{1,0:T(8,128)(2,1)} %get-tuple-element.23), channel_id=1, source_target_pairs={{0,2},{2,0},{32,34},{34,32},{64,66},{66,64},{96,98},{98,96},{1,3},... | collective-permute-start | bytes 589832 | tf_op jit(solution)/shard_map/ppermute | solution.py:276
  22.6 19.9 %copy-start.3 = (bf16[4,96,1024]{2,1,0:T(8,128)(2,1)}, bf16[4,96,1024]{2,1,0:T(8,128)(2,1)S(1)}, u32[]{:S(2)}) copy-start(bf16[4,96,1024]{2,1,0:T(8,128)(2,1)S(1)} %pad_maximum_fusion.refs_10_) | copy-start | bytes 2359300
  22.6 20.0 %copy-start.23 = (bf16[96,256]{1,0:T(8,128)(2,1)S(1)}, bf16[96,256]{1,0:T(8,128)(2,1)}, u32[]{:S(2)}) copy-start(bf16[96,256]{1,0:T(8,128)(2,1)} %get-tuple-element.20) | copy-start | bytes 147460
  22.6 20.5 %copy-start.22 = (bf16[96,256]{1,0:T(8,128)(2,1)S(1)}, bf16[96,256]{1,0:T(8,128)(2,1)}, u32[]{:S(2)}) copy-start(bf16[96,256]{1,0:T(8,128)(2,1)} %get-tuple-element.21) | copy-start | bytes 147460
  22.6 22.5 %copy-start.21 = (bf16[96,256]{1,0:T(8,128)(2,1)S(1)}, bf16[96,256]{1,0:T(8,128)(2,1)}, u32[]{:S(2)}) copy-start(bf16[96,256]{1,0:T(8,128)(2,1)} %get-tuple-element.22) | copy-start | bytes 147460
  22.7 26.2 %copy-start.16 = (bf16[8,96,256]{2,1,0:T(8,128)(2,1)S(1)}, bf16[8,96,256]{2,1,0:T(8,128)(2,1)}, u32[]{:S(2)}) copy-start(bf16[8,96,256]{2,1,0:T(8,128)(2,1)} %get-tuple-element.18) | copy-start | bytes 1179652
  22.7 27.2 %copy-start.10 = (bf16[256,256]{1,0:T(8,128)(2,1)S(1)}, bf16[256,256]{1,0:T(8,128)(2,1)}, u32[]{:S(2)}) copy-start(bf16[256,256]{1,0:T(8,128)(2,1)} %param.8) | copy-start | bytes 393220
  22.7 19.8 %collective-permute-start.13 = (bf16[4,96,1024]{2,1,0:T(8,128)(2,1)S(1)}, bf16[4,96,1024]{2,1,0:T(8,128)(2,1)S(1)}, u32[]{:S(2)}, u32[]{:S(2)}) collective-permute-start(bf16[4,96,1024]{2,1,0:T(8,128)(2,1)S(1)} %pad_maximum_fusion.refs_10_), channel_id=1, source_target_pairs={{0,32},{2,34},{32,0},{34,2},{64,96},{66,98},{96,64},{98,66},{1,33}... | collective-permute-start | bytes 2359304 | tf_op jit(solution)/shard_map/ppermute | solution.py:276
  26.1 24.5 %copy-start.11 = (bf16[256,256]{1,0:T(8,128)(2,1)S(1)}, bf16[256,256]{1,0:T(8,128)(2,1)}, u32[]{:S(2)}) copy-start(bf16[256,256]{1,0:T(8,128)(2,1)} %param.10) | copy-start | bytes 393220
  26.1 25.2 %copy-start.8 = (bf16[1024,128]{1,0:T(8,128)(2,1)S(1)}, bf16[1024,128]{1,0:T(8,128)(2,1)}, u32[]{:S(2)}) copy-start(bf16[1024,128]{1,0:T(8,128)(2,1)} %param.13) | copy-start | bytes 786436
  26.2 30.0 %copy-start.9 = (bf16[256,512]{1,0:T(8,128)(2,1)S(1)}, bf16[256,512]{1,0:T(8,128)(2,1)}, u32[]{:S(2)}) copy-start(bf16[256,512]{1,0:T(8,128)(2,1)} %param.9) | copy-start | bytes 786436
  42.5 40.5 %copy-start.15 = (bf16[8,96,1024]{2,1,0:T(8,128)(2,1)}, bf16[8,96,1024]{2,1,0:T(8,128)(2,1)S(1)}, u32[]{:S(2)}) copy-start(bf16[8,96,1024]{2,1,0:T(8,128)(2,1)S(1)} %constant_dynamic-update-slice_fusion.refs_5_) | copy-start | bytes 4718596
  42.5 44.0 %collective-permute-start.14 = (bf16[8,96,1024]{2,1,0:T(8,128)(2,1)S(1)}, bf16[8,96,1024]{2,1,0:T(8,128)(2,1)}, u32[]{:S(2)}, u32[]{:S(2)}) collective-permute-start(bf16[8,96,1024]{2,1,0:T(8,128)(2,1)S(1)} %constant_dynamic-update-slice_fusion.refs_5_), channel_id=1, source_target_pairs={{0,1},{1,0},{2,3},{3,2},{4,5},{5,4},{6,7},{7,6},{8,9},{9,8},{10,11... | collective-permute-start | bytes 4718600 | tf_op jit(solution)/shard_map/ppermute | solution.py:276
  42.6 4.1 %collective-permute-start.3 = (bf16[96,256]{1,0:T(8,128)(2,1)S(1)}, bf16[96,256]{1,0:T(8,128)(2,1)S(1)}, u32[]{:S(2)}, u32[]{:S(2)}) collective-permute-start(bf16[96,256]{1,0:T(8,128)(2,1)S(1)} %copy-done.23), channel_id=1, source_target_pairs={{0,1},{1,0},{2,3},{3,2},{4,5},{5,4},{6,7},{7,6},{8,9},{9,8},{10,11... | collective-permute-start | bytes 147464 | tf_op jit(solution)/shard_map/ppermute | solution.py:276
  43.1 5.7 %collective-permute-start.4 = (bf16[96,256]{1,0:T(8,128)(2,1)S(1)}, bf16[96,256]{1,0:T(8,128)(2,1)S(1)}, u32[]{:S(2)}, u32[]{:S(2)}) collective-permute-start(bf16[96,256]{1,0:T(8,128)(2,1)S(1)} %copy-done.22), channel_id=1, source_target_pairs={{0,2},{1,3},{2,0},{3,1},{4,6},{5,7},{6,4},{7,5},{8,10},{9,11},{10,... | collective-permute-start | bytes 147464 | tf_op jit(solution)/shard_map/ppermute | solution.py:276
  45.2 7.1 %collective-permute-start.5 = (bf16[96,256]{1,0:T(8,128)(2,1)S(1)}, bf16[96,256]{1,0:T(8,128)(2,1)S(1)}, u32[]{:S(2)}, u32[]{:S(2)}) collective-permute-start(bf16[96,256]{1,0:T(8,128)(2,1)S(1)} %copy-done.21), channel_id=1, source_target_pairs={{0,3},{1,2},{2,1},{3,0},{4,7},{5,6},{6,5},{7,4},{8,11},{9,10},{10,... | collective-permute-start | bytes 147464 | tf_op jit(solution)/shard_map/ppermute | solution.py:276
  46.1 21.6 %collective-permute-start = (bf16[8,96,256]{2,1,0:T(8,128)(2,1)}, bf16[8,96,256]{2,1,0:T(8,128)(2,1)S(1)}, u32[]{:S(2)}, u32[]{:S(2)}) collective-permute-start(bf16[8,96,256]{2,1,0:T(8,128)(2,1)} %get-tuple-element.16), channel_id=1, source_target_pairs={{0,1},{1,0},{2,3},{3,2},{4,5},{5,4},{6,7},{7,6},{8,9},{9,8},{10,11... | collective-permute-start | bytes 1179656 | tf_op jit(solution)/shard_map/ppermute | solution.py:276
  46.8 20.9 %collective-permute-start.1 = (bf16[8,96,256]{2,1,0:T(8,128)(2,1)}, bf16[8,96,256]{2,1,0:T(8,128)(2,1)}, u32[]{:S(2)}, u32[]{:S(2)}) collective-permute-start(bf16[8,96,256]{2,1,0:T(8,128)(2,1)} %get-tuple-element.17), channel_id=1, source_target_pairs={{0,2},{1,3},{2,0},{3,1},{4,6},{5,7},{6,4},{7,5},{8,10},{9,11},{10,... | collective-permute-start | bytes 1179656 | tf_op jit(solution)/shard_map/ppermute | solution.py:276
  48.8 19.8 %collective-permute-start.2 = (bf16[8,96,256]{2,1,0:T(8,128)(2,1)S(1)}, bf16[8,96,256]{2,1,0:T(8,128)(2,1)}, u32[]{:S(2)}, u32[]{:S(2)}) collective-permute-start(bf16[8,96,256]{2,1,0:T(8,128)(2,1)S(1)} %copy-done.16), channel_id=1, source_target_pairs={{0,3},{1,2},{2,1},{3,0},{4,7},{5,6},{6,5},{7,4},{8,11},{9,10},{10,... | collective-permute-start | bytes 1179656 | tf_op jit(solution)/shard_map/ppermute | solution.py:276
  54.6 7.9 %collective-permute-start.6 = (bf16[8,32,384]{2,1,0:T(8,128)(2,1)}, bf16[8,32,384]{2,1,0:T(8,128)(2,1)S(1)}, u32[]{:S(2)}, u32[]{:S(2)}) collective-permute-start(bf16[8,32,384]{2,1,0:T(8,128)(2,1)} %bitcast.40), channel_id=1, source_target_pairs={{0,16},{4,20},{8,24},{12,28},{16,0},{20,4},{24,8},{28,12},{1,17},{... | collective-permute-start | bytes 589832 | tf_op jit(solution)/shard_map/ppermute | solution.py:276
  63.4 22.2 %collective-permute-start.9 = (bf16[2,8,32,384]{3,2,1,0:T(8,128)(2,1)S(1)}, bf16[2,8,32,384]{3,2,1,0:T(8,128)(2,1)S(1)}, u32[]{:S(2)}, u32[]{:S(2)}) collective-permute-start(bf16[2,8,32,384]{3,2,1,0:T(8,128)(2,1)S(1)} %pad_maximum_fusion.1.refs_9_.refs_1_), channel_id=1, source_target_pairs={{0,12},{4,8},{8,4},{12,0},{16,28},{20,24},{24,20},{28,16},{1,13},{... | collective-permute-start | bytes 1179656 | tf_op jit(solution)/shard_map/ppermute | solution.py:276
  67.7 18.0 %collective-permute-start.8 = (bf16[2,8,32,384]{3,2,1,0:T(8,128)(2,1)S(1)}, bf16[2,8,32,384]{3,2,1,0:T(8,128)(2,1)S(1)}, u32[]{:S(2)}, u32[]{:S(2)}) collective-permute-start(bf16[2,8,32,384]{3,2,1,0:T(8,128)(2,1)S(1)} %pad_maximum_fusion.1.refs_9_.refs_1_), channel_id=1, source_target_pairs={{0,8},{4,12},{8,0},{12,4},{16,24},{20,28},{24,16},{28,20},{1,9},{5... | collective-permute-start | bytes 1179656 | tf_op jit(solution)/shard_map/ppermute | solution.py:276
  67.7 18.8 %collective-permute-start.7 = (bf16[2,8,32,384]{3,2,1,0:T(8,128)(2,1)S(1)}, bf16[2,8,32,384]{3,2,1,0:T(8,128)(2,1)}, u32[]{:S(2)}, u32[]{:S(2)}) collective-permute-start(bf16[2,8,32,384]{3,2,1,0:T(8,128)(2,1)S(1)} %pad_maximum_fusion.1.refs_9_.refs_1_), channel_id=1, source_target_pairs={{0,4},{4,0},{8,12},{12,8},{16,20},{20,16},{24,28},{28,24},{1,5},{5... | collective-permute-start | bytes 1179656 | tf_op jit(solution)/shard_map/ppermute | solution.py:276
  95.7 19.8 %all-to-all-start.1 = ((bf16[8,4,128,128]{3,2,1,0:T(8,128)(2,1)}), bf16[8,4,128,128]{3,2,1,0:T(8,128)(2,1)S(1)}, u32[]{:S(2)}, u32[]{:S(2)}) async-start(bf16[8,4,128,128]{3,2,1,0:T(8,128)(2,1)} %shard_map.87.refs_8_), calls=%async_computation.1 | async-start | bytes 2097152 | tf_op jit(solution)/shard_map/all_to_all | solution.py:303
  115.5 20.6 %copy-start = (bf16[8,4,128,128]{3,2,1,0:T(8,128)(2,1)}, bf16[8,4,128,128]{3,2,1,0:T(8,128)(2,1)S(1)}, u32[]{:S(2)}) copy-start(bf16[8,4,128,128]{3,2,1,0:T(8,128)(2,1)S(1)} %all-to-all-done.1) | copy-start | bytes 3145732
  115.5 29.2 %all-to-all-start = ((bf16[8,4,128,128]{3,2,1,0:T(8,128)(2,1)}), bf16[8,4,128,128]{3,2,1,0:T(8,128)(2,1)S(1)}, u32[]{:S(2)}, u32[]{:S(2)}) async-start(bf16[8,4,128,128]{3,2,1,0:T(8,128)(2,1)} %shard_map.88.refs_9_), calls=%async_computation | async-start | bytes 2097152 | tf_op jit(solution)/shard_map/all_to_all | solution.py:305
  119.2 19.5 %collective-permute-start.16 = (bf16[768,256]{1,0:T(8,128)(2,1)S(1)}, bf16[768,256]{1,0:T(8,128)(2,1)S(1)}, u32[]{:S(2)}, u32[]{:S(2)}) collective-permute-start(bf16[768,256]{1,0:T(8,128)(2,1)S(1)} %copy-done.18), channel_id=1, source_target_pairs={{0,2},{1,3},{2,0},{3,1},{4,6},{5,7},{6,4},{7,5},{8,10},{9,11},{10,... | collective-permute-start | bytes 1179656 | tf_op jit(solution)/shard_map/ppermute | solution.py:276
  120.7 18.0 %collective-permute-start.17 = (bf16[768,256]{1,0:T(8,128)(2,1)}, bf16[768,256]{1,0:T(8,128)(2,1)S(1)}, u32[]{:S(2)}, u32[]{:S(2)}) collective-permute-start(bf16[768,256]{1,0:T(8,128)(2,1)} %get-tuple-element.27), channel_id=1, source_target_pairs={{0,3},{1,2},{2,1},{3,0},{4,7},{5,6},{6,5},{7,4},{8,11},{9,10},{10,... | collective-permute-start | bytes 1179656 | tf_op jit(solution)/shard_map/ppermute | solution.py:276
  136.2 2.7 %collective-permute-start.15 = (bf16[768,256]{1,0:T(8,128)(2,1)}, bf16[768,256]{1,0:T(8,128)(2,1)S(1)}, u32[]{:S(2)}, u32[]{:S(2)}) collective-permute-start(bf16[768,256]{1,0:T(8,128)(2,1)} %get-tuple-element.26), channel_id=1, source_target_pairs={{0,1},{1,0},{2,3},{3,2},{4,5},{5,4},{6,7},{7,6},{8,9},{9,8},{10,11... | collective-permute-start | bytes 1179656 | tf_op jit(solution)/shard_map/ppermute | solution.py:276
  (12 other events, 30.1 us)

commit v3 on v2

v3 whole, which is shorter than its diff:
```python
import math

import jax
import jax.numpy as jnp
from jax import lax
from jax.experimental import pallas as pl
from jax.experimental.pallas import tpu as pltpu
from jax.sharding import Mesh
from jax.sharding import PartitionSpec as P


HEADS = 8
HC = 32
EPS = 1e-05
SEQ = ("xh", "c")
ROWS = ("yl", "z")
XY = ("xl", "yh", "xh")
SPLIT = 2
AT_ONCE = 2
NT = (((1,), (1,)), ((), ()))
NN = (((1,), (0,)), ((), ()))
TN = (((0,), (0,)), ((), ()))
TT = (((0,), (1,)), ((), ()))
F32 = jnp.float32
BF16 = jnp.bfloat16


def dot(a, b, dims):
    return lax.dot_general(a, b, dims, preferred_element_type=F32)


def after(*arrays):
    return [pl.BlockSpec(memory_space=pl.ANY)] * len(arrays)


def front_kernel(x_ref, wf_ref, n0, n1, n2, n3, l0, l1, l2, l3, r_ref, nf, nb, lf, rf, lb):
    rows = x_ref.shape[0]
    seqs = rows // 32
    step = 256

    def one(n, _):
        at = pl.ds(pl.multiple_of(n * step, step), step)
        v = x_ref[at, :].astype(F32)
        v = v - jnp.mean(v, axis=-1, keepdims=True)
        spread = jnp.mean(v * v, axis=-1, keepdims=True)
        y = v * lax.rsqrt(spread + EPS)
        nf[0, at, :] = y[:, :128]
        nf[1, at, :] = y[:, 128:]
        return 0

    lax.fori_loop(0, rows // step, one, 0)
    for r in range(32):
        at = pl.ds(r, seqs, stride=32)
        x = jnp.concatenate([nf[0, at, :], nf[1, at, :]], axis=1).astype(BF16)
        nb[r] = x
        f = dot(wf_ref[...], x, NT)
        lf[r * 32:(r + 1) * 32, :seqs] = f[:32]
        rf[pl.ds(r, 32, stride=32), :] = jnp.concatenate([f[32:], jnp.zeros((32, 128 - seqs), F32)], axis=1)
    for g in range(8):
        sl = slice(g * 128, (g + 1) * 128)
        piece = rf[sl, :].T[:seqs].astype(BF16)
        for k in range(8):
            r_ref[k, :, sl] = piece
        lb[g // 2, :, (g % 2) * 128:(g % 2 + 1) * 128] = lf[sl, :].T[:seqs].astype(BF16)
    q = lax.axis_index(SEQ)
    for k, (n_ref, l_ref) in enumerate(((n0, l0), (n1, l1), (n2, l2), (n3, l3))):
        for r in range(8):
            n_ref[r] = nb[(q ^ k) * 8 + r]
        l_ref[...] = lb[q ^ k]


def front(x, wf_t):
    rows = x.shape[0]
    seqs = rows // 32
    vmem = pl.BlockSpec(memory_space=pltpu.VMEM)
    outs = pl.pallas_call(
        front_kernel,
        in_specs=[vmem, vmem],
        out_shape=[jax.ShapeDtypeStruct((8, seqs, 256), BF16)] * 4
        + [jax.ShapeDtypeStruct((seqs, 256), BF16)] * 4
        + [jax.ShapeDtypeStruct((8, seqs, 1024), BF16)],
        scratch_shapes=[
            pltpu.VMEM((2, rows, 128), F32),
            pltpu.VMEM((32, seqs, 256), BF16),
            pltpu.VMEM((1024, 128), F32),
            pltpu.VMEM((1024, 128), F32),
            pltpu.VMEM((4, seqs, 256), BF16),
        ],
        cost_estimate=pl.CostEstimate(flops=800_000_000, transcendentals=rows, bytes_accessed=4 * rows * 256),
        name="front",
    )(x, wf_t)
    return outs[:4], outs[4:8], outs[8]


def merge_left(pieces):
    seqs = pieces[0].shape[0] * 4

    def kernel(p0, p1, p2, p3, o_ref):
        x = jnp.concatenate([p0[...], p1[...], p2[...], p3[...]], axis=0).astype(F32)
        o_ref[...] = x.T.astype(BF16)

    vmem = pl.BlockSpec(memory_space=pltpu.VMEM)
    out = pl.pallas_call(
        kernel,
        in_specs=[vmem] * 4,
        out_shape=jax.ShapeDtypeStruct((256, seqs), BF16),
        cost_estimate=pl.CostEstimate(flops=100_000_000, transcendentals=0, bytes_accessed=4 * 256 * seqs),
        name="merge_left",
    )(*pieces)
    return out.reshape(8, 32, seqs)


def attend(mine, keys, v_t, wq, wg, wo):
    seqs = mine.shape[0]
    q_t = dot(wq, mine, TT)
    q_t = jnp.concatenate([q_t, q_t], axis=1)
    first = lax.broadcasted_iota(jnp.int32, q_t.shape, 1) < seqs
    q_even = jnp.where(first, q_t, 0.0).astype(BF16)
    q_odd = jnp.where(first, 0.0, q_t).astype(BF16)
    g_t = jax.nn.sigmoid(dot(wg, mine, TT))
    ones = jnp.ones((16, keys.shape[0]), BF16)
    scale = math.log2(math.e) / math.sqrt(HC)
    gated = []

    def spread(h):
        parts = [q_even[h * HC:(h + 1) * HC], q_odd[(h + 1) * HC:(h + 2) * HC]]
        if h:
            parts.insert(0, jnp.zeros((h * HC, 2 * seqs), BF16))
        if h < HEADS - 2:
            parts.append(jnp.zeros(((HEADS - 2 - h) * HC, 2 * seqs), BF16))
        return jnp.concatenate(parts, axis=0)

    for p in range(HEADS // 4):
        rhs = jnp.concatenate([spread(4 * p), spread(4 * p + 2)], axis=1)
        scores = dot(keys, rhs, NN)
        weights = jnp.exp2(scores * scale).astype(BF16)
        tiles = []
        for u in range(3):
            h = 4 * p + u
            lhs = jnp.concatenate([v_t[h * HC:(h + 2) * HC], ones], axis=0)
            out = dot(lhs, weights[:, u * 256:(u + 1) * 256], NN)
            tiles.append(out[:2 * HC] / out[2 * HC:2 * HC + 1])
        lo, hi = slice(0, HC), slice(HC, 2 * HC)
        heads = (
            tiles[0][lo, :192],
            jnp.concatenate([tiles[0][hi, 192:], tiles[1][lo, :128]], axis=1),
            jnp.concatenate([tiles[1][hi, 128:], tiles[2][lo, :64]], axis=1),
            tiles[2][hi, 64:],
        )
        for u, att in enumerate(heads):
            h = 4 * p + u
            gated.append((g_t[h * HC:(h + 1) * HC] * att).astype(BF16))
    gated = jnp.concatenate(gated, axis=0)
    return dot(gated, wo, TN)


def finish(g, of, part, o_refs):
    @pl.when(g == pl.num_programs(0) - 1)
    def _():
        for k, o_ref in enumerate(o_refs):
            sl = slice(k * part * 8, (k + 1) * part * 8)
            o_ref[:, :128] = of[0, sl, :].astype(BF16)
            o_ref[:, 128:] = of[1, sl, :].astype(BF16)


def far_kernel(n_wait, *refs):
    x_refs, (wq_ref, wkv_ref, wg_ref, wo_ref) = refs[:4], refs[4:8]
    oa, ob, k_ref, v_ref, of = refs[8 + n_wait:]
    g = pl.program_id(0)
    at_once, part = x_refs[0].shape[:2]
    for n in range(at_once):
        x = jnp.concatenate([b[n] for b in x_refs], axis=0)
        keys = dot(x, wkv_ref[:, :256], NN).astype(BF16)
        v_t = dot(wkv_ref[:, 256:], x, TT).astype(BF16)
        k_ref[n] = keys
        v_ref[n] = v_t
        update = attend(x[2 * part:], keys, v_t, wq_ref[...], wg_ref[...], wo_ref[...])
        rows = pl.ds(g * at_once + n, 2 * part, stride=8)
        of[0, rows, :] = update[:, :128]
        of[1, rows, :] = update[:, 128:]
    finish(g, of, part, (oa, ob))


def near_kernel(n_wait, *refs):
    x_refs, (k_ref, v_ref), (wq_ref, wg_ref, wo_ref) = refs[:2], refs[2:4], refs[4:7]
    oa, ob, of = refs[7 + n_wait:]
    g = pl.program_id(0)
    at_once, part = x_refs[0].shape[:2]
    for n in range(at_once):
        mine = jnp.concatenate([b[n] for b in x_refs], axis=0)
        update = attend(mine, k_ref[n], v_ref[n], wq_ref[...], wg_ref[...], wo_ref[...])
        rows = pl.ds(g * at_once + n, 2 * part, stride=8)
        of[0, rows, :] = update[:, :128]
        of[1, rows, :] = update[:, 128:]
    finish(g, of, part, (oa, ob))


def attention(blocks, kept, weights, waits):
    count, part, width = blocks[0].shape
    seqs = 4 * part
    full = pl.BlockSpec((256, 256), lambda r: (0, 0))
    by_residue = lambda *tail: pl.BlockSpec((AT_ONCE, *tail), lambda r: (r, 0, 0))
    out_specs = [pl.BlockSpec((part * count, width), lambda r: (0, 0))] * 2
    out_shape = [jax.ShapeDtypeStruct((part * count, width), BF16)] * 2
    wq, wkv, wg, wo = weights
    if kept is None:
        kernel = far_kernel
        operands = (*blocks, wq, wkv, wg, wo)
        in_specs = [by_residue(part, width)] * 4 + [full, pl.BlockSpec((256, 512), lambda r: (0, 0)), full, full]
        out_specs += [by_residue(seqs, width), by_residue(width, seqs)]
        out_shape += [
            jax.ShapeDtypeStruct((count, seqs, width), BF16),
            jax.ShapeDtypeStruct((count, width, seqs), BF16),
        ]
    else:
        kernel = near_kernel
        operands = (*blocks[:2], *kept, wq, wg, wo)
        in_specs = [by_residue(part, width)] * 2 + [by_residue(seqs, width), by_residue(width, seqs)] + [full] * 3
    return pl.pallas_call(
        lambda *refs: kernel(len(waits), *refs),
        grid=(count // AT_ONCE,),
        in_specs=in_specs + after(*waits),
        out_specs=out_specs,
        out_shape=out_shape,
        scratch_shapes=[pltpu.VMEM((2, 2 * part * count, 128), F32)],
        cost_estimate=pl.CostEstimate(
            flops=count * (seqs * seqs * 256 * 9 + 2 * seqs * 256 * 256 * 4),
            transcendentals=count * HEADS * seqs * seqs // 2,
            bytes_accessed=4 * count * seqs * width,
        ),
    )(*operands, *waits)


def pair_kernel(scaling, r0, count, *refs):
    l_refs, right_refs, w_ref = refs[:8], refs[8:10], refs[10]
    o_ref, scr = refs[-2:]
    seqs = l_refs[0].shape[-1]
    rows = 8 * count
    xy = lax.axis_index(XY)
    left = jnp.concatenate([l[r0:r0 + count].reshape(count * 32, seqs) for l in l_refs], axis=0)
    for n in range(8):
        lanes = slice(n * 128, (n + 1) * 128)
        src = []
        for b in range(4):
            m = (b % 2) * 4 + (b // 2) * 2
            src.append(
                jnp.concatenate([x[xy ^ (m + h), :, lanes] for h in range(2) for x in right_refs], axis=0)
            )
        right = jnp.concatenate([x[:, e * 32:(e + 1) * 32] for e in range(4) for x in src], axis=1)
        o = dot(left, right, NN).astype(BF16)
        for i in range(rows):
            for e in range(4):
                row = (n * 4 + e) * 32
                scr[i, row:row + 32, :] = o[i * 32:(i + 1) * 32, e * 128:(e + 1) * 128]
    at = lax.axis_index(ROWS)
    for k in range(rows // 2):
        rhs = jnp.concatenate([scr[2 * k], scr[2 * k + 1]], axis=1)
        t = dot(w_ref[...], rhs, NN) * scaling
        for u in range(2):
            i = 2 * k + u
            o_ref[at ^ (i // count), i % count] = t[:, u * 128:(u + 1) * 128].T.astype(BF16)


def pair_block(left, rights, w_t, r0, count, scaling, waits):
    seqs = left[0].shape[-1]
    vmem = pl.BlockSpec(memory_space=pltpu.VMEM)
    return pl.pallas_call(
        lambda *refs: pair_kernel(scaling, r0, count, *refs),
        in_specs=[vmem] * 11 + after(*waits),
        out_specs=vmem,
        out_shape=jax.ShapeDtypeStruct((8, count, 128, 128), BF16),
        scratch_shapes=[pltpu.VMEM((8 * count, 1024, 128), BF16)],
        cost_estimate=pl.CostEstimate(
            flops=(2 * 256 * 4096 * seqs + 2 * 8 * 128 * 128 * 1024) * count,
            transcendentals=0,
            bytes_accessed=2 * (4096 + 512) * seqs,
        ),
    )(*left, *rights, w_t, *waits)


def place(blocks, wheres, shape, prior):
    n = len(blocks)
    more = [] if prior is None else [prior]

    def kernel(*refs):
        ins, out, sems = refs[:n], refs[-2], refs[-1]
        pairs = [p for b, where in zip(ins, wheres) for p in where(b, out)]
        copies = [pltpu.make_async_copy(a, to, sems.at[k]) for k, (a, to) in enumerate(pairs)]
        for c in copies:
            c.start()
        for c in copies:
            c.wait()

    hbm = pl.BlockSpec(memory_space=pltpu.HBM)
    return pl.pallas_call(
        kernel,
        in_specs=[pl.BlockSpec(memory_space=pltpu.VMEM)] * n + [hbm] * len(more),
        out_specs=hbm,
        out_shape=jax.ShapeDtypeStruct(shape, BF16),
        scratch_shapes=[pltpu.SemaphoreType.DMA((32,))],
        input_output_aliases={n: 0} if more else {},
        cost_estimate=pl.CostEstimate(flops=300_000_000, transcendentals=0, bytes_accessed=4_000_000),
    )(*blocks, *more)


def place_update(blocks):
    seqs, own, width = blocks[0].shape

    def to_group(k):
        return lambda b, out: [(b, out.at[:, lax.axis_index(SEQ) ^ k])]

    out = place(blocks, [to_group(k) for k in range(4)], (seqs, 4, own, width), None)
    return out.reshape(seqs, 4 * own, width)


def place_pair(got, prior, r0):
    count = got.shape[1]

    def where(g, out):
        pairs = []
        for b in range(4):
            v = lax.axis_index(("yh", "xl")) ^ b
            a = (v % 2) * 2 + v // 2
            for k in range(8):
                pairs.append((g.at[k, :, b], out.at[pl.ds(r0, count), a, k]))
        return pairs

    return place([got.reshape(8, count, 4, 32, 128)], [where], (8, 4, 8, 32, 128), prior)


def swap(x, axes, k):
    n = lax.axis_size(axes)
    return lax.ppermute(x, axes, [(j, j ^ k) for j in range(n)])


def layer(alignment, query_weight, w_keyval, w_gate, output_weight, w_factors, w_pair_out):
    seqs, residues, width = alignment.shape
    own = residues // 4
    total = seqs * 4
    normed, lefts, right = front(alignment.reshape(seqs * residues, width), w_factors.T)
    blocks = [normed[0]] + [swap(normed[k], SEQ, k) for k in (1, 2, 3)]
    near = lax.all_to_all(right, XY, 0, 0)
    pieces = [lefts[0]] + [swap(lefts[k], SEQ, k) for k in (1, 2, 3)]
    left = merge_left(pieces)
    left_y = swap(left, ROWS, 4)
    left8 = [left] + [swap(left, ROWS, k) for k in (1, 2, 3)]
    left8 += [left_y] + [swap(left_y, ROWS, k) for k in (1, 2, 3)]
    rights = [near, swap(near, ("c",), 1)]

    w_pair_out, left = lax.optimization_barrier((w_pair_out, left))
    weights = (query_weight, w_keyval, w_gate, output_weight)
    w_t = w_pair_out.reshape(32, 32, 128).transpose(2, 1, 0).reshape(128, 1024)
    scaling = 1.0 / total
    u2, u3, *kept = attention(blocks, None, weights, (left_y,))
    backs = [None, None, swap(u2, SEQ, 2), swap(u3, SEQ, 3)]
    out0 = pair_block(left8, rights, w_t, 0, SPLIT, scaling, (u2,))
    got0 = lax.all_to_all(out0, ROWS, 0, 0)
    out1 = pair_block(left8, rights, w_t, SPLIT, 8 - SPLIT, scaling, (out0,))
    got1 = lax.all_to_all(out1, ROWS, 0, 0)
    pair = place_pair(got0, None, 0)
    u0, u1 = attention(blocks, kept, weights, (out1, pair))
    backs[0], backs[1] = u0, swap(u1, SEQ, 1)
    alignment_update = place_update([b.reshape(seqs, own, width) for b in backs])
    pair = place_pair(got1, pair, SPLIT)
    return alignment_update, pair.reshape(8, 1024, 128)


def solution(mesh):
    split = Mesh(
        mesh.devices.reshape(2, 2, 2, 4, 2, 2), ("xl", "yh", "yl", "z", "xh", "c")
    )
    res = ("xl", "yh", "yl", "z")
    in_specs = (P(SEQ, res, None), P(), P(), P(), P(), P(), P())
    out_specs = (P(SEQ, res, None), P((*res, *SEQ), None, None))
    return jax.shard_map(layer, mesh=split, in_specs=in_specs, out_specs=out_specs, check_vma=False)
```

time: 150 us -> 151 us (level)
  blocking collectives: 0 us -> 30 us
  waiting for transfers between devices: 40.4 us -> 18.3 us
  starting transfers between devices: 34.8 us -> 32.1 us
  other arithmetic: 2 us -> 0 us
    all_to_all x0 -> x1, blocking collectives: none -> 30 us  [layer(): near = lax.all_to_all(right, XY, 0, 0)]
    ppermute x18 -> x17, waiting for transfers between devices: 34.9 us -> 18.3 us  [swap(): return lax.ppermute(x, axes, [(j, j ^ k) for j in range(n)])]
    all_to_all x1, waiting for transfers between devices: 5.42 us -> 0.01 us  [layer(): got0 = lax.all_to_all(out0, ROWS, 0, 0)]
    ppermute x18 -> x17, starting transfers between devices: 26 us -> 21.1 us  [swap(): return lax.ppermute(x, axes, [(j, j ^ k) for j in range(n)])]
    all_to_all x1, starting transfers between devices: 3.64 us -> 5.7 us  [layer(): got1 = lax.all_to_all(out1, ROWS, 0, 0)]
    another operation x2 -> x0, other arithmetic: 2 us -> none  [the longest x1 1.03 us: layer(): jnp.stack([right, swap(right, XY, 1), swap(right, XY, 4), swap(right, XY,...]
    unnamed x55 -> x48, local copies, waits for them, and re-layouts: 4.98 us -> 4.27 us
  transfers between devices with their start and end apart: 20 -> 19, of which waited for: 10 -> 6; matrix products, arithmetic and copies ran while one was open for 3% -> 1% of each run, Pallas kernels for 30% -> 30%
where the time goes in v3:
time: 151 us; the launch traced here: 149 us
  Pallas kernels  62.4 us (41%)
  starting transfers between devices  32.1 us (21%)
  blocking collectives  30 us (20%)
  waiting for transfers between devices  18.3 us (12%)
  local copies, waits for them, and re-layouts  5.21 us (3%)
    all_to_all x1, blocking collectives, layer(): near = lax.all_to_all(right, XY, 0, 0)  30 us
    pallas_call x2, Pallas kernels, attention(): pl.pallas_call(lambda *refs: kernel(len(waits), *refs), grid=(count // AT...  25.7 us
    ppermute x17, starting transfers between devices, swap(): return lax.ppermute(x, axes, [(j, j ^ k) for j in range(n)])  21.1 us
    pallas_call x2, Pallas kernels, pair_block(): pl.pallas_call(lambda *refs: pair_kernel(scaling, r0, count, *refs), in_s...  19.3 us
    ppermute x17, waiting for transfers between devices, swap(): return lax.ppermute(x, axes, [(j, j ^ k) for j in range(n)])  18.3 us
    pallas_call x1, Pallas kernels, front(): pl.pallas_call(front_kernel, in_specs=[vmem, vmem], out_shape=[jax.ShapeD...  8.05 us
    pallas_call x3, Pallas kernels, place(): pl.pallas_call(kernel, in_specs=[pl.BlockSpec(memory_space=pltpu.VMEM)] *...  7.66 us
    all_to_all x1, starting transfers between devices, layer(): got1 = lax.all_to_all(out1, ROWS, 0, 0)  5.7 us
  transfers between devices with their start and end apart: 19, of which 6 were waited for; matrix products, arithmetic and copies ran while one was open for 1% of the time, Pallas kernels for 30%

profile of v3, /device:TPU:0, one launch (start us, length us, event | category | flops | bytes accessed | tf_op | source)
XLA Modules:
  0.0 149.0 jit_solution(9977751946014374884)
XLA Ops:
  0.6 8.0 %front.1 = (bf16[8,96,256]{2,1,0:T(8,128)(2,1)}, bf16[8,96,256]{2,1,0:T(8,128)(2,1)}, bf16[8,96,256]{2,1,0:T(8,128)(2,1)}, bf16[8,96,256]{2,1,0:T(8,128)(2,1)}, ...) custom-call(bf16[3072,256]{1,0:T(8,128)(2,1)} %bitcast.31, ...), custom_call_target="tpu_custom_call" | custom-call | flops 800000000 | bytes 3145728 | tf_op jit(solution)/shard_map/front/pallas_call | solution.py:76
  8.7 30.0 %all_to_all.15.refs_8_ = bf16[8,96,1024]{2,1,0:T(8,128)(2,1)S(1)} all-to-all(bf16[8,96,1024]{2,1,0:T(8,128)(2,1)} %get-tuple-element.28), channel_id=1, replica_groups=mesh['xl'=2,'yh'=2,'yl'=2,'z'=4,'xh'=2,'c'=2] {'xl','yh','xh'}, dimensions={0} | all-to-all | bytes 3145728 | tf_op jit(solution)/shard_map/all_to_all | solution.py:342
  39.2 0.9 collective-permute-start.4
  40.1 2.1 %collective-permute-start.5 = (bf16[96,256]{1,0:T(8,128)(2,1)S(1)}, bf16[96,256]{1,0:T(8,128)(2,1)S(1)}, u32[]{:S(2)}, u32[]{:S(2)}) collective-permute-start(bf16[96,256]{1,0:T(8,128)(2,1)S(1)} %copy-done.21), channel_id=1, source_target_pairs={{0,3},{1,2},{2,1},{3,0},{4,7},{5,6},{6,5},{7,4},{8,11},{9,10},{10,... | collective-permute-start | bytes 147464 | tf_op jit(solution)/shard_map/ppermute | solution.py:333
  42.3 2.8 %collective-permute-done.4.p2 = bf16[96,256]{1,0:T(8,128)(2,1)S(1)} collective-permute-done((bf16[96,256]{1,0:T(8,128)(2,1)S(1)}, bf16[96,256]{1,0:T(8,128)(2,1)S(1)}, u32[]{:S(2)}, u32[]{:S(2)}) %collective-permute-start.4) | collective-permute-done | bytes 49184 | tf_op jit(solution)/shard_map/ppermute | solution.py:333
  45.1 0.6 collective-permute-done.5.p3
  46.3 1.7 %merge_left.1 = bf16[256,384]{1,0:T(8,128)(2,1)} custom-call(bf16[96,256]{1,0:T(8,128)(2,1)} %get-tuple-element.22.p0, bf16[96,256]{1,0:T(8,128)(2,1)} %copy-done.7, bf16[96,256]{1,0:T(8,128)(2,1)} %copy-done.8, bf16[96,256]{1,0:T(8,128)(2,1)} %copy-done.9), custom_call_target="tpu_custom_call" | custom-call | flops 100000000 | bytes 393216 | tf_op jit(solution)/shard_map/merge_left/pallas_call | solution.py:103
  47.9 4.0 %collective-permute-start.9 = (bf16[8,32,384]{2,1,0:T(8,128)(2,1)}, bf16[8,32,384]{2,1,0:T(8,128)(2,1)S(1)}, u32[]{:S(2)}, u32[]{:S(2)}) collective-permute-start(bf16[8,32,384]{2,1,0:T(8,128)(2,1)} %bitcast.25), channel_id=1, source_target_pairs={{0,12},{4,8},{8,4},{12,0},{16,28},{20,24},{24,20},{28,16},{1,13},{... | collective-permute-start | bytes 589832 | tf_op jit(solution)/shard_map/ppermute | solution.py:333
  52.0 2.7 %collective-permute-start.1 = (bf16[8,96,256]{2,1,0:T(8,128)(2,1)S(1)}, bf16[8,96,256]{2,1,0:T(8,128)(2,1)}, u32[]{:S(2)}, u32[]{:S(2)}) collective-permute-start(bf16[8,96,256]{2,1,0:T(8,128)(2,1)S(1)} %copy-done.12), channel_id=1, source_target_pairs={{0,2},{1,3},{2,0},{3,1},{4,6},{5,7},{6,4},{7,5},{8,10},{9,11},{10,... | collective-permute-start | bytes 1179656 | tf_op jit(solution)/shard_map/ppermute | solution.py:333
  54.7 6.8 %collective-permute-done.9.refs_3_ = bf16[8,32,384]{2,1,0:T(8,128)(2,1)S(1)} collective-permute-done((bf16[8,32,384]{2,1,0:T(8,128)(2,1)}, bf16[8,32,384]{2,1,0:T(8,128)(2,1)S(1)}, u32[]{:S(2)}, u32[]{:S(2)}) %collective-permute-start.9) | collective-permute-done | bytes 196640 | tf_op jit(solution)/shard_map/ppermute | solution.py:333
  61.6 1.8 %collective-permute-start.2 = (bf16[8,96,256]{2,1,0:T(8,128)(2,1)S(1)}, bf16[8,96,256]{2,1,0:T(8,128)(2,1)}, u32[]{:S(2)}, u32[]{:S(2)}) collective-permute-start(bf16[8,96,256]{2,1,0:T(8,128)(2,1)S(1)} %copy-done.11), channel_id=1, source_target_pairs={{0,3},{1,2},{2,1},{3,0},{4,7},{5,6},{6,5},{7,4},{8,11},{9,10},{10,... | collective-permute-start | bytes 1179656 | tf_op jit(solution)/shard_map/ppermute | solution.py:333
  63.4 0.7 collective-permute-start.6
  64.2 0.8 copy.15.refs_10_
  65.0 6.4 %collective-permute-done.6.refs_8_.refs_4_ = bf16[8,32,384]{2,1,0:T(8,128)(2,1)} collective-permute-done((bf16[8,32,384]{2,1,0:T(8,128)(2,1)}, bf16[8,32,384]{2,1,0:T(8,128)(2,1)}, u32[]{:S(2)}, u32[]{:S(2)}) %collective-permute-start.6) | collective-permute-done | bytes 196640 | tf_op jit(solution)/shard_map/ppermute | solution.py:333
  71.4 3.1 %collective-permute-start.12 = (bf16[8,32,384]{2,1,0:T(8,128)(2,1)}, bf16[8,32,384]{2,1,0:T(8,128)(2,1)S(1)}, u32[]{:S(2)}, u32[]{:S(2)}) collective-permute-start(bf16[8,32,384]{2,1,0:T(8,128)(2,1)} %collective-permute-done.6.refs_8_.refs_4_), channel_id=1, source_target_pairs={{0,12},{4,8},{8,4},{12,0},{16,28},{20,24},{24,20},{28,16},{1,13},{... | collective-permute-start | bytes 589832 | tf_op jit(solution)/shard_map/ppermute | solution.py:333
  74.5 1.5 collective-permute-start.11
  76.1 13.5 %shard_map.86 = (bf16[768,256]{1,0:T(8,128)(2,1)}, bf16[768,256]{1,0:T(8,128)(2,1)}, bf16[8,384,256]{2,1,0:T(8,128)(2,1)}, bf16[8,256,384]{2,1,0:T(8,128)(2,1)}) custom-call(bf16[8,96,256]{2,1,0:T(8,128)(2,1)} %get-tuple-element.18.refs_0_, bf16[8,96,256]{2,1,0:T(8,128)(2,1)} %copy-done.10, bf16[8,96,256]{2,1,0:T(8,128)(2,1)} %collective-permute-done.1.refs_2_, ...), custom_call_target="tpu_custom_call" | custom-call | flops 4328521728 | bytes 3145728 | tf_op jit(solution)/shard_map/pallas_call | solution.py:219
  89.7 0.6 copy-done.17
  90.6 7.0 %shard_map.87.refs_11_ = bf16[8,2,128,128]{3,2,1,0:T(8,128)(2,1)} custom-call(bf16[8,32,384]{2,1,0:T(8,128)(2,1)} %bitcast.29, bf16[8,32,384]{2,1,0:T(8,128)(2,1)} %copy-done.17, bf16[8,32,384]{2,1,0:T(8,128)(2,1)} %copy-done.16, bf16[8,32,384]{2,1,0:T(8,128)(2,1)} %copy-done.15, bf16[8,32,384]{2,1,0:T(8,128)(2,1)} %collective-permute-done.6.refs_8_.refs_4_, ...), custom_call_target="tpu_custom_call" | custom-call | flops 2147483648 | bytes 3538944 | tf_op jit(solution)/shard_map/pallas_call | solution.py:267
  97.6 5.3 %all-to-all-start.1 = ((bf16[8,2,128,128]{3,2,1,0:T(8,128)(2,1)}), bf16[8,2,128,128]{3,2,1,0:T(8,128)(2,1)S(1)}, u32[]{:S(2)}, u32[]{:S(2)}) async-start(bf16[8,2,128,128]{3,2,1,0:T(8,128)(2,1)} %shard_map.87.refs_11_), calls=%async_computation.1 | async-start | bytes 1048576 | tf_op jit(solution)/shard_map/all_to_all | solution.py:357
  102.9 12.3 %shard_map.88.refs_7_ = bf16[8,6,128,128]{3,2,1,0:T(8,128)(2,1)} custom-call(bf16[8,32,384]{2,1,0:T(8,128)(2,1)} %bitcast.30, bf16[8,32,384]{2,1,0:T(8,128)(2,1)} %copy-done.17, bf16[8,32,384]{2,1,0:T(8,128)(2,1)} %copy-done.16, bf16[8,32,384]{2,1,0:T(8,128)(2,1)} %copy-done.15, bf16[8,32,384]{2,1,0:T(8,128)(2,1)} %collective-permute-done.6.refs_8_.refs_4_, ...), custom_call_target="tpu_custom_call" | custom-call | flops 6442450944 | bytes 3538944 | tf_op jit(solution)/shard_map/pallas_call | solution.py:267
  115.2 0.8 copy-done.1
  116.0 5.7 %all-to-all-start.2 = ((bf16[8,6,128,128]{3,2,1,0:T(8,128)(2,1)}), bf16[8,6,128,128]{3,2,1,0:T(8,128)(2,1)S(1)}, u32[]{:S(2)}, u32[]{:S(2)}) async-start(bf16[8,6,128,128]{3,2,1,0:T(8,128)(2,1)} %shard_map.88.refs_7_), calls=%async_computation.2 | async-start | bytes 3145728 | tf_op jit(solution)/shard_map/all_to_all | solution.py:359
  121.7 1.7 %collective-permute-start.15 = (bf16[768,256]{1,0:T(8,128)(2,1)S(1)}, bf16[768,256]{1,0:T(8,128)(2,1)S(1)}, u32[]{:S(2)}, u32[]{:S(2)}) collective-permute-start(bf16[768,256]{1,0:T(8,128)(2,1)S(1)} %copy-done.13), channel_id=1, source_target_pairs={{0,2},{1,3},{2,0},{3,1},{4,6},{5,7},{6,4},{7,5},{8,10},{9,11},{10,... | collective-permute-start | bytes 1179656 | tf_op jit(solution)/shard_map/ppermute | solution.py:333
  123.3 2.1 %shard_map.89.refs_8_.refs_1_ = bf16[8,4,8,32,128]{4,3,2,1,0:T(8,128)(2,1)} custom-call(bf16[8,2,4,32,128]{4,3,2,1,0:T(8,128)(2,1)} %bitcast.17), custom_call_target="tpu_custom_call" | custom-call | flops 300000000 | bytes 4000000 | tf_op jit(solution)/shard_map/pallas_call | solution.py:295
  125.5 12.2 %shard_map.90 = (bf16[768,256]{1,0:T(8,128)(2,1)}, bf16[768,256]{1,0:T(8,128)(2,1)}) custom-call(bf16[8,96,256]{2,1,0:T(8,128)(2,1)} %get-tuple-element.18.refs_0_, bf16[8,96,256]{2,1,0:T(8,128)(2,1)} %copy-done.10, bf16[8,384,256]{2,1,0:T(8,128)(2,1)} %get-tuple-element.26.refs_2_, bf16[8,256,384]{2,1,0:T(8,128)(2,1)} %get-tuple-element.27.refs_3_, ...), custom_call_target="tpu_custom_call" | custom-call | flops 4328521728 | bytes 3145728 | tf_op jit(solution)/shard_map/pallas_call | solution.py:219
  137.7 2.1 %collective-permute-start.14 = (bf16[768,256]{1,0:T(8,128)(2,1)}, bf16[768,256]{1,0:T(8,128)(2,1)S(1)}, u32[]{:S(2)}, u32[]{:S(2)}) collective-permute-start(bf16[768,256]{1,0:T(8,128)(2,1)} %get-tuple-element.32), channel_id=1, source_target_pairs={{0,1},{1,0},{2,3},{3,2},{4,5},{5,4},{6,7},{7,6},{8,9},{9,8},{10,11... | collective-permute-start | bytes 1179656 | tf_op jit(solution)/shard_map/ppermute | solution.py:333
  139.8 1.5 %collective-permute-done.14 = bf16[768,256]{1,0:T(8,128)(2,1)S(1)} collective-permute-done((bf16[768,256]{1,0:T(8,128)(2,1)}, bf16[768,256]{1,0:T(8,128)(2,1)S(1)}, u32[]{:S(2)}, u32[]{:S(2)}) %collective-permute-start.14) | collective-permute-done | bytes 393248 | tf_op jit(solution)/shard_map/ppermute | solution.py:333
  141.3 0.7 copy-done.5
  142.0 2.8 %shard_map.91 = bf16[96,4,8,256]{3,2,1,0:T(8,128)(2,1)} custom-call(bf16[96,8,256]{2,1,0:T(8,128)(2,1)} %bitcast.22, bf16[96,8,256]{2,1,0:T(8,128)(2,1)} %bitcast.23, bf16[96,8,256]{2,1,0:T(8,128)(2,1)} %bitcast.20, bf16[96,8,256]{2,1,0:T(8,128)(2,1)} %bitcast.21), custom_call_target="tpu_custom_call" | custom-call | flops 300000000 | bytes 4000000 | tf_op jit(solution)/shard_map/pallas_call | solution.py:295
  144.8 1.2 copy-done
  146.0 2.8 %shard_map.92 = bf16[8,4,8,32,128]{4,3,2,1,0:T(8,128)(2,1)} custom-call(bf16[8,6,4,32,128]{4,3,2,1,0:T(8,128)(2,1)} %bitcast.16, bf16[8,4,8,32,128]{4,3,2,1,0:T(8,128)(2,1)} %shard_map.89.refs_8_.refs_1_), custom_call_target="tpu_custom_call", output_to_operand_aliasing={{}: (1, {})} | custom-call | flops 300000000 | bytes 4000000 | tf_op jit(solution)/shard_map/pallas_call | solution.py:295
  (66 shorter events, 1.8 us)
Async XLA Ops:
  8.7 30.1 %copy-start.23 = (bf16[96,256]{1,0:T(8,128)(2,1)S(1)}, bf16[96,256]{1,0:T(8,128)(2,1)}, u32[]{:S(2)}) copy-start(bf16[96,256]{1,0:T(8,128)(2,1)} %get-tuple-element.23) | copy-start | bytes 147460
  8.7 30.6 %copy-start.22 = (bf16[96,256]{1,0:T(8,128)(2,1)S(1)}, bf16[96,256]{1,0:T(8,128)(2,1)}, u32[]{:S(2)}) copy-start(bf16[96,256]{1,0:T(8,128)(2,1)} %get-tuple-element.24) | copy-start | bytes 147460
  8.7 31.4 %copy-start.21 = (bf16[96,256]{1,0:T(8,128)(2,1)S(1)}, bf16[96,256]{1,0:T(8,128)(2,1)}, u32[]{:S(2)}) copy-start(bf16[96,256]{1,0:T(8,128)(2,1)} %get-tuple-element.25) | copy-start | bytes 147460
  8.7 43.3 %copy-start.12 = (bf16[8,96,256]{2,1,0:T(8,128)(2,1)S(1)}, bf16[8,96,256]{2,1,0:T(8,128)(2,1)}, u32[]{:S(2)}) copy-start(bf16[8,96,256]{2,1,0:T(8,128)(2,1)} %get-tuple-element.20) | copy-start | bytes 1179652
  8.7 52.9 %copy-start.11 = (bf16[8,96,256]{2,1,0:T(8,128)(2,1)S(1)}, bf16[8,96,256]{2,1,0:T(8,128)(2,1)}, u32[]{:S(2)}) copy-start(bf16[8,96,256]{2,1,0:T(8,128)(2,1)} %get-tuple-element.21) | copy-start | bytes 1179652
  8.7 55.3 %copy-start.6 = (bf16[1024,128]{1,0:T(8,128)(2,1)S(1)}, bf16[1024,128]{1,0:T(8,128)(2,1)}, u32[]{:S(2)}) copy-start(bf16[1024,128]{1,0:T(8,128)(2,1)} %param.13) | copy-start | bytes 786436
  38.7 50.9 %copy-start.2 = (bf16[8,96,1024]{2,1,0:T(8,128)(2,1)}, bf16[8,96,1024]{2,1,0:T(8,128)(2,1)S(1)}, u32[]{:S(2)}) copy-start(bf16[8,96,1024]{2,1,0:T(8,128)(2,1)S(1)} %all_to_all.15.refs_8_) | copy-start | bytes 4718596
  38.7 51.0 %collective-permute-start.13 = (bf16[8,96,1024]{2,1,0:T(8,128)(2,1)S(1)}, bf16[8,96,1024]{2,1,0:T(8,128)(2,1)}, u32[]{:S(2)}, u32[]{:S(2)}) collective-permute-start(bf16[8,96,1024]{2,1,0:T(8,128)(2,1)S(1)} %all_to_all.15.refs_8_), channel_id=1, source_target_pairs={{0,1},{1,0},{2,3},{3,2},{4,5},{5,4},{6,7},{7,6},{8,9},{9,8},{10,11... | collective-permute-start | bytes 4718600 | tf_op jit(solution)/shard_map/ppermute | solution.py:333
  38.7 3.5 %collective-permute-start.3 = (bf16[96,256]{1,0:T(8,128)(2,1)S(1)}, bf16[96,256]{1,0:T(8,128)(2,1)S(1)}, u32[]{:S(2)}, u32[]{:S(2)}) collective-permute-start(bf16[96,256]{1,0:T(8,128)(2,1)S(1)} %copy-done.23), channel_id=1, source_target_pairs={{0,1},{1,0},{2,3},{3,2},{4,5},{5,4},{6,7},{7,6},{8,9},{9,8},{10,11... | collective-permute-start | bytes 147464 | tf_op jit(solution)/shard_map/ppermute | solution.py:333
  39.2 5.8 %collective-permute-start.4 = (bf16[96,256]{1,0:T(8,128)(2,1)S(1)}, bf16[96,256]{1,0:T(8,128)(2,1)S(1)}, u32[]{:S(2)}, u32[]{:S(2)}) collective-permute-start(bf16[96,256]{1,0:T(8,128)(2,1)S(1)} %copy-done.22), channel_id=1, source_target_pairs={{0,2},{1,3},{2,0},{3,1},{4,6},{5,7},{6,4},{7,5},{8,10},{9,11},{10,... | collective-permute-start | bytes 147464 | tf_op jit(solution)/shard_map/ppermute | solution.py:333
  40.1 5.5 %collective-permute-start.5 = (bf16[96,256]{1,0:T(8,128)(2,1)S(1)}, bf16[96,256]{1,0:T(8,128)(2,1)S(1)}, u32[]{:S(2)}, u32[]{:S(2)}) collective-permute-start(bf16[96,256]{1,0:T(8,128)(2,1)S(1)} %copy-done.21), channel_id=1, source_target_pairs={{0,3},{1,2},{2,1},{3,0},{4,7},{5,6},{6,5},{7,4},{8,11},{9,10},{10,... | collective-permute-start | bytes 147464 | tf_op jit(solution)/shard_map/ppermute | solution.py:333
  42.3 3.4 %copy-start.7 = (bf16[96,256]{1,0:T(8,128)(2,1)}, bf16[96,256]{1,0:T(8,128)(2,1)S(1)}, u32[]{:S(2)}) copy-start(bf16[96,256]{1,0:T(8,128)(2,1)S(1)} %collective-permute-done.3.p1) | copy-start | bytes 147460
  47.9 13.6 %collective-permute-start.9 = (bf16[8,32,384]{2,1,0:T(8,128)(2,1)}, bf16[8,32,384]{2,1,0:T(8,128)(2,1)S(1)}, u32[]{:S(2)}, u32[]{:S(2)}) collective-permute-start(bf16[8,32,384]{2,1,0:T(8,128)(2,1)} %bitcast.25), channel_id=1, source_target_pairs={{0,12},{4,8},{8,4},{12,0},{16,28},{20,24},{24,20},{28,16},{1,13},{... | collective-permute-start | bytes 589832 | tf_op jit(solution)/shard_map/ppermute | solution.py:333
  52.0 11.4 %collective-permute-start.8 = (bf16[8,32,384]{2,1,0:T(8,128)(2,1)}, bf16[8,32,384]{2,1,0:T(8,128)(2,1)S(1)}, u32[]{:S(2)}, u32[]{:S(2)}) collective-permute-start(bf16[8,32,384]{2,1,0:T(8,128)(2,1)} %bitcast.26), channel_id=1, source_target_pairs={{0,8},{4,12},{8,0},{12,4},{16,24},{20,28},{24,16},{28,20},{1,9},{5... | collective-permute-start | bytes 589832 | tf_op jit(solution)/shard_map/ppermute | solution.py:333
  52.0 19.5 %collective-permute-start = (bf16[8,96,256]{2,1,0:T(8,128)(2,1)}, bf16[8,96,256]{2,1,0:T(8,128)(2,1)S(1)}, u32[]{:S(2)}, u32[]{:S(2)}) collective-permute-start(bf16[8,96,256]{2,1,0:T(8,128)(2,1)} %get-tuple-element.19), channel_id=1, source_target_pairs={{0,1},{1,0},{2,3},{3,2},{4,5},{5,4},{6,7},{7,6},{8,9},{9,8},{10,11... | collective-permute-start | bytes 1179656 | tf_op jit(solution)/shard_map/ppermute | solution.py:333
  52.0 22.5 %collective-permute-start.1 = (bf16[8,96,256]{2,1,0:T(8,128)(2,1)S(1)}, bf16[8,96,256]{2,1,0:T(8,128)(2,1)}, u32[]{:S(2)}, u32[]{:S(2)}) collective-permute-start(bf16[8,96,256]{2,1,0:T(8,128)(2,1)S(1)} %copy-done.12), channel_id=1, source_target_pairs={{0,2},{1,3},{2,0},{3,1},{4,6},{5,7},{6,4},{7,5},{8,10},{9,11},{10,... | collective-permute-start | bytes 1179656 | tf_op jit(solution)/shard_map/ppermute | solution.py:333
  61.6 28.0 %copy-start.15 = (bf16[8,32,384]{2,1,0:T(8,128)(2,1)}, bf16[8,32,384]{2,1,0:T(8,128)(2,1)S(1)}, u32[]{:S(2)}) copy-start(bf16[8,32,384]{2,1,0:T(8,128)(2,1)S(1)} %collective-permute-done.9.refs_3_) | copy-start | bytes 589828
  61.6 14.4 %collective-permute-start.2 = (bf16[8,96,256]{2,1,0:T(8,128)(2,1)S(1)}, bf16[8,96,256]{2,1,0:T(8,128)(2,1)}, u32[]{:S(2)}, u32[]{:S(2)}) collective-permute-start(bf16[8,96,256]{2,1,0:T(8,128)(2,1)S(1)} %copy-done.11), channel_id=1, source_target_pairs={{0,3},{1,2},{2,1},{3,0},{4,7},{5,6},{6,5},{7,4},{8,11},{9,10},{10,... | collective-permute-start | bytes 1179656 | tf_op jit(solution)/shard_map/ppermute | solution.py:333
  63.4 8.1 %collective-permute-start.6 = (bf16[8,32,384]{2,1,0:T(8,128)(2,1)}, bf16[8,32,384]{2,1,0:T(8,128)(2,1)}, u32[]{:S(2)}, u32[]{:S(2)}) collective-permute-start(bf16[8,32,384]{2,1,0:T(8,128)(2,1)} %bitcast.27), channel_id=1, source_target_pairs={{0,16},{4,20},{8,24},{12,28},{16,0},{20,4},{24,8},{28,12},{1,17},{... | collective-permute-start | bytes 589832 | tf_op jit(solution)/shard_map/ppermute | solution.py:333
  71.4 18.2 %collective-permute-start.7 = (bf16[8,32,384]{2,1,0:T(8,128)(2,1)}, bf16[8,32,384]{2,1,0:T(8,128)(2,1)S(1)}, u32[]{:S(2)}, u32[]{:S(2)}) collective-permute-start(bf16[8,32,384]{2,1,0:T(8,128)(2,1)} %bitcast.28), channel_id=1, source_target_pairs={{0,4},{4,0},{8,12},{12,8},{16,20},{20,16},{24,28},{28,24},{1,5},{5... | collective-permute-start | bytes 589832 | tf_op jit(solution)/shard_map/ppermute | solution.py:333
  71.4 4.7 %copy-start.10 = (bf16[8,96,256]{2,1,0:T(8,128)(2,1)}, bf16[8,96,256]{2,1,0:T(8,128)(2,1)S(1)}, u32[]{:S(2)}) copy-start(bf16[8,96,256]{2,1,0:T(8,128)(2,1)S(1)} %collective-permute-done.refs_1_) | copy-start | bytes 1179652
  71.4 18.2 %collective-permute-start.12 = (bf16[8,32,384]{2,1,0:T(8,128)(2,1)}, bf16[8,32,384]{2,1,0:T(8,128)(2,1)S(1)}, u32[]{:S(2)}, u32[]{:S(2)}) collective-permute-start(bf16[8,32,384]{2,1,0:T(8,128)(2,1)} %collective-permute-done.6.refs_8_.refs_4_), channel_id=1, source_target_pairs={{0,12},{4,8},{8,4},{12,0},{16,28},{20,24},{24,20},{28,16},{1,13},{... | collective-permute-start | bytes 589832 | tf_op jit(solution)/shard_map/ppermute | solution.py:333
  74.5 15.2 %collective-permute-start.11 = (bf16[8,32,384]{2,1,0:T(8,128)(2,1)}, bf16[8,32,384]{2,1,0:T(8,128)(2,1)S(1)}, u32[]{:S(2)}, u32[]{:S(2)}) collective-permute-start(bf16[8,32,384]{2,1,0:T(8,128)(2,1)} %collective-permute-done.6.refs_8_.refs_4_), channel_id=1, source_target_pairs={{0,8},{4,12},{8,0},{12,4},{16,24},{20,28},{24,16},{28,20},{1,9},{5... | collective-permute-start | bytes 589832 | tf_op jit(solution)/shard_map/ppermute | solution.py:333
  76.0 13.7 %collective-permute-start.10 = (bf16[8,32,384]{2,1,0:T(8,128)(2,1)}, bf16[8,32,384]{2,1,0:T(8,128)(2,1)S(1)}, u32[]{:S(2)}, u32[]{:S(2)}) collective-permute-start(bf16[8,32,384]{2,1,0:T(8,128)(2,1)} %collective-permute-done.6.refs_8_.refs_4_), channel_id=1, source_target_pairs={{0,4},{4,0},{8,12},{12,8},{16,20},{20,16},{24,28},{28,24},{1,5},{5... | collective-permute-start | bytes 589832 | tf_op jit(solution)/shard_map/ppermute | solution.py:333
  97.6 17.6 %all-to-all-start.1 = ((bf16[8,2,128,128]{3,2,1,0:T(8,128)(2,1)}), bf16[8,2,128,128]{3,2,1,0:T(8,128)(2,1)S(1)}, u32[]{:S(2)}, u32[]{:S(2)}) async-start(bf16[8,2,128,128]{3,2,1,0:T(8,128)(2,1)} %shard_map.87.refs_11_), calls=%async_computation.1 | async-start | bytes 1048576 | tf_op jit(solution)/shard_map/all_to_all | solution.py:357
  115.2 6.5 %copy-start.13 = (bf16[768,256]{1,0:T(8,128)(2,1)S(1)}, bf16[768,256]{1,0:T(8,128)(2,1)}, u32[]{:S(2)}) copy-start(bf16[768,256]{1,0:T(8,128)(2,1)} %get-tuple-element.30.refs_11_) | copy-start | bytes 1179652
  115.2 8.2 %copy-start.14 = (bf16[768,256]{1,0:T(8,128)(2,1)S(1)}, bf16[768,256]{1,0:T(8,128)(2,1)}, u32[]{:S(2)}) copy-start(bf16[768,256]{1,0:T(8,128)(2,1)} %get-tuple-element.33) | copy-start | bytes 1179652
  116.0 28.8 %all-to-all-start.2 = ((bf16[8,6,128,128]{3,2,1,0:T(8,128)(2,1)}), bf16[8,6,128,128]{3,2,1,0:T(8,128)(2,1)S(1)}, u32[]{:S(2)}, u32[]{:S(2)}) async-start(bf16[8,6,128,128]{3,2,1,0:T(8,128)(2,1)} %shard_map.88.refs_7_), calls=%async_computation.2 | async-start | bytes 3145728 | tf_op jit(solution)/shard_map/all_to_all | solution.py:359
  121.7 18.1 %collective-permute-start.15 = (bf16[768,256]{1,0:T(8,128)(2,1)S(1)}, bf16[768,256]{1,0:T(8,128)(2,1)S(1)}, u32[]{:S(2)}, u32[]{:S(2)}) collective-permute-start(bf16[768,256]{1,0:T(8,128)(2,1)S(1)} %copy-done.13), channel_id=1, source_target_pairs={{0,2},{1,3},{2,0},{3,1},{4,6},{5,7},{6,4},{7,5},{8,10},{9,11},{10,... | collective-permute-start | bytes 1179656 | tf_op jit(solution)/shard_map/ppermute | solution.py:333
  123.3 16.4 %collective-permute-start.16 = (bf16[768,256]{1,0:T(8,128)(2,1)S(1)}, bf16[768,256]{1,0:T(8,128)(2,1)S(1)}, u32[]{:S(2)}, u32[]{:S(2)}) collective-permute-start(bf16[768,256]{1,0:T(8,128)(2,1)S(1)} %copy-done.14), channel_id=1, source_target_pairs={{0,3},{1,2},{2,1},{3,0},{4,7},{5,6},{6,5},{7,4},{8,11},{9,10},{10,... | collective-permute-start | bytes 1179656 | tf_op jit(solution)/shard_map/ppermute | solution.py:333
  137.7 3.6 %collective-permute-start.14 = (bf16[768,256]{1,0:T(8,128)(2,1)}, bf16[768,256]{1,0:T(8,128)(2,1)S(1)}, u32[]{:S(2)}, u32[]{:S(2)}) collective-permute-start(bf16[768,256]{1,0:T(8,128)(2,1)} %get-tuple-element.32), channel_id=1, source_target_pairs={{0,1},{1,0},{2,3},{3,2},{4,5},{5,4},{6,7},{7,6},{8,9},{9,8},{10,11... | collective-permute-start | bytes 1179656 | tf_op jit(solution)/shard_map/ppermute | solution.py:333
  139.7 1.6 %copy-start.4 = (bf16[768,256]{1,0:T(8,128)(2,1)}, bf16[768,256]{1,0:T(8,128)(2,1)S(1)}, u32[]{:S(2)}) copy-start(bf16[768,256]{1,0:T(8,128)(2,1)S(1)} %collective-permute-done.16) | copy-start | bytes 1179652
  (11 other events, 9.3 us)

commit v4 on v3

--- a/solution.py
+++ b/solution.py
@@ -16,7 +16,8 @@
 ROWS = ("yl", "z")
 XY = ("xl", "yh", "xh")
 SPLIT = 2
-AT_ONCE = 2
+PAD = 40
+AT_ONCE = 4
 NT = (((1,), (1,)), ((), ()))
 NN = (((1,), (0,)), ((), ()))
 TN = (((0,), (0,)), ((), ()))
@@ -44,21 +45,24 @@
         v = v - jnp.mean(v, axis=-1, keepdims=True)
         spread = jnp.mean(v * v, axis=-1, keepdims=True)
         y = v * lax.rsqrt(spread + EPS)
-        nf[0, at, :] = y[:, :128]
-        nf[1, at, :] = y[:, 128:]
+        for j in range(step // 32):
+            to = pl.ds(pl.multiple_of((n * (step // 32) + j) * PAD, 8), 32)
+            nf[0, to, :] = y[j * 32:(j + 1) * 32, :128]
+            nf[1, to, :] = y[j * 32:(j + 1) * 32, 128:]
         return 0
 
     lax.fori_loop(0, rows // step, one, 0)
     for r in range(32):
-        at = pl.ds(r, seqs, stride=32)
+        at = pl.ds(r, seqs, stride=PAD)
         x = jnp.concatenate([nf[0, at, :], nf[1, at, :]], axis=1).astype(BF16)
         nb[r] = x
         f = dot(wf_ref[...], x, NT)
         lf[r * 32:(r + 1) * 32, :seqs] = f[:32]
-        rf[pl.ds(r, 32, stride=32), :] = jnp.concatenate([f[32:], jnp.zeros((32, 128 - seqs), F32)], axis=1)
+        rf[pl.ds(r, 32, stride=PAD), :] = jnp.concatenate([f[32:], jnp.zeros((32, 128 - seqs), F32)], axis=1)
     for g in range(8):
         sl = slice(g * 128, (g + 1) * 128)
-        piece = rf[sl, :].T[:seqs].astype(BF16)
+        piece = jnp.concatenate([rf[e * PAD:e * PAD + 32, :] for e in range(4 * g, 4 * g + 4)], axis=0)
+        piece = piece.T[:seqs].astype(BF16)
         for k in range(8):
             r_ref[k, :, sl] = piece
         lb[g // 2, :, (g % 2) * 128:(g % 2 + 1) * 128] = lf[sl, :].T[:seqs].astype(BF16)
@@ -80,10 +84,10 @@
         + [jax.ShapeDtypeStruct((seqs, 256), BF16)] * 4
         + [jax.ShapeDtypeStruct((8, seqs, 1024), BF16)],
         scratch_shapes=[
-            pltpu.VMEM((2, rows, 128), F32),
+            pltpu.VMEM((2, seqs * PAD, 128), F32),
             pltpu.VMEM((32, seqs, 256), BF16),
             pltpu.VMEM((1024, 128), F32),
-            pltpu.VMEM((1024, 128), F32),
+            pltpu.VMEM((32 * PAD, 128), F32),
             pltpu.VMEM((4, seqs, 256), BF16),
         ],
         cost_estimate=pl.CostEstimate(flops=800_000_000, transcendentals=rows, bytes_accessed=4 * rows * 256),
@@ -110,19 +114,22 @@
     return out.reshape(8, 32, seqs)
 
 
-def attend(mine, keys, v_t, wq, wg, wo):
-    seqs = mine.shape[0]
-    q_t = dot(wq, mine, TT)
-    q_t = jnp.concatenate([q_t, q_t], axis=1)
-    first = lax.broadcasted_iota(jnp.int32, q_t.shape, 1) < seqs
-    q_even = jnp.where(first, q_t, 0.0).astype(BF16)
-    q_odd = jnp.where(first, 0.0, q_t).astype(BF16)
-    g_t = jax.nn.sigmoid(dot(wg, mine, TT))
-    ones = jnp.ones((16, keys.shape[0]), BF16)
+def attend(items, wq, wg, wo):
+    seqs = items[0][0].shape[0]
+    ones = jnp.ones((16, items[0][1].shape[0]), BF16)
     scale = math.log2(math.e) / math.sqrt(HC)
-    gated = []
-
-    def spread(h):
+    quads = HEADS // 4
+    ready = []
+    for mine, keys, v_t in items:
+        q_t = dot(wq, mine, TT)
+        q_t = jnp.concatenate([q_t, q_t], axis=1)
+        first = lax.broadcasted_iota(jnp.int32, q_t.shape, 1) < seqs
+        q_even = jnp.where(first, q_t, 0.0).astype(BF16)
+        q_odd = jnp.where(first, 0.0, q_t).astype(BF16)
+        ready.append((q_even, q_odd, jax.nn.sigmoid(dot(wg, mine, TT))))
+
+    def spread(n, h):
+        q_even, q_odd, _ = ready[n]
         parts = [q_even[h * HC:(h + 1) * HC], q_odd[(h + 1) * HC:(h + 2) * HC]]
         if h:
             parts.insert(0, jnp.zeros((h * HC, 2 * seqs), BF16))
@@ -130,10 +137,20 @@
             parts.append(jnp.zeros(((HEADS - 2 - h) * HC, 2 * seqs), BF16))
         return jnp.concatenate(parts, axis=0)
 
-    for p in range(HEADS // 4):
-        rhs = jnp.concatenate([spread(4 * p), spread(4 * p + 2)], axis=1)
-        scores = dot(keys, rhs, NN)
+    def scores_of(n, p):
+        rhs = jnp.concatenate([spread(n, 4 * p), spread(n, 4 * p + 2)], axis=1)
+        return dot(items[n][1], rhs, NN)
+
+    order = [(n, p) for n in range(len(items)) for p in range(quads)]
+    gated = [[] for _ in items]
+    updates = []
+    ahead = scores_of(*order[0])
+    for at, (n, p) in enumerate(order):
+        scores = ahead
+        if at + 1 < len(order):
+            ahead = scores_of(*order[at + 1])
         weights = jnp.exp2(scores * scale).astype(BF16)
+        v_t, g_t = items[n][2], ready[n][2]
         tiles = []
         for u in range(3):
             h = 4 * p + u
@@ -149,9 +166,10 @@
         )
         for u, att in enumerate(heads):
             h = 4 * p + u
-            gated.append((g_t[h * HC:(h + 1) * HC] * att).astype(BF16))
-    gated = jnp.concatenate(gated, axis=0)
-    return dot(gated, wo, TN)
+            gated[n].append((g_t[h * HC:(h + 1) * HC] * att).astype(BF16))
+        if p == quads - 1:
+            updates.append(dot(jnp.concatenate(gated[n], axis=0), wo, TN))
+    return updates
 
 
 def finish(g, of, part, o_refs):
@@ -168,13 +186,15 @@
     oa, ob, k_ref, v_ref, of = refs[8 + n_wait:]
     g = pl.program_id(0)
     at_once, part = x_refs[0].shape[:2]
+    items = []
     for n in range(at_once):
         x = jnp.concatenate([b[n] for b in x_refs], axis=0)
         keys = dot(x, wkv_ref[:, :256], NN).astype(BF16)
         v_t = dot(wkv_ref[:, 256:], x, TT).astype(BF16)
         k_ref[n] = keys
         v_ref[n] = v_t
-        update = attend(x[2 * part:], keys, v_t, wq_ref[...], wg_ref[...], wo_ref[...])
+        items.append((x[2 * part:], keys, v_t))
+    for n, update in enumerate(attend(items, wq_ref[...], wg_ref[...], wo_ref[...])):
         rows = pl.ds(g * at_once + n, 2 * part, stride=8)
         of[0, rows, :] = update[:, :128]
         of[1, rows, :] = update[:, 128:]
@@ -186,9 +206,10 @@
     oa, ob, of = refs[7 + n_wait:]
     g = pl.program_id(0)
     at_once, part = x_refs[0].shape[:2]
-    for n in range(at_once):
-        mine = jnp.concatenate([b[n] for b in x_refs], axis=0)
-        update = attend(mine, k_ref[n], v_ref[n], wq_ref[...], wg_ref[...], wo_ref[...])
+    items = [
+        (jnp.concatenate([b[n] for b in x_refs], axis=0), k_ref[n], v_ref[n]) for n in range(at_once)
+    ]
+    for n, update in enumerate(attend(items, wq_ref[...], wg_ref[...], wo_ref[...])):
         rows = pl.ds(g * at_once + n, 2 * part, stride=8)
         of[0, rows, :] = update[:, :128]
         of[1, rows, :] = update[:, 128:]
@@ -315,17 +336,40 @@
 
 def place_pair(got, prior, r0):
     count = got.shape[1]
-
-    def where(g, out):
-        pairs = []
-        for b in range(4):
-            v = lax.axis_index(("yh", "xl")) ^ b
-            a = (v % 2) * 2 + v // 2
-            for k in range(8):
-                pairs.append((g.at[k, :, b], out.at[pl.ds(r0, count), a, k]))
-        return pairs
-
-    return place([got.reshape(8, count, 4, 32, 128)], [where], (8, 4, 8, 32, 128), prior)
+    shape = (8, 4, 8, 32, 128)
+    more = [] if prior is None else [prior]
+
+    def kernel(g_hbm, *refs):
+        out, buf, in_sems, out_sems = refs[-4:]
+        loads = [pltpu.make_async_copy(g_hbm.at[k], buf.at[k], in_sems.at[k]) for k in range(8)]
+        for c in loads:
+            c.start()
+        stores = []
+        for k in range(8):
+            loads[k].wait()
+            for b in range(4):
+                v = lax.axis_index(("yh", "xl")) ^ b
+                a = (v % 2) * 2 + v // 2
+                to = out.at[pl.ds(r0, count), a, k]
+                stores.append(pltpu.make_async_copy(buf.at[k, :, b], to, out_sems.at[4 * k + b]))
+                stores[-1].start()
+        for c in stores:
+            c.wait()
+
+    hbm = pl.BlockSpec(memory_space=pltpu.HBM)
+    return pl.pallas_call(
+        kernel,
+        in_specs=[hbm] * (1 + len(more)),
+        out_specs=hbm,
+        out_shape=jax.ShapeDtypeStruct(shape, BF16),
+        scratch_shapes=[
+            pltpu.VMEM((8, count, 4, 32, 128), BF16),
+            pltpu.SemaphoreType.DMA((8,)),
+            pltpu.SemaphoreType.DMA((32,)),
+        ],
+        input_output_aliases={1: 0} if more else {},
+        cost_estimate=pl.CostEstimate(flops=300_000_000, transcendentals=0, bytes_accessed=4_000_000),
+    )(got.reshape(8, count, 4, 32, 128), *more)
 
 
 def swap(x, axes, k):

time: 151 us -> 146 us (0.967)
  Pallas kernels: 62.4 us -> 55.8 us
    pallas_call x3 -> x1, Pallas kernels: 7.66 us -> 2.77 us  [place(): pl.pallas_call(kernel, in_specs=[pl.BlockSpec(memory_space=pltpu.VMEM)] *...]
    pallas_call x2, Pallas kernels: 25.7 us -> 20.9 us  [attention(): pl.pallas_call(lambda *refs: kernel(len(waits), *refs), grid=(count // AT...]
    pallas_call x0 -> x2, Pallas kernels: none -> 4.52 us  [place_pair(): pl.pallas_call(kernel, in_specs=[hbm] * (1 + len(more)), out_specs=hbm, o...]
  transfers between devices with their start and end apart: 19 -> 19, of which waited for: 6 -> 6; matrix products, arithmetic and copies ran while one was open for 1% -> 1% of each run, Pallas kernels for 30% -> 28%
where the time goes in v4:
time: 146 us; the launch traced here: 143 us
  Pallas kernels  55.8 us (38%)
  starting transfers between devices  32.1 us (22%)
  blocking collectives  30 us (21%)
  waiting for transfers between devices  18.7 us (13%)
  local copies, waits for them, and re-layouts  5.47 us (4%)
    all_to_all x1, blocking collectives, layer(): near = lax.all_to_all(right, XY, 0, 0)  30 us
    ppermute x17, starting transfers between devices, swap(): return lax.ppermute(x, axes, [(j, j ^ k) for j in range(n)])  21.1 us
    pallas_call x2, Pallas kernels, attention(): pl.pallas_call(lambda *refs: kernel(len(waits), *refs), grid=(count // AT...  20.9 us
    pallas_call x2, Pallas kernels, pair_block(): pl.pallas_call(lambda *refs: pair_kernel(scaling, r0, count, *refs), in_s...  19.3 us
    ppermute x17, waiting for transfers between devices, swap(): return lax.ppermute(x, axes, [(j, j ^ k) for j in range(n)])  18.7 us
    pallas_call x1, Pallas kernels, front(): pl.pallas_call(front_kernel, in_specs=[vmem, vmem], out_shape=[jax.ShapeD...  6.67 us
    all_to_all x1, starting transfers between devices, layer(): got1 = lax.all_to_all(out1, ROWS, 0, 0)  5.7 us
    all_to_all x1, starting transfers between devices, layer(): got0 = lax.all_to_all(out0, ROWS, 0, 0)  5.27 us
  transfers between devices with their start and end apart: 19, of which 6 were waited for; matrix products, arithmetic and copies ran while one was open for 1% of the time, Pallas kernels for 28%

profile of v4, /device:TPU:0, one launch (start us, length us, event | category | flops | bytes accessed | tf_op | source)
XLA Modules:
  0.0 143.1 jit_solution(4027098457504089003)
XLA Ops:
  0.6 6.7 %front.1 = (bf16[8,96,256]{2,1,0:T(8,128)(2,1)}, bf16[8,96,256]{2,1,0:T(8,128)(2,1)}, bf16[8,96,256]{2,1,0:T(8,128)(2,1)}, bf16[8,96,256]{2,1,0:T(8,128)(2,1)}, ...) custom-call(bf16[3072,256]{1,0:T(8,128)(2,1)} %bitcast.31, ...), custom_call_target="tpu_custom_call" | custom-call | flops 800000000 | bytes 3145728 | tf_op jit(solution)/shard_map/front/pallas_call | solution.py:80
  7.3 30.0 %all_to_all.15.refs_8_ = bf16[8,96,1024]{2,1,0:T(8,128)(2,1)S(1)} all-to-all(bf16[8,96,1024]{2,1,0:T(8,128)(2,1)} %get-tuple-element.28), channel_id=1, replica_groups=mesh['xl'=2,'yh'=2,'yl'=2,'z'=4,'xh'=2,'c'=2] {'xl','yh','xh'}, dimensions={0} | all-to-all | bytes 3145728 | tf_op jit(solution)/shard_map/all_to_all | solution.py:386
  37.9 0.9 collective-permute-start.4
  38.7 2.1 %collective-permute-start.5 = (bf16[96,256]{1,0:T(8,128)(2,1)S(1)}, bf16[96,256]{1,0:T(8,128)(2,1)S(1)}, u32[]{:S(2)}, u32[]{:S(2)}) collective-permute-start(bf16[96,256]{1,0:T(8,128)(2,1)S(1)} %copy-done.21), channel_id=1, source_target_pairs={{0,3},{1,2},{2,1},{3,0},{4,7},{5,6},{6,5},{7,4},{8,11},{9,10},{10,... | collective-permute-start | bytes 147464 | tf_op jit(solution)/shard_map/ppermute | solution.py:377
  40.9 2.8 %collective-permute-done.4.p2 = bf16[96,256]{1,0:T(8,128)(2,1)S(1)} collective-permute-done((bf16[96,256]{1,0:T(8,128)(2,1)S(1)}, bf16[96,256]{1,0:T(8,128)(2,1)S(1)}, u32[]{:S(2)}, u32[]{:S(2)}) %collective-permute-start.4) | collective-permute-done | bytes 49184 | tf_op jit(solution)/shard_map/ppermute | solution.py:377
  43.7 0.6 collective-permute-done.5.p3
  44.9 1.7 %merge_left.1 = bf16[256,384]{1,0:T(8,128)(2,1)} custom-call(bf16[96,256]{1,0:T(8,128)(2,1)} %get-tuple-element.22.p0, bf16[96,256]{1,0:T(8,128)(2,1)} %copy-done.7, bf16[96,256]{1,0:T(8,128)(2,1)} %copy-done.8, bf16[96,256]{1,0:T(8,128)(2,1)} %copy-done.9), custom_call_target="tpu_custom_call" | custom-call | flops 100000000 | bytes 393216 | tf_op jit(solution)/shard_map/merge_left/pallas_call | solution.py:107
  46.6 4.0 %collective-permute-start.9 = (bf16[8,32,384]{2,1,0:T(8,128)(2,1)}, bf16[8,32,384]{2,1,0:T(8,128)(2,1)S(1)}, u32[]{:S(2)}, u32[]{:S(2)}) collective-permute-start(bf16[8,32,384]{2,1,0:T(8,128)(2,1)} %bitcast.25), channel_id=1, source_target_pairs={{0,12},{4,8},{8,4},{12,0},{16,28},{20,24},{24,20},{28,16},{1,13},{... | collective-permute-start | bytes 589832 | tf_op jit(solution)/shard_map/ppermute | solution.py:377
  50.6 2.7 %collective-permute-start.1 = (bf16[8,96,256]{2,1,0:T(8,128)(2,1)S(1)}, bf16[8,96,256]{2,1,0:T(8,128)(2,1)}, u32[]{:S(2)}, u32[]{:S(2)}) collective-permute-start(bf16[8,96,256]{2,1,0:T(8,128)(2,1)S(1)} %copy-done.12), channel_id=1, source_target_pairs={{0,2},{1,3},{2,0},{3,1},{4,6},{5,7},{6,4},{7,5},{8,10},{9,11},{10,... | collective-permute-start | bytes 1179656 | tf_op jit(solution)/shard_map/ppermute | solution.py:377
  53.3 6.8 %collective-permute-done.9.refs_3_ = bf16[8,32,384]{2,1,0:T(8,128)(2,1)S(1)} collective-permute-done((bf16[8,32,384]{2,1,0:T(8,128)(2,1)}, bf16[8,32,384]{2,1,0:T(8,128)(2,1)S(1)}, u32[]{:S(2)}, u32[]{:S(2)}) %collective-permute-start.9) | collective-permute-done | bytes 196640 | tf_op jit(solution)/shard_map/ppermute | solution.py:377
  60.2 1.8 %collective-permute-start.2 = (bf16[8,96,256]{2,1,0:T(8,128)(2,1)S(1)}, bf16[8,96,256]{2,1,0:T(8,128)(2,1)}, u32[]{:S(2)}, u32[]{:S(2)}) collective-permute-start(bf16[8,96,256]{2,1,0:T(8,128)(2,1)S(1)} %copy-done.11), channel_id=1, source_target_pairs={{0,3},{1,2},{2,1},{3,0},{4,7},{5,6},{6,5},{7,4},{8,11},{9,10},{10,... | collective-permute-start | bytes 1179656 | tf_op jit(solution)/shard_map/ppermute | solution.py:377
  62.0 0.7 collective-permute-start.6
  62.8 0.8 copy.15.refs_10_
  63.6 6.4 %collective-permute-done.6.refs_8_.refs_4_ = bf16[8,32,384]{2,1,0:T(8,128)(2,1)} collective-permute-done((bf16[8,32,384]{2,1,0:T(8,128)(2,1)}, bf16[8,32,384]{2,1,0:T(8,128)(2,1)}, u32[]{:S(2)}, u32[]{:S(2)}) %collective-permute-start.6) | collective-permute-done | bytes 196640 | tf_op jit(solution)/shard_map/ppermute | solution.py:377
  70.1 3.1 %collective-permute-start.12 = (bf16[8,32,384]{2,1,0:T(8,128)(2,1)}, bf16[8,32,384]{2,1,0:T(8,128)(2,1)S(1)}, u32[]{:S(2)}, u32[]{:S(2)}) collective-permute-start(bf16[8,32,384]{2,1,0:T(8,128)(2,1)} %collective-permute-done.6.refs_8_.refs_4_), channel_id=1, source_target_pairs={{0,12},{4,8},{8,4},{12,0},{16,28},{20,24},{24,20},{28,16},{1,13},{... | collective-permute-start | bytes 589832 | tf_op jit(solution)/shard_map/ppermute | solution.py:377
  73.1 1.5 %collective-permute-start.11 = (bf16[8,32,384]{2,1,0:T(8,128)(2,1)}, bf16[8,32,384]{2,1,0:T(8,128)(2,1)S(1)}, u32[]{:S(2)}, u32[]{:S(2)}) collective-permute-start(bf16[8,32,384]{2,1,0:T(8,128)(2,1)} %collective-permute-done.6.refs_8_.refs_4_), channel_id=1, source_target_pairs={{0,8},{4,12},{8,0},{12,4},{16,24},{20,28},{24,16},{28,20},{1,9},{5... | collective-permute-start | bytes 589832 | tf_op jit(solution)/shard_map/ppermute | solution.py:377
  74.7 11.1 %shard_map.86 = (bf16[768,256]{1,0:T(8,128)(2,1)}, bf16[768,256]{1,0:T(8,128)(2,1)}, bf16[8,384,256]{2,1,0:T(8,128)(2,1)}, bf16[8,256,384]{2,1,0:T(8,128)(2,1)}) custom-call(bf16[8,96,256]{2,1,0:T(8,128)(2,1)} %get-tuple-element.18.refs_0_, bf16[8,96,256]{2,1,0:T(8,128)(2,1)} %copy-done.10, bf16[8,96,256]{2,1,0:T(8,128)(2,1)} %collective-permute-done.1.refs_2_, ...), custom_call_target="tpu_custom_call" | custom-call | flops 4328521728 | bytes 3145728 | tf_op jit(solution)/shard_map/pallas_call | solution.py:240
  85.9 0.6 copy-done.17
  86.8 7.0 %shard_map.87.refs_11_ = bf16[8,2,128,128]{3,2,1,0:T(8,128)(2,1)} custom-call(bf16[8,32,384]{2,1,0:T(8,128)(2,1)} %bitcast.29, bf16[8,32,384]{2,1,0:T(8,128)(2,1)} %copy-done.17, bf16[8,32,384]{2,1,0:T(8,128)(2,1)} %copy-done.16, bf16[8,32,384]{2,1,0:T(8,128)(2,1)} %copy-done.15, bf16[8,32,384]{2,1,0:T(8,128)(2,1)} %collective-permute-done.6.refs_8_.refs_4_, ...), custom_call_target="tpu_custom_call" | custom-call | flops 2147483648 | bytes 3538944 | tf_op jit(solution)/shard_map/pallas_call | solution.py:288
  93.8 5.3 %all-to-all-start.1 = ((bf16[8,2,128,128]{3,2,1,0:T(8,128)(2,1)}), bf16[8,2,128,128]{3,2,1,0:T(8,128)(2,1)S(1)}, u32[]{:S(2)}, u32[]{:S(2)}) async-start(bf16[8,2,128,128]{3,2,1,0:T(8,128)(2,1)} %shard_map.87.refs_11_), calls=%async_computation.1 | async-start | bytes 1048576 | tf_op jit(solution)/shard_map/all_to_all | solution.py:401
  99.1 12.3 %shard_map.88.refs_7_ = bf16[8,6,128,128]{3,2,1,0:T(8,128)(2,1)} custom-call(bf16[8,32,384]{2,1,0:T(8,128)(2,1)} %bitcast.30, bf16[8,32,384]{2,1,0:T(8,128)(2,1)} %copy-done.17, bf16[8,32,384]{2,1,0:T(8,128)(2,1)} %copy-done.16, bf16[8,32,384]{2,1,0:T(8,128)(2,1)} %copy-done.15, bf16[8,32,384]{2,1,0:T(8,128)(2,1)} %collective-permute-done.6.refs_8_.refs_4_, ...), custom_call_target="tpu_custom_call" | custom-call | flops 6442450944 | bytes 3538944 | tf_op jit(solution)/shard_map/pallas_call | solution.py:288
  111.4 0.8 copy-done.1
  112.2 5.7 %all-to-all-start.2 = ((bf16[8,6,128,128]{3,2,1,0:T(8,128)(2,1)}), bf16[8,6,128,128]{3,2,1,0:T(8,128)(2,1)S(1)}, u32[]{:S(2)}, u32[]{:S(2)}) async-start(bf16[8,6,128,128]{3,2,1,0:T(8,128)(2,1)} %shard_map.88.refs_7_), calls=%async_computation.2 | async-start | bytes 3145728 | tf_op jit(solution)/shard_map/all_to_all | solution.py:403
  117.9 1.6 %collective-permute-start.15 = (bf16[768,256]{1,0:T(8,128)(2,1)S(1)}, bf16[768,256]{1,0:T(8,128)(2,1)S(1)}, u32[]{:S(2)}, u32[]{:S(2)}) collective-permute-start(bf16[768,256]{1,0:T(8,128)(2,1)S(1)} %copy-done.13), channel_id=1, source_target_pairs={{0,2},{1,3},{2,0},{3,1},{4,6},{5,7},{6,4},{7,5},{8,10},{9,11},{10,... | collective-permute-start | bytes 1179656 | tf_op jit(solution)/shard_map/ppermute | solution.py:377
  119.6 2.0 %shard_map.89.refs_8_.refs_0_ = bf16[8,4,8,32,128]{4,3,2,1,0:T(8,128)(2,1)} custom-call(bf16[8,2,4,32,128]{4,3,2,1,0:T(8,128)(2,1)} %bitcast.17), custom_call_target="tpu_custom_call" | custom-call | flops 300000000 | bytes 4000000 | tf_op jit(solution)/shard_map/pallas_call | solution.py:360
  121.6 9.8 %shard_map.90 = (bf16[768,256]{1,0:T(8,128)(2,1)}, bf16[768,256]{1,0:T(8,128)(2,1)}) custom-call(bf16[8,96,256]{2,1,0:T(8,128)(2,1)} %get-tuple-element.18.refs_0_, bf16[8,96,256]{2,1,0:T(8,128)(2,1)} %copy-done.10, bf16[8,384,256]{2,1,0:T(8,128)(2,1)} %get-tuple-element.26.refs_2_, bf16[8,256,384]{2,1,0:T(8,128)(2,1)} %get-tuple-element.27.refs_3_, ...), custom_call_target="tpu_custom_call" | custom-call | flops 4328521728 | bytes 3145728 | tf_op jit(solution)/shard_map/pallas_call | solution.py:240
  131.4 2.1 %collective-permute-start.14 = (bf16[768,256]{1,0:T(8,128)(2,1)}, bf16[768,256]{1,0:T(8,128)(2,1)S(1)}, u32[]{:S(2)}, u32[]{:S(2)}) collective-permute-start(bf16[768,256]{1,0:T(8,128)(2,1)} %get-tuple-element.32), channel_id=1, source_target_pairs={{0,1},{1,0},{2,3},{3,2},{4,5},{5,4},{6,7},{7,6},{8,9},{9,8},{10,11... | collective-permute-start | bytes 1179656 | tf_op jit(solution)/shard_map/ppermute | solution.py:377
  133.5 2.0 %collective-permute-done.16 = bf16[768,256]{1,0:T(8,128)(2,1)S(1)} collective-permute-done((bf16[768,256]{1,0:T(8,128)(2,1)S(1)}, bf16[768,256]{1,0:T(8,128)(2,1)S(1)}, u32[]{:S(2)}, u32[]{:S(2)}) %collective-permute-start.16) | collective-permute-done | bytes 393248 | tf_op jit(solution)/shard_map/ppermute | solution.py:377
  135.4 0.7 copy-done.4
  136.4 2.8 %shard_map.91 = bf16[96,4,8,256]{3,2,1,0:T(8,128)(2,1)} custom-call(bf16[96,8,256]{2,1,0:T(8,128)(2,1)} %bitcast.22, bf16[96,8,256]{2,1,0:T(8,128)(2,1)} %bitcast.23, bf16[96,8,256]{2,1,0:T(8,128)(2,1)} %bitcast.20, bf16[96,8,256]{2,1,0:T(8,128)(2,1)} %bitcast.21), custom_call_target="tpu_custom_call" | custom-call | flops 300000000 | bytes 4000000 | tf_op jit(solution)/shard_map/pallas_call | solution.py:316
  139.2 1.2 copy-done
  140.4 2.5 %shard_map.92 = bf16[8,4,8,32,128]{4,3,2,1,0:T(8,128)(2,1)} custom-call(bf16[8,6,4,32,128]{4,3,2,1,0:T(8,128)(2,1)} %bitcast.16, bf16[8,4,8,32,128]{4,3,2,1,0:T(8,128)(2,1)} %shard_map.89.refs_8_.refs_0_), custom_call_target="tpu_custom_call", output_to_operand_aliasing={{}: (1, {})} | custom-call | flops 300000000 | bytes 4000000 | tf_op jit(solution)/shard_map/pallas_call | solution.py:360
  (66 shorter events, 2.1 us)
Async XLA Ops:
  7.3 30.1 %copy-start.23 = (bf16[96,256]{1,0:T(8,128)(2,1)S(1)}, bf16[96,256]{1,0:T(8,128)(2,1)}, u32[]{:S(2)}) copy-start(bf16[96,256]{1,0:T(8,128)(2,1)} %get-tuple-element.23) | copy-start | bytes 147460
  7.3 30.6 %copy-start.22 = (bf16[96,256]{1,0:T(8,128)(2,1)S(1)}, bf16[96,256]{1,0:T(8,128)(2,1)}, u32[]{:S(2)}) copy-start(bf16[96,256]{1,0:T(8,128)(2,1)} %get-tuple-element.24) | copy-start | bytes 147460
  7.3 31.4 %copy-start.21 = (bf16[96,256]{1,0:T(8,128)(2,1)S(1)}, bf16[96,256]{1,0:T(8,128)(2,1)}, u32[]{:S(2)}) copy-start(bf16[96,256]{1,0:T(8,128)(2,1)} %get-tuple-element.25) | copy-start | bytes 147460
  7.3 43.3 %copy-start.12 = (bf16[8,96,256]{2,1,0:T(8,128)(2,1)S(1)}, bf16[8,96,256]{2,1,0:T(8,128)(2,1)}, u32[]{:S(2)}) copy-start(bf16[8,96,256]{2,1,0:T(8,128)(2,1)} %get-tuple-element.20) | copy-start | bytes 1179652
  7.3 52.9 %copy-start.11 = (bf16[8,96,256]{2,1,0:T(8,128)(2,1)S(1)}, bf16[8,96,256]{2,1,0:T(8,128)(2,1)}, u32[]{:S(2)}) copy-start(bf16[8,96,256]{2,1,0:T(8,128)(2,1)} %get-tuple-element.21) | copy-start | bytes 1179652
  7.3 55.3 %copy-start.6 = (bf16[1024,128]{1,0:T(8,128)(2,1)S(1)}, bf16[1024,128]{1,0:T(8,128)(2,1)}, u32[]{:S(2)}) copy-start(bf16[1024,128]{1,0:T(8,128)(2,1)} %param.13) | copy-start | bytes 786436
  37.3 48.5 %copy-start.2 = (bf16[8,96,1024]{2,1,0:T(8,128)(2,1)}, bf16[8,96,1024]{2,1,0:T(8,128)(2,1)S(1)}, u32[]{:S(2)}) copy-start(bf16[8,96,1024]{2,1,0:T(8,128)(2,1)S(1)} %all_to_all.15.refs_8_) | copy-start | bytes 4718596
  37.3 48.6 %collective-permute-start.13 = (bf16[8,96,1024]{2,1,0:T(8,128)(2,1)S(1)}, bf16[8,96,1024]{2,1,0:T(8,128)(2,1)}, u32[]{:S(2)}, u32[]{:S(2)}) collective-permute-start(bf16[8,96,1024]{2,1,0:T(8,128)(2,1)S(1)} %all_to_all.15.refs_8_), channel_id=1, source_target_pairs={{0,1},{1,0},{2,3},{3,2},{4,5},{5,4},{6,7},{7,6},{8,9},{9,8},{10,11... | collective-permute-start | bytes 4718600 | tf_op jit(solution)/shard_map/ppermute | solution.py:377
  37.4 3.5 %collective-permute-start.3 = (bf16[96,256]{1,0:T(8,128)(2,1)S(1)}, bf16[96,256]{1,0:T(8,128)(2,1)S(1)}, u32[]{:S(2)}, u32[]{:S(2)}) collective-permute-start(bf16[96,256]{1,0:T(8,128)(2,1)S(1)} %copy-done.23), channel_id=1, source_target_pairs={{0,1},{1,0},{2,3},{3,2},{4,5},{5,4},{6,7},{7,6},{8,9},{9,8},{10,11... | collective-permute-start | bytes 147464 | tf_op jit(solution)/shard_map/ppermute | solution.py:377
  37.9 5.8 %collective-permute-start.4 = (bf16[96,256]{1,0:T(8,128)(2,1)S(1)}, bf16[96,256]{1,0:T(8,128)(2,1)S(1)}, u32[]{:S(2)}, u32[]{:S(2)}) collective-permute-start(bf16[96,256]{1,0:T(8,128)(2,1)S(1)} %copy-done.22), channel_id=1, source_target_pairs={{0,2},{1,3},{2,0},{3,1},{4,6},{5,7},{6,4},{7,5},{8,10},{9,11},{10,... | collective-permute-start | bytes 147464 | tf_op jit(solution)/shard_map/ppermute | solution.py:377
  38.7 5.5 %collective-permute-start.5 = (bf16[96,256]{1,0:T(8,128)(2,1)S(1)}, bf16[96,256]{1,0:T(8,128)(2,1)S(1)}, u32[]{:S(2)}, u32[]{:S(2)}) collective-permute-start(bf16[96,256]{1,0:T(8,128)(2,1)S(1)} %copy-done.21), channel_id=1, source_target_pairs={{0,3},{1,2},{2,1},{3,0},{4,7},{5,6},{6,5},{7,4},{8,11},{9,10},{10,... | collective-permute-start | bytes 147464 | tf_op jit(solution)/shard_map/ppermute | solution.py:377
  40.9 3.4 %copy-start.7 = (bf16[96,256]{1,0:T(8,128)(2,1)}, bf16[96,256]{1,0:T(8,128)(2,1)S(1)}, u32[]{:S(2)}) copy-start(bf16[96,256]{1,0:T(8,128)(2,1)S(1)} %collective-permute-done.3.p1) | copy-start | bytes 147460
  46.6 13.6 %collective-permute-start.9 = (bf16[8,32,384]{2,1,0:T(8,128)(2,1)}, bf16[8,32,384]{2,1,0:T(8,128)(2,1)S(1)}, u32[]{:S(2)}, u32[]{:S(2)}) collective-permute-start(bf16[8,32,384]{2,1,0:T(8,128)(2,1)} %bitcast.25), channel_id=1, source_target_pairs={{0,12},{4,8},{8,4},{12,0},{16,28},{20,24},{24,20},{28,16},{1,13},{... | collective-permute-start | bytes 589832 | tf_op jit(solution)/shard_map/ppermute | solution.py:377
  50.6 11.4 %collective-permute-start.8 = (bf16[8,32,384]{2,1,0:T(8,128)(2,1)}, bf16[8,32,384]{2,1,0:T(8,128)(2,1)S(1)}, u32[]{:S(2)}, u32[]{:S(2)}) collective-permute-start(bf16[8,32,384]{2,1,0:T(8,128)(2,1)} %bitcast.26), channel_id=1, source_target_pairs={{0,8},{4,12},{8,0},{12,4},{16,24},{20,28},{24,16},{28,20},{1,9},{5... | collective-permute-start | bytes 589832 | tf_op jit(solution)/shard_map/ppermute | solution.py:377
  50.6 19.5 %collective-permute-start = (bf16[8,96,256]{2,1,0:T(8,128)(2,1)}, bf16[8,96,256]{2,1,0:T(8,128)(2,1)S(1)}, u32[]{:S(2)}, u32[]{:S(2)}) collective-permute-start(bf16[8,96,256]{2,1,0:T(8,128)(2,1)} %get-tuple-element.19), channel_id=1, source_target_pairs={{0,1},{1,0},{2,3},{3,2},{4,5},{5,4},{6,7},{7,6},{8,9},{9,8},{10,11... | collective-permute-start | bytes 1179656 | tf_op jit(solution)/shard_map/ppermute | solution.py:377
  50.6 22.5 %collective-permute-start.1 = (bf16[8,96,256]{2,1,0:T(8,128)(2,1)S(1)}, bf16[8,96,256]{2,1,0:T(8,128)(2,1)}, u32[]{:S(2)}, u32[]{:S(2)}) collective-permute-start(bf16[8,96,256]{2,1,0:T(8,128)(2,1)S(1)} %copy-done.12), channel_id=1, source_target_pairs={{0,2},{1,3},{2,0},{3,1},{4,6},{5,7},{6,4},{7,5},{8,10},{9,11},{10,... | collective-permute-start | bytes 1179656 | tf_op jit(solution)/shard_map/ppermute | solution.py:377
  60.2 25.6 %copy-start.15 = (bf16[8,32,384]{2,1,0:T(8,128)(2,1)}, bf16[8,32,384]{2,1,0:T(8,128)(2,1)S(1)}, u32[]{:S(2)}) copy-start(bf16[8,32,384]{2,1,0:T(8,128)(2,1)S(1)} %collective-permute-done.9.refs_3_) | copy-start | bytes 589828
  60.2 14.4 %collective-permute-start.2 = (bf16[8,96,256]{2,1,0:T(8,128)(2,1)S(1)}, bf16[8,96,256]{2,1,0:T(8,128)(2,1)}, u32[]{:S(2)}, u32[]{:S(2)}) collective-permute-start(bf16[8,96,256]{2,1,0:T(8,128)(2,1)S(1)} %copy-done.11), channel_id=1, source_target_pairs={{0,3},{1,2},{2,1},{3,0},{4,7},{5,6},{6,5},{7,4},{8,11},{9,10},{10,... | collective-permute-start | bytes 1179656 | tf_op jit(solution)/shard_map/ppermute | solution.py:377
  62.0 8.1 %collective-permute-start.6 = (bf16[8,32,384]{2,1,0:T(8,128)(2,1)}, bf16[8,32,384]{2,1,0:T(8,128)(2,1)}, u32[]{:S(2)}, u32[]{:S(2)}) collective-permute-start(bf16[8,32,384]{2,1,0:T(8,128)(2,1)} %bitcast.27), channel_id=1, source_target_pairs={{0,16},{4,20},{8,24},{12,28},{16,0},{20,4},{24,8},{28,12},{1,17},{... | collective-permute-start | bytes 589832 | tf_op jit(solution)/shard_map/ppermute | solution.py:377
  70.1 15.8 %collective-permute-start.7 = (bf16[8,32,384]{2,1,0:T(8,128)(2,1)}, bf16[8,32,384]{2,1,0:T(8,128)(2,1)S(1)}, u32[]{:S(2)}, u32[]{:S(2)}) collective-permute-start(bf16[8,32,384]{2,1,0:T(8,128)(2,1)} %bitcast.28), channel_id=1, source_target_pairs={{0,4},{4,0},{8,12},{12,8},{16,20},{20,16},{24,28},{28,24},{1,5},{5... | collective-permute-start | bytes 589832 | tf_op jit(solution)/shard_map/ppermute | solution.py:377
  70.1 4.7 %copy-start.10 = (bf16[8,96,256]{2,1,0:T(8,128)(2,1)}, bf16[8,96,256]{2,1,0:T(8,128)(2,1)S(1)}, u32[]{:S(2)}) copy-start(bf16[8,96,256]{2,1,0:T(8,128)(2,1)S(1)} %collective-permute-done.refs_1_) | copy-start | bytes 1179652
  70.1 15.8 %collective-permute-start.12 = (bf16[8,32,384]{2,1,0:T(8,128)(2,1)}, bf16[8,32,384]{2,1,0:T(8,128)(2,1)S(1)}, u32[]{:S(2)}, u32[]{:S(2)}) collective-permute-start(bf16[8,32,384]{2,1,0:T(8,128)(2,1)} %collective-permute-done.6.refs_8_.refs_4_), channel_id=1, source_target_pairs={{0,12},{4,8},{8,4},{12,0},{16,28},{20,24},{24,20},{28,16},{1,13},{... | collective-permute-start | bytes 589832 | tf_op jit(solution)/shard_map/ppermute | solution.py:377
  73.1 12.8 %collective-permute-start.11 = (bf16[8,32,384]{2,1,0:T(8,128)(2,1)}, bf16[8,32,384]{2,1,0:T(8,128)(2,1)S(1)}, u32[]{:S(2)}, u32[]{:S(2)}) collective-permute-start(bf16[8,32,384]{2,1,0:T(8,128)(2,1)} %collective-permute-done.6.refs_8_.refs_4_), channel_id=1, source_target_pairs={{0,8},{4,12},{8,0},{12,4},{16,24},{20,28},{24,16},{28,20},{1,9},{5... | collective-permute-start | bytes 589832 | tf_op jit(solution)/shard_map/ppermute | solution.py:377
  74.6 11.3 %collective-permute-start.10 = (bf16[8,32,384]{2,1,0:T(8,128)(2,1)}, bf16[8,32,384]{2,1,0:T(8,128)(2,1)S(1)}, u32[]{:S(2)}, u32[]{:S(2)}) collective-permute-start(bf16[8,32,384]{2,1,0:T(8,128)(2,1)} %collective-permute-done.6.refs_8_.refs_4_), channel_id=1, source_target_pairs={{0,4},{4,0},{8,12},{12,8},{16,20},{20,16},{24,28},{28,24},{1,5},{5... | collective-permute-start | bytes 589832 | tf_op jit(solution)/shard_map/ppermute | solution.py:377
  93.8 17.6 %all-to-all-start.1 = ((bf16[8,2,128,128]{3,2,1,0:T(8,128)(2,1)}), bf16[8,2,128,128]{3,2,1,0:T(8,128)(2,1)S(1)}, u32[]{:S(2)}, u32[]{:S(2)}) async-start(bf16[8,2,128,128]{3,2,1,0:T(8,128)(2,1)} %shard_map.87.refs_11_), calls=%async_computation.1 | async-start | bytes 1048576 | tf_op jit(solution)/shard_map/all_to_all | solution.py:401
  111.4 6.5 %copy-start.13 = (bf16[768,256]{1,0:T(8,128)(2,1)S(1)}, bf16[768,256]{1,0:T(8,128)(2,1)}, u32[]{:S(2)}) copy-start(bf16[768,256]{1,0:T(8,128)(2,1)} %get-tuple-element.30.refs_11_) | copy-start | bytes 1179652
  111.4 8.2 %copy-start.14 = (bf16[768,256]{1,0:T(8,128)(2,1)S(1)}, bf16[768,256]{1,0:T(8,128)(2,1)}, u32[]{:S(2)}) copy-start(bf16[768,256]{1,0:T(8,128)(2,1)} %get-tuple-element.33) | copy-start | bytes 1179652
  112.2 27.0 %all-to-all-start.2 = ((bf16[8,6,128,128]{3,2,1,0:T(8,128)(2,1)}), bf16[8,6,128,128]{3,2,1,0:T(8,128)(2,1)S(1)}, u32[]{:S(2)}, u32[]{:S(2)}) async-start(bf16[8,6,128,128]{3,2,1,0:T(8,128)(2,1)} %shard_map.88.refs_7_), calls=%async_computation.2 | async-start | bytes 3145728 | tf_op jit(solution)/shard_map/all_to_all | solution.py:403
  117.9 17.5 %collective-permute-start.15 = (bf16[768,256]{1,0:T(8,128)(2,1)S(1)}, bf16[768,256]{1,0:T(8,128)(2,1)S(1)}, u32[]{:S(2)}, u32[]{:S(2)}) collective-permute-start(bf16[768,256]{1,0:T(8,128)(2,1)S(1)} %copy-done.13), channel_id=1, source_target_pairs={{0,2},{1,3},{2,0},{3,1},{4,6},{5,7},{6,4},{7,5},{8,10},{9,11},{10,... | collective-permute-start | bytes 1179656 | tf_op jit(solution)/shard_map/ppermute | solution.py:377
  119.6 15.8 %collective-permute-start.16 = (bf16[768,256]{1,0:T(8,128)(2,1)S(1)}, bf16[768,256]{1,0:T(8,128)(2,1)S(1)}, u32[]{:S(2)}, u32[]{:S(2)}) collective-permute-start(bf16[768,256]{1,0:T(8,128)(2,1)S(1)} %copy-done.14), channel_id=1, source_target_pairs={{0,3},{1,2},{2,1},{3,0},{4,7},{5,6},{6,5},{7,4},{8,11},{9,10},{10,... | collective-permute-start | bytes 1179656 | tf_op jit(solution)/shard_map/ppermute | solution.py:377
  131.4 4.0 %collective-permute-start.14 = (bf16[768,256]{1,0:T(8,128)(2,1)}, bf16[768,256]{1,0:T(8,128)(2,1)S(1)}, u32[]{:S(2)}, u32[]{:S(2)}) collective-permute-start(bf16[768,256]{1,0:T(8,128)(2,1)} %get-tuple-element.32), channel_id=1, source_target_pairs={{0,1},{1,0},{2,3},{3,2},{4,5},{5,4},{6,7},{7,6},{8,9},{9,8},{10,11... | collective-permute-start | bytes 1179656 | tf_op jit(solution)/shard_map/ppermute | solution.py:377
  139.2 1.2 copy-start
  (11 other events, 8.5 us)

commit v5 on v4

--- a/solution.py
+++ b/solution.py
@@ -15,7 +15,7 @@
 SEQ = ("xh", "c")
 ROWS = ("yl", "z")
 XY = ("xl", "yh", "xh")
-SPLIT = 2
+SPLIT = 3
 PAD = 40
 AT_ONCE = 4
 NT = (((1,), (1,)), ((), ()))
@@ -369,7 +369,7 @@
         ],
         input_output_aliases={1: 0} if more else {},
         cost_estimate=pl.CostEstimate(flops=300_000_000, transcendentals=0, bytes_accessed=4_000_000),
-    )(got.reshape(8, count, 4, 32, 128), *more)
+    )(pltpu.with_memory_space_constraint(got.reshape(8, count, 4, 32, 128), pltpu.HBM), *more)
 
 
 def swap(x, axes, k):
@@ -395,7 +395,7 @@
     weights = (query_weight, w_keyval, w_gate, output_weight)
     w_t = w_pair_out.reshape(32, 32, 128).transpose(2, 1, 0).reshape(128, 1024)
     scaling = 1.0 / total
-    u2, u3, *kept = attention(blocks, None, weights, (left_y,))
+    u2, u3, *kept = attention(blocks, None, weights, (left_y, w_t))
     backs = [None, None, swap(u2, SEQ, 2), swap(u3, SEQ, 3)]
     out0 = pair_block(left8, rights, w_t, 0, SPLIT, scaling, (u2,))
     got0 = lax.all_to_all(out0, ROWS, 0, 0)

time: 146 us -> 145 us (level)
    unnamed x48 -> x46, local copies, waits for them, and re-layouts: 4.53 us -> 3.68 us
  transfers between devices with their start and end apart: 19 -> 19, of which waited for: 6 -> 7; matrix products, arithmetic and copies ran while one was open for 1% -> 1% of each run, Pallas kernels for 28% -> 27%
where the time goes in v5:
time: 145 us; the launch traced here: 142 us
  Pallas kernels  55.4 us (38%)
  starting transfers between devices  31.8 us (22%)
  blocking collectives  30 us (21%)
  waiting for transfers between devices  19.1 us (13%)
  local copies, waits for them, and re-layouts  4.64 us (3%)
    all_to_all x1, blocking collectives, layer(): near = lax.all_to_all(right, XY, 0, 0)  30 us
    ppermute x17, starting transfers between devices, swap(): return lax.ppermute(x, axes, [(j, j ^ k) for j in range(n)])  21.1 us
    pallas_call x2, Pallas kernels, attention(): pl.pallas_call(lambda *refs: kernel(len(waits), *refs), grid=(count // AT...  20.9 us
    pallas_call x2, Pallas kernels, pair_block(): pl.pallas_call(lambda *refs: pair_kernel(scaling, r0, count, *refs), in_s...  18.8 us
    ppermute x17, waiting for transfers between devices, swap(): return lax.ppermute(x, axes, [(j, j ^ k) for j in range(n)])  18.6 us
    pallas_call x1, Pallas kernels, front(): pl.pallas_call(front_kernel, in_specs=[vmem, vmem], out_shape=[jax.ShapeD...  6.67 us
    all_to_all x1, starting transfers between devices, layer(): got1 = lax.all_to_all(out1, ROWS, 0, 0)  5.42 us
    all_to_all x1, starting transfers between devices, layer(): got0 = lax.all_to_all(out0, ROWS, 0, 0)  5.26 us
  transfers between devices with their start and end apart: 19, of which 7 were waited for; matrix products, arithmetic and copies ran while one was open for 1% of the time, Pallas kernels for 27%

profile of v5, /device:TPU:0, one launch (start us, length us, event | category | flops | bytes accessed | tf_op | source)
XLA Modules:
  0.0 141.9 jit_solution(3881657857914299531)
XLA Ops:
  0.6 6.7 %front.1 = (bf16[8,96,256]{2,1,0:T(8,128)(2,1)}, bf16[8,96,256]{2,1,0:T(8,128)(2,1)}, bf16[8,96,256]{2,1,0:T(8,128)(2,1)}, bf16[8,96,256]{2,1,0:T(8,128)(2,1)}, ...) custom-call(bf16[3072,256]{1,0:T(8,128)(2,1)} %bitcast.31, ...), custom_call_target="tpu_custom_call" | custom-call | flops 800000000 | bytes 3145728 | tf_op jit(solution)/shard_map/front/pallas_call | solution.py:80
  7.3 30.0 %all_to_all.15.refs_8_ = bf16[8,96,1024]{2,1,0:T(8,128)(2,1)S(1)} all-to-all(bf16[8,96,1024]{2,1,0:T(8,128)(2,1)} %get-tuple-element.29), channel_id=1, replica_groups=mesh['xl'=2,'yh'=2,'yl'=2,'z'=4,'xh'=2,'c'=2] {'xl','yh','xh'}, dimensions={0} | all-to-all | bytes 3145728 | tf_op jit(solution)/shard_map/all_to_all | solution.py:386
  37.9 0.9 collective-permute-start.4
  38.7 2.1 %collective-permute-start.5 = (bf16[96,256]{1,0:T(8,128)(2,1)S(1)}, bf16[96,256]{1,0:T(8,128)(2,1)S(1)}, u32[]{:S(2)}, u32[]{:S(2)}) collective-permute-start(bf16[96,256]{1,0:T(8,128)(2,1)S(1)} %copy-done.20), channel_id=1, source_target_pairs={{0,3},{1,2},{2,1},{3,0},{4,7},{5,6},{6,5},{7,4},{8,11},{9,10},{10,... | collective-permute-start | bytes 147464 | tf_op jit(solution)/shard_map/ppermute | solution.py:377
  40.9 2.8 %collective-permute-done.4.p2 = bf16[96,256]{1,0:T(8,128)(2,1)S(1)} collective-permute-done((bf16[96,256]{1,0:T(8,128)(2,1)S(1)}, bf16[96,256]{1,0:T(8,128)(2,1)S(1)}, u32[]{:S(2)}, u32[]{:S(2)}) %collective-permute-start.4) | collective-permute-done | bytes 49184 | tf_op jit(solution)/shard_map/ppermute | solution.py:377
  43.7 0.6 collective-permute-done.5.p3
  44.3 0.6 copy-done.9
  44.9 1.7 %merge_left.1 = bf16[256,384]{1,0:T(8,128)(2,1)} custom-call(bf16[96,256]{1,0:T(8,128)(2,1)} %get-tuple-element.22.p0, bf16[96,256]{1,0:T(8,128)(2,1)} %copy-done.7, bf16[96,256]{1,0:T(8,128)(2,1)} %copy-done.8, bf16[96,256]{1,0:T(8,128)(2,1)} %copy-done.9), custom_call_target="tpu_custom_call" | custom-call | flops 100000000 | bytes 393216 | tf_op jit(solution)/shard_map/merge_left/pallas_call | solution.py:107
  46.6 4.0 %collective-permute-start.9 = (bf16[8,32,384]{2,1,0:T(8,128)(2,1)}, bf16[8,32,384]{2,1,0:T(8,128)(2,1)S(1)}, u32[]{:S(2)}, u32[]{:S(2)}) collective-permute-start(bf16[8,32,384]{2,1,0:T(8,128)(2,1)} %bitcast.25), channel_id=1, source_target_pairs={{0,12},{4,8},{8,4},{12,0},{16,28},{20,24},{24,20},{28,16},{1,13},{... | collective-permute-start | bytes 589832 | tf_op jit(solution)/shard_map/ppermute | solution.py:377
  50.6 2.7 %collective-permute-start.1 = (bf16[8,96,256]{2,1,0:T(8,128)(2,1)S(1)}, bf16[8,96,256]{2,1,0:T(8,128)(2,1)}, u32[]{:S(2)}, u32[]{:S(2)}) collective-permute-start(bf16[8,96,256]{2,1,0:T(8,128)(2,1)S(1)} %copy-done.12), channel_id=1, source_target_pairs={{0,2},{1,3},{2,0},{3,1},{4,6},{5,7},{6,4},{7,5},{8,10},{9,11},{10,... | collective-permute-start | bytes 1179656 | tf_op jit(solution)/shard_map/ppermute | solution.py:377
  53.4 6.8 %collective-permute-done.9.refs_3_ = bf16[8,32,384]{2,1,0:T(8,128)(2,1)S(1)} collective-permute-done((bf16[8,32,384]{2,1,0:T(8,128)(2,1)}, bf16[8,32,384]{2,1,0:T(8,128)(2,1)S(1)}, u32[]{:S(2)}, u32[]{:S(2)}) %collective-permute-start.9) | collective-permute-done | bytes 196640 | tf_op jit(solution)/shard_map/ppermute | solution.py:377
  60.2 1.8 %collective-permute-start.2 = (bf16[8,96,256]{2,1,0:T(8,128)(2,1)S(1)}, bf16[8,96,256]{2,1,0:T(8,128)(2,1)}, u32[]{:S(2)}, u32[]{:S(2)}) collective-permute-start(bf16[8,96,256]{2,1,0:T(8,128)(2,1)S(1)} %copy-done.11), channel_id=1, source_target_pairs={{0,3},{1,2},{2,1},{3,0},{4,7},{5,6},{6,5},{7,4},{8,11},{9,10},{10,... | collective-permute-start | bytes 1179656 | tf_op jit(solution)/shard_map/ppermute | solution.py:377
  62.0 0.7 collective-permute-start.6
  62.8 0.9 copy.15.refs_9_.refs_10_
  63.6 6.4 %collective-permute-done.6.refs_8_.refs_4_ = bf16[8,32,384]{2,1,0:T(8,128)(2,1)} collective-permute-done((bf16[8,32,384]{2,1,0:T(8,128)(2,1)}, bf16[8,32,384]{2,1,0:T(8,128)(2,1)}, u32[]{:S(2)}, u32[]{:S(2)}) %collective-permute-start.6) | collective-permute-done | bytes 196640 | tf_op jit(solution)/shard_map/ppermute | solution.py:377
  70.1 3.1 %collective-permute-start.12 = (bf16[8,32,384]{2,1,0:T(8,128)(2,1)}, bf16[8,32,384]{2,1,0:T(8,128)(2,1)S(1)}, u32[]{:S(2)}, u32[]{:S(2)}) collective-permute-start(bf16[8,32,384]{2,1,0:T(8,128)(2,1)} %collective-permute-done.6.refs_8_.refs_4_), channel_id=1, source_target_pairs={{0,12},{4,8},{8,4},{12,0},{16,28},{20,24},{24,20},{28,16},{1,13},{... | collective-permute-start | bytes 589832 | tf_op jit(solution)/shard_map/ppermute | solution.py:377
  73.1 1.5 %collective-permute-start.11 = (bf16[8,32,384]{2,1,0:T(8,128)(2,1)}, bf16[8,32,384]{2,1,0:T(8,128)(2,1)S(1)}, u32[]{:S(2)}, u32[]{:S(2)}) collective-permute-start(bf16[8,32,384]{2,1,0:T(8,128)(2,1)} %collective-permute-done.6.refs_8_.refs_4_), channel_id=1, source_target_pairs={{0,8},{4,12},{8,0},{12,4},{16,24},{20,28},{24,16},{28,20},{1,9},{5... | collective-permute-start | bytes 589832 | tf_op jit(solution)/shard_map/ppermute | solution.py:377
  74.8 11.1 %shard_map.86 = (bf16[768,256]{1,0:T(8,128)(2,1)}, bf16[768,256]{1,0:T(8,128)(2,1)}, bf16[8,384,256]{2,1,0:T(8,128)(2,1)}, bf16[8,256,384]{2,1,0:T(8,128)(2,1)}) custom-call(bf16[8,96,256]{2,1,0:T(8,128)(2,1)} %get-tuple-element.18.refs_0_, bf16[8,96,256]{2,1,0:T(8,128)(2,1)} %copy-done.10, bf16[8,96,256]{2,1,0:T(8,128)(2,1)} %collective-permute-done.1.refs_2_, ...), custom_call_target="tpu_custom_call" | custom-call | flops 4328521728 | bytes 3145728 | tf_op jit(solution)/shard_map/pallas_call | solution.py:240
  85.9 0.6 copy-done.16
  86.8 8.0 %shard_map.87.refs_11_ = bf16[8,3,128,128]{3,2,1,0:T(8,128)(2,1)} custom-call(bf16[8,32,384]{2,1,0:T(8,128)(2,1)} %bitcast.29, bf16[8,32,384]{2,1,0:T(8,128)(2,1)} %copy-done.16, bf16[8,32,384]{2,1,0:T(8,128)(2,1)} %copy-done.15, bf16[8,32,384]{2,1,0:T(8,128)(2,1)} %copy-done.14, bf16[8,32,384]{2,1,0:T(8,128)(2,1)} %collective-permute-done.6.refs_8_.refs_4_, ...), custom_call_target="tpu_custom_call" | custom-call | flops 3221225472 | bytes 3538944 | tf_op jit(solution)/shard_map/pallas_call | solution.py:288
  94.8 5.3 %all-to-all-start.1 = ((bf16[8,3,128,128]{3,2,1,0:T(8,128)(2,1)}), bf16[8,3,128,128]{3,2,1,0:T(8,128)(2,1)S(1)}, u32[]{:S(2)}, u32[]{:S(2)}) async-start(bf16[8,3,128,128]{3,2,1,0:T(8,128)(2,1)} %shard_map.87.refs_11_), calls=%async_computation.1 | async-start | bytes 1572864 | tf_op jit(solution)/shard_map/all_to_all | solution.py:401
  100.1 10.8 %shard_map.88.refs_7_ = bf16[8,5,128,128]{3,2,1,0:T(8,128)(2,1)} custom-call(bf16[8,32,384]{2,1,0:T(8,128)(2,1)} %bitcast.30, bf16[8,32,384]{2,1,0:T(8,128)(2,1)} %copy-done.16, bf16[8,32,384]{2,1,0:T(8,128)(2,1)} %copy-done.15, bf16[8,32,384]{2,1,0:T(8,128)(2,1)} %copy-done.14, bf16[8,32,384]{2,1,0:T(8,128)(2,1)} %collective-permute-done.6.refs_8_.refs_4_, ...), custom_call_target="tpu_custom_call" | custom-call | flops 5368709120 | bytes 3538944 | tf_op jit(solution)/shard_map/pallas_call | solution.py:288
  111.4 5.4 %all-to-all-start.2 = ((bf16[8,5,128,128]{3,2,1,0:T(8,128)(2,1)}), bf16[8,5,128,128]{3,2,1,0:T(8,128)(2,1)S(1)}, u32[]{:S(2)}, u32[]{:S(2)}) async-start(bf16[8,5,128,128]{3,2,1,0:T(8,128)(2,1)} %shard_map.88.refs_7_), calls=%async_computation.2 | async-start | bytes 2621440 | tf_op jit(solution)/shard_map/all_to_all | solution.py:403
  116.8 1.6 %collective-permute-start.15 = (bf16[768,256]{1,0:T(8,128)(2,1)S(1)}, bf16[768,256]{1,0:T(8,128)(2,1)S(1)}, u32[]{:S(2)}, u32[]{:S(2)}) collective-permute-start(bf16[768,256]{1,0:T(8,128)(2,1)S(1)} %copy-done.13), channel_id=1, source_target_pairs={{0,2},{1,3},{2,0},{3,1},{4,6},{5,7},{6,4},{7,5},{8,10},{9,11},{10,... | collective-permute-start | bytes 1179656 | tf_op jit(solution)/shard_map/ppermute | solution.py:377
  118.5 2.2 %shard_map.89.refs_8_.refs_0_ = bf16[8,4,8,32,128]{4,3,2,1,0:T(8,128)(2,1)} custom-call(bf16[8,3,4,32,128]{4,3,2,1,0:T(8,128)(2,1)} %bitcast.17), custom_call_target="tpu_custom_call" | custom-call | flops 300000000 | bytes 4000000 | tf_op jit(solution)/shard_map/pallas_call | solution.py:360
  120.7 9.8 %shard_map.90 = (bf16[768,256]{1,0:T(8,128)(2,1)}, bf16[768,256]{1,0:T(8,128)(2,1)}) custom-call(bf16[8,96,256]{2,1,0:T(8,128)(2,1)} %get-tuple-element.18.refs_0_, bf16[8,96,256]{2,1,0:T(8,128)(2,1)} %copy-done.10, bf16[8,384,256]{2,1,0:T(8,128)(2,1)} %get-tuple-element.27.refs_2_, bf16[8,256,384]{2,1,0:T(8,128)(2,1)} %get-tuple-element.28.refs_3_, ...), custom_call_target="tpu_custom_call" | custom-call | flops 4328521728 | bytes 3145728 | tf_op jit(solution)/shard_map/pallas_call | solution.py:240
  130.4 2.1 %collective-permute-start.14 = (bf16[768,256]{1,0:T(8,128)(2,1)}, bf16[768,256]{1,0:T(8,128)(2,1)S(1)}, u32[]{:S(2)}, u32[]{:S(2)}) collective-permute-start(bf16[768,256]{1,0:T(8,128)(2,1)} %get-tuple-element.32), channel_id=1, source_target_pairs={{0,1},{1,0},{2,3},{3,2},{4,5},{5,4},{6,7},{7,6},{8,9},{9,8},{10,11... | collective-permute-start | bytes 1179656 | tf_op jit(solution)/shard_map/ppermute | solution.py:377
  132.5 1.9 %collective-permute-done.16 = bf16[768,256]{1,0:T(8,128)(2,1)S(1)} collective-permute-done((bf16[768,256]{1,0:T(8,128)(2,1)}, bf16[768,256]{1,0:T(8,128)(2,1)S(1)}, u32[]{:S(2)}, u32[]{:S(2)}) %collective-permute-start.16) | collective-permute-done | bytes 393248 | tf_op jit(solution)/shard_map/ppermute | solution.py:377
  134.4 0.7 copy-done.4
  135.4 2.8 %shard_map.91 = bf16[96,4,8,256]{3,2,1,0:T(8,128)(2,1)} custom-call(bf16[96,8,256]{2,1,0:T(8,128)(2,1)} %bitcast.22, bf16[96,8,256]{2,1,0:T(8,128)(2,1)} %bitcast.23, bf16[96,8,256]{2,1,0:T(8,128)(2,1)} %bitcast.20, bf16[96,8,256]{2,1,0:T(8,128)(2,1)} %bitcast.21), custom_call_target="tpu_custom_call" | custom-call | flops 300000000 | bytes 4000000 | tf_op jit(solution)/shard_map/pallas_call | solution.py:316
  138.2 1.1 copy-done
  139.3 2.4 %shard_map.92 = bf16[8,4,8,32,128]{4,3,2,1,0:T(8,128)(2,1)} custom-call(bf16[8,5,4,32,128]{4,3,2,1,0:T(8,128)(2,1)} %bitcast.16, bf16[8,4,8,32,128]{4,3,2,1,0:T(8,128)(2,1)} %shard_map.89.refs_8_.refs_0_), custom_call_target="tpu_custom_call", output_to_operand_aliasing={{}: (1, {})} | custom-call | flops 300000000 | bytes 4000000 | tf_op jit(solution)/shard_map/pallas_call | solution.py:360
  (64 shorter events, 1.9 us)
Async XLA Ops:
  7.3 30.1 %copy-start.22 = (bf16[96,256]{1,0:T(8,128)(2,1)S(1)}, bf16[96,256]{1,0:T(8,128)(2,1)}, u32[]{:S(2)}) copy-start(bf16[96,256]{1,0:T(8,128)(2,1)} %get-tuple-element.23) | copy-start | bytes 147460
  7.3 30.6 %copy-start.21 = (bf16[96,256]{1,0:T(8,128)(2,1)S(1)}, bf16[96,256]{1,0:T(8,128)(2,1)}, u32[]{:S(2)}) copy-start(bf16[96,256]{1,0:T(8,128)(2,1)} %get-tuple-element.24) | copy-start | bytes 147460
  7.3 31.4 %copy-start.20 = (bf16[96,256]{1,0:T(8,128)(2,1)S(1)}, bf16[96,256]{1,0:T(8,128)(2,1)}, u32[]{:S(2)}) copy-start(bf16[96,256]{1,0:T(8,128)(2,1)} %get-tuple-element.25) | copy-start | bytes 147460
  7.3 43.3 %copy-start.12 = (bf16[8,96,256]{2,1,0:T(8,128)(2,1)S(1)}, bf16[8,96,256]{2,1,0:T(8,128)(2,1)}, u32[]{:S(2)}) copy-start(bf16[8,96,256]{2,1,0:T(8,128)(2,1)} %get-tuple-element.20) | copy-start | bytes 1179652
  7.3 52.9 %copy-start.11 = (bf16[8,96,256]{2,1,0:T(8,128)(2,1)S(1)}, bf16[8,96,256]{2,1,0:T(8,128)(2,1)}, u32[]{:S(2)}) copy-start(bf16[8,96,256]{2,1,0:T(8,128)(2,1)} %get-tuple-element.21) | copy-start | bytes 1179652
  7.3 55.3 %copy-start.6 = (bf16[1024,128]{1,0:T(8,128)(2,1)S(1)}, bf16[1024,128]{1,0:T(8,128)(2,1)}, u32[]{:S(2)}) copy-start(bf16[1024,128]{1,0:T(8,128)(2,1)} %param.13) | copy-start | bytes 786436
  37.3 48.5 %copy-start.2 = (bf16[8,96,1024]{2,1,0:T(8,128)(2,1)}, bf16[8,96,1024]{2,1,0:T(8,128)(2,1)S(1)}, u32[]{:S(2)}) copy-start(bf16[8,96,1024]{2,1,0:T(8,128)(2,1)S(1)} %all_to_all.15.refs_8_) | copy-start | bytes 4718596
  37.3 48.6 %collective-permute-start.13 = (bf16[8,96,1024]{2,1,0:T(8,128)(2,1)S(1)}, bf16[8,96,1024]{2,1,0:T(8,128)(2,1)}, u32[]{:S(2)}, u32[]{:S(2)}) collective-permute-start(bf16[8,96,1024]{2,1,0:T(8,128)(2,1)S(1)} %all_to_all.15.refs_8_), channel_id=1, source_target_pairs={{0,1},{1,0},{2,3},{3,2},{4,5},{5,4},{6,7},{7,6},{8,9},{9,8},{10,11... | collective-permute-start | bytes 4718600 | tf_op jit(solution)/shard_map/ppermute | solution.py:377
  37.4 3.5 %collective-permute-start.3 = (bf16[96,256]{1,0:T(8,128)(2,1)S(1)}, bf16[96,256]{1,0:T(8,128)(2,1)S(1)}, u32[]{:S(2)}, u32[]{:S(2)}) collective-permute-start(bf16[96,256]{1,0:T(8,128)(2,1)S(1)} %copy-done.22), channel_id=1, source_target_pairs={{0,1},{1,0},{2,3},{3,2},{4,5},{5,4},{6,7},{7,6},{8,9},{9,8},{10,11... | collective-permute-start | bytes 147464 | tf_op jit(solution)/shard_map/ppermute | solution.py:377
  37.9 5.8 %collective-permute-start.4 = (bf16[96,256]{1,0:T(8,128)(2,1)S(1)}, bf16[96,256]{1,0:T(8,128)(2,1)S(1)}, u32[]{:S(2)}, u32[]{:S(2)}) collective-permute-start(bf16[96,256]{1,0:T(8,128)(2,1)S(1)} %copy-done.21), channel_id=1, source_target_pairs={{0,2},{1,3},{2,0},{3,1},{4,6},{5,7},{6,4},{7,5},{8,10},{9,11},{10,... | collective-permute-start | bytes 147464 | tf_op jit(solution)/shard_map/ppermute | solution.py:377
  38.7 5.5 %collective-permute-start.5 = (bf16[96,256]{1,0:T(8,128)(2,1)S(1)}, bf16[96,256]{1,0:T(8,128)(2,1)S(1)}, u32[]{:S(2)}, u32[]{:S(2)}) collective-permute-start(bf16[96,256]{1,0:T(8,128)(2,1)S(1)} %copy-done.20), channel_id=1, source_target_pairs={{0,3},{1,2},{2,1},{3,0},{4,7},{5,6},{6,5},{7,4},{8,11},{9,10},{10,... | collective-permute-start | bytes 147464 | tf_op jit(solution)/shard_map/ppermute | solution.py:377
  40.9 3.4 %copy-start.7 = (bf16[96,256]{1,0:T(8,128)(2,1)}, bf16[96,256]{1,0:T(8,128)(2,1)S(1)}, u32[]{:S(2)}) copy-start(bf16[96,256]{1,0:T(8,128)(2,1)S(1)} %collective-permute-done.3.p1) | copy-start | bytes 147460
  46.6 13.6 %collective-permute-start.9 = (bf16[8,32,384]{2,1,0:T(8,128)(2,1)}, bf16[8,32,384]{2,1,0:T(8,128)(2,1)S(1)}, u32[]{:S(2)}, u32[]{:S(2)}) collective-permute-start(bf16[8,32,384]{2,1,0:T(8,128)(2,1)} %bitcast.25), channel_id=1, source_target_pairs={{0,12},{4,8},{8,4},{12,0},{16,28},{20,24},{24,20},{28,16},{1,13},{... | collective-permute-start | bytes 589832 | tf_op jit(solution)/shard_map/ppermute | solution.py:377
  50.6 11.4 %collective-permute-start.8 = (bf16[8,32,384]{2,1,0:T(8,128)(2,1)}, bf16[8,32,384]{2,1,0:T(8,128)(2,1)S(1)}, u32[]{:S(2)}, u32[]{:S(2)}) collective-permute-start(bf16[8,32,384]{2,1,0:T(8,128)(2,1)} %bitcast.26), channel_id=1, source_target_pairs={{0,8},{4,12},{8,0},{12,4},{16,24},{20,28},{24,16},{28,20},{1,9},{5... | collective-permute-start | bytes 589832 | tf_op jit(solution)/shard_map/ppermute | solution.py:377
  50.6 19.5 %collective-permute-start = (bf16[8,96,256]{2,1,0:T(8,128)(2,1)}, bf16[8,96,256]{2,1,0:T(8,128)(2,1)S(1)}, u32[]{:S(2)}, u32[]{:S(2)}) collective-permute-start(bf16[8,96,256]{2,1,0:T(8,128)(2,1)} %get-tuple-element.19), channel_id=1, source_target_pairs={{0,1},{1,0},{2,3},{3,2},{4,5},{5,4},{6,7},{7,6},{8,9},{9,8},{10,11... | collective-permute-start | bytes 1179656 | tf_op jit(solution)/shard_map/ppermute | solution.py:377
  50.6 22.5 %collective-permute-start.1 = (bf16[8,96,256]{2,1,0:T(8,128)(2,1)S(1)}, bf16[8,96,256]{2,1,0:T(8,128)(2,1)}, u32[]{:S(2)}, u32[]{:S(2)}) collective-permute-start(bf16[8,96,256]{2,1,0:T(8,128)(2,1)S(1)} %copy-done.12), channel_id=1, source_target_pairs={{0,2},{1,3},{2,0},{3,1},{4,6},{5,7},{6,4},{7,5},{8,10},{9,11},{10,... | collective-permute-start | bytes 1179656 | tf_op jit(solution)/shard_map/ppermute | solution.py:377
  60.2 25.6 %copy-start.14 = (bf16[8,32,384]{2,1,0:T(8,128)(2,1)}, bf16[8,32,384]{2,1,0:T(8,128)(2,1)S(1)}, u32[]{:S(2)}) copy-start(bf16[8,32,384]{2,1,0:T(8,128)(2,1)S(1)} %collective-permute-done.9.refs_3_) | copy-start | bytes 589828
  60.2 14.4 %collective-permute-start.2 = (bf16[8,96,256]{2,1,0:T(8,128)(2,1)S(1)}, bf16[8,96,256]{2,1,0:T(8,128)(2,1)}, u32[]{:S(2)}, u32[]{:S(2)}) collective-permute-start(bf16[8,96,256]{2,1,0:T(8,128)(2,1)S(1)} %copy-done.11), channel_id=1, source_target_pairs={{0,3},{1,2},{2,1},{3,0},{4,7},{5,6},{6,5},{7,4},{8,11},{9,10},{10,... | collective-permute-start | bytes 1179656 | tf_op jit(solution)/shard_map/ppermute | solution.py:377
  62.0 8.1 %collective-permute-start.6 = (bf16[8,32,384]{2,1,0:T(8,128)(2,1)}, bf16[8,32,384]{2,1,0:T(8,128)(2,1)}, u32[]{:S(2)}, u32[]{:S(2)}) collective-permute-start(bf16[8,32,384]{2,1,0:T(8,128)(2,1)} %bitcast.27), channel_id=1, source_target_pairs={{0,16},{4,20},{8,24},{12,28},{16,0},{20,4},{24,8},{28,12},{1,17},{... | collective-permute-start | bytes 589832 | tf_op jit(solution)/shard_map/ppermute | solution.py:377
  70.1 15.8 %collective-permute-start.7 = (bf16[8,32,384]{2,1,0:T(8,128)(2,1)}, bf16[8,32,384]{2,1,0:T(8,128)(2,1)S(1)}, u32[]{:S(2)}, u32[]{:S(2)}) collective-permute-start(bf16[8,32,384]{2,1,0:T(8,128)(2,1)} %bitcast.28), channel_id=1, source_target_pairs={{0,4},{4,0},{8,12},{12,8},{16,20},{20,16},{24,28},{28,24},{1,5},{5... | collective-permute-start | bytes 589832 | tf_op jit(solution)/shard_map/ppermute | solution.py:377
  70.1 4.7 %copy-start.10 = (bf16[8,96,256]{2,1,0:T(8,128)(2,1)}, bf16[8,96,256]{2,1,0:T(8,128)(2,1)S(1)}, u32[]{:S(2)}) copy-start(bf16[8,96,256]{2,1,0:T(8,128)(2,1)S(1)} %collective-permute-done.refs_1_) | copy-start | bytes 1179652
  70.1 15.8 %collective-permute-start.12 = (bf16[8,32,384]{2,1,0:T(8,128)(2,1)}, bf16[8,32,384]{2,1,0:T(8,128)(2,1)S(1)}, u32[]{:S(2)}, u32[]{:S(2)}) collective-permute-start(bf16[8,32,384]{2,1,0:T(8,128)(2,1)} %collective-permute-done.6.refs_8_.refs_4_), channel_id=1, source_target_pairs={{0,12},{4,8},{8,4},{12,0},{16,28},{20,24},{24,20},{28,16},{1,13},{... | collective-permute-start | bytes 589832 | tf_op jit(solution)/shard_map/ppermute | solution.py:377
  73.1 12.7 %collective-permute-start.11 = (bf16[8,32,384]{2,1,0:T(8,128)(2,1)}, bf16[8,32,384]{2,1,0:T(8,128)(2,1)S(1)}, u32[]{:S(2)}, u32[]{:S(2)}) collective-permute-start(bf16[8,32,384]{2,1,0:T(8,128)(2,1)} %collective-permute-done.6.refs_8_.refs_4_), channel_id=1, source_target_pairs={{0,8},{4,12},{8,0},{12,4},{16,24},{20,28},{24,16},{28,20},{1,9},{5... | collective-permute-start | bytes 589832 | tf_op jit(solution)/shard_map/ppermute | solution.py:377
  74.6 11.3 %collective-permute-start.10 = (bf16[8,32,384]{2,1,0:T(8,128)(2,1)}, bf16[8,32,384]{2,1,0:T(8,128)(2,1)S(1)}, u32[]{:S(2)}, u32[]{:S(2)}) collective-permute-start(bf16[8,32,384]{2,1,0:T(8,128)(2,1)} %collective-permute-done.6.refs_8_.refs_4_), channel_id=1, source_target_pairs={{0,4},{4,0},{8,12},{12,8},{16,20},{20,16},{24,28},{28,24},{1,5},{5... | collective-permute-start | bytes 589832 | tf_op jit(solution)/shard_map/ppermute | solution.py:377
  94.8 16.5 %all-to-all-start.1 = ((bf16[8,3,128,128]{3,2,1,0:T(8,128)(2,1)}), bf16[8,3,128,128]{3,2,1,0:T(8,128)(2,1)S(1)}, u32[]{:S(2)}, u32[]{:S(2)}) async-start(bf16[8,3,128,128]{3,2,1,0:T(8,128)(2,1)} %shard_map.87.refs_11_), calls=%async_computation.1 | async-start | bytes 1572864 | tf_op jit(solution)/shard_map/all_to_all | solution.py:401
  110.9 5.9 %copy-start.13 = (bf16[768,256]{1,0:T(8,128)(2,1)S(1)}, bf16[768,256]{1,0:T(8,128)(2,1)}, u32[]{:S(2)}) copy-start(bf16[768,256]{1,0:T(8,128)(2,1)} %get-tuple-element.30.refs_11_) | copy-start | bytes 1179652
  111.4 7.1 %copy-start.1 = (bf16[8,3,128,128]{3,2,1,0:T(8,128)(2,1)}, bf16[8,3,128,128]{3,2,1,0:T(8,128)(2,1)S(1)}, u32[]{:S(2)}) copy-start(bf16[8,3,128,128]{3,2,1,0:T(8,128)(2,1)S(1)} %all-to-all-done.1) | copy-start | bytes 2359300
  111.4 26.8 %all-to-all-start.2 = ((bf16[8,5,128,128]{3,2,1,0:T(8,128)(2,1)}), bf16[8,5,128,128]{3,2,1,0:T(8,128)(2,1)S(1)}, u32[]{:S(2)}, u32[]{:S(2)}) async-start(bf16[8,5,128,128]{3,2,1,0:T(8,128)(2,1)} %shard_map.88.refs_7_), calls=%async_computation.2 | async-start | bytes 2621440 | tf_op jit(solution)/shard_map/all_to_all | solution.py:403
  116.8 17.6 %collective-permute-start.15 = (bf16[768,256]{1,0:T(8,128)(2,1)S(1)}, bf16[768,256]{1,0:T(8,128)(2,1)S(1)}, u32[]{:S(2)}, u32[]{:S(2)}) collective-permute-start(bf16[768,256]{1,0:T(8,128)(2,1)S(1)} %copy-done.13), channel_id=1, source_target_pairs={{0,2},{1,3},{2,0},{3,1},{4,6},{5,7},{6,4},{7,5},{8,10},{9,11},{10,... | collective-permute-start | bytes 1179656 | tf_op jit(solution)/shard_map/ppermute | solution.py:377
  118.4 16.0 %collective-permute-start.16 = (bf16[768,256]{1,0:T(8,128)(2,1)}, bf16[768,256]{1,0:T(8,128)(2,1)S(1)}, u32[]{:S(2)}, u32[]{:S(2)}) collective-permute-start(bf16[768,256]{1,0:T(8,128)(2,1)} %get-tuple-element.33), channel_id=1, source_target_pairs={{0,3},{1,2},{2,1},{3,0},{4,7},{5,6},{6,5},{7,4},{8,11},{9,10},{10,... | collective-permute-start | bytes 1179656 | tf_op jit(solution)/shard_map/ppermute | solution.py:377
  130.4 4.0 %collective-permute-start.14 = (bf16[768,256]{1,0:T(8,128)(2,1)}, bf16[768,256]{1,0:T(8,128)(2,1)S(1)}, u32[]{:S(2)}, u32[]{:S(2)}) collective-permute-start(bf16[768,256]{1,0:T(8,128)(2,1)} %get-tuple-element.32), channel_id=1, source_target_pairs={{0,1},{1,0},{2,3},{3,2},{4,5},{5,4},{6,7},{7,6},{8,9},{9,8},{10,11... | collective-permute-start | bytes 1179656 | tf_op jit(solution)/shard_map/ppermute | solution.py:377
  138.2 1.1 copy-start
  (10 other events, 7.8 us)
